TPU v7x, 32 devices: a whole 2x2x4 slice. The times are simulated.
32 devices in a mesh: replica: 8 (over z, core), shard: 4 (over y, x).
Axes of the slice: x: 2, y: 2, z: 4, core: 2. Of those that a mesh axis runs over, the one named last changes fastest.
Arguments:
- block_input: bfloat16 [4096, 1536], P(('replica', 'shard')), may hold values from -6 to 6
- attn_gain: bfloat16 [1536], P('shard'), may hold values from 0.099609375 to 1.8984375
- qkv_weight: bfloat16 [1536, 2048], P('shard'), may hold values from -0.15625 to 0.15625
- qkv_bias: bfloat16 [2048], P('shard'), may hold values from -3 to 3
- out_weight: bfloat16 [1536, 1536], P('shard'), may hold values from -0.875 to 0.875
- mlp_gain: bfloat16 [1536], P('shard'), may hold values from 0.099609375 to 1.8984375
- gate_weight: bfloat16 [1536, 8960], P('shard'), may hold values from -0.15625 to 0.15625
- up_weight: bfloat16 [1536, 8960], P('shard'), may hold values from -0.15625 to 0.15625
- down_weight: bfloat16 [8960, 1536], P('shard'), may hold values from -0.09375 to 0.09375
- cotangent: bfloat16 [4096, 1536], P(('replica', 'shard')), may hold values from -6 to 6
Outputs:
- block_output: bfloat16 [4096, 1536], P(('replica', 'shard'))
- input_grad: float32 [4096, 1536], P(('replica', 'shard'))
- attn_gain_grad: float32 [1536], P('shard')
- qkv_weight_grad: float32 [1536, 2048], P('shard')
- qkv_bias_grad: float32 [2048], P('shard')
- out_weight_grad: float32 [1536, 1536], P('shard')
- mlp_gain_grad: float32 [1536], P('shard')
- gate_weight_grad: float32 [1536, 8960], P('shard')
- up_weight_grad: float32 [1536, 8960], P('shard')
- down_weight_grad: float32 [8960, 1536], P('shard')
All inputs are finite; a program needn't handle non-finite values.
Results may differ from a plain program's by a relative error of at most 0.013.
Values may be sent and summed in bfloat16 or wider, within the bound.
A program may use at most 320 MiB of HBM per device.

v0:
```python
import math

import jax
import jax.numpy as jnp
from jax import lax
from jax.sharding import PartitionSpec as P

HEADS = 12
KV = 2
HD = 128


NORM_EPS = 1e-06
ROPE_BASE = 1000000.0


def rope_tables(tok_count):
    half_dim = HD // 2
    position = jnp.arange(tok_count, dtype=jnp.float32)
    inverse = ROPE_BASE ** (-(jnp.arange(half_dim, dtype=jnp.float32) * 2.0 / HD))
    angles = position[:, None] * inverse[None, :]
    return (jnp.cos(angles)[:, None, :], jnp.sin(angles)[:, None, :])


def rotate(vectors, cosine, sine_table):
    half_dim = HD // 2
    lower_half = vectors[..., :half_dim]
    upper_half = vectors[..., half_dim:]
    return jnp.concatenate(
        [
            lower_half * cosine - upper_half * sine_table,
            upper_half * cosine + lower_half * sine_table,
        ],
        axis=-1,
    )


def unrotate(grads, cosine, sine_table):
    half_dim = HD // 2
    lower_half = grads[..., :half_dim]
    upper_half = grads[..., half_dim:]
    return jnp.concatenate(
        [
            lower_half * cosine + upper_half * sine_table,
            upper_half * cosine - lower_half * sine_table,
        ],
        axis=-1,
    )


def block_scores(query_block, key_rot, first_row):
    row_count = query_block.shape[0]
    scores = jnp.einsum(
        "qkgd,skd->kgqs", query_block, key_rot, preferred_element_type=jnp.float32
    ) * (1.0 / math.sqrt(HD))
    causal = (first_row + jnp.arange(row_count))[:, None] >= jnp.arange(key_rot.shape[0])[None, :]
    return jnp.where(causal, scores, -1e30)


def block_layout(tok_count):
    block_rows = min(tok_count, 512)
    block_count = tok_count // block_rows
    firsts = jnp.arange(block_count, dtype=jnp.int32) * block_rows
    return (block_rows, block_count, firsts)


def attend_forward(queries, key_rot, values):
    tok_count = queries.shape[0]
    block_rows, block_count, firsts = block_layout(tok_count)
    query_blocks = queries.reshape(block_count, block_rows, KV, HEADS // KV, HD)

    def one_block(inputs):
        query_block, first_row = inputs
        scores = block_scores(query_block, key_rot, first_row)
        row_max = jnp.max(scores, axis=-1, keepdims=True)
        logsum = row_max + jnp.log(jnp.sum(jnp.exp(scores - row_max), axis=-1, keepdims=True))
        attn_probs = jnp.exp(scores - logsum).astype(jnp.bfloat16)
        context = jnp.einsum(
            "kgqs,skd->qkgd", attn_probs, values, preferred_element_type=jnp.float32
        ).astype(jnp.bfloat16)
        return (context, logsum)

    context, logsum = lax.map(one_block, (query_blocks, firsts))
    return (context.reshape(tok_count, HEADS * HD), logsum)


def attend_backward(queries, key_rot, values, logsum, context_grad):
    tok_count = queries.shape[0]
    block_rows, block_count, firsts = block_layout(tok_count)
    query_blocks = queries.reshape(block_count, block_rows, KV, HEADS // KV, HD)
    grad_blocks = context_grad.reshape(block_count, block_rows, KV, HEADS // KV, HD)
    score_scale = 1.0 / math.sqrt(HD)

    def one_block(running, inputs):
        key_total, value_total = running
        query_block, grad_block, log_block, first_row = inputs
        scores = block_scores(query_block, key_rot, first_row)
        attn_probs = jnp.exp(scores - log_block).astype(jnp.bfloat16)
        prob_grad = jnp.einsum(
            "qkgd,skd->kgqs", grad_block, values, preferred_element_type=jnp.float32
        )
        wide_probs = attn_probs.astype(jnp.float32)
        row_delta = jnp.sum(wide_probs * prob_grad, axis=-1, keepdims=True)
        score_grad = (wide_probs * (prob_grad - row_delta) * score_scale).astype(jnp.bfloat16)
        query_grad = jnp.einsum(
            "kgqs,skd->qkgd", score_grad, key_rot, preferred_element_type=jnp.float32
        )
        key_total = key_total + jnp.einsum(
            "kgqs,qkgd->skd", score_grad, query_block, preferred_element_type=jnp.float32
        )
        value_total = value_total + jnp.einsum(
            "kgqs,qkgd->skd", attn_probs, grad_block, preferred_element_type=jnp.float32
        )
        return ((key_total, value_total), query_grad)

    zero_keys = jnp.zeros((tok_count, KV, HD), jnp.float32)
    (key_grad, value_grad), query_grad = lax.scan(
        one_block, (zero_keys, zero_keys), (query_blocks, grad_blocks, logsum, firsts)
    )
    return (query_grad.reshape(tok_count, HEADS, HD), key_grad, value_grad)


def per_device(
    block_input,
    attn_gain,
    qkv_weight,
    qkv_bias,
    out_weight,
    mlp_gain,
    gate_weight,
    up_weight,
    down_weight,
    cotangent,
):
    f32 = jnp.float32
    bf16 = jnp.bfloat16
    tok_count = block_input.shape[0]
    grad_scale = 1.0 / math.sqrt(tok_count * lax.axis_size("replica") * lax.axis_size("shard"))
    q_width = HEADS * HD
    k_end = q_width + KV * HD
    cosine, sine_table = rope_tables(tok_count)
    attn_full = (
        lax.all_gather(attn_gain, "shard", axis=0, tiled=True),
        lax.all_gather(qkv_weight, "shard", axis=0, tiled=True),
        lax.all_gather(qkv_bias, "shard", axis=0, tiled=True),
        lax.all_gather(out_weight, "shard", axis=0, tiled=True),
    )
    gain_full, qkv_full, bias_full, out_full = attn_full
    gain_one = gain_full.astype(f32)
    xfloat = block_input.astype(f32)
    inv_one = lax.rsqrt(jnp.mean(xfloat * xfloat, axis=-1, keepdims=True) + NORM_EPS)
    normed_one = (xfloat * inv_one * gain_one).astype(bf16)
    projected = jnp.dot(normed_one, qkv_full, preferred_element_type=f32) + bias_full.astype(f32)
    queries = rotate(
        projected[:, :q_width].reshape(tok_count, HEADS, HD), cosine, sine_table
    ).astype(bf16)
    queries = queries.reshape(tok_count, KV, HEADS // KV, HD)
    key_rot = rotate(
        projected[:, q_width:k_end].reshape(tok_count, KV, HD), cosine, sine_table
    ).astype(bf16)
    values = projected[:, k_end:].reshape(tok_count, KV, HD).astype(bf16)
    context, logsum = attend_forward(queries, key_rot, values)
    hidden_res = xfloat + jnp.dot(context, out_full, preferred_element_type=f32)
    mlp_full = (
        lax.all_gather(mlp_gain, "shard", axis=0, tiled=True),
        lax.all_gather(gate_weight, "shard", axis=0, tiled=True),
        lax.all_gather(up_weight, "shard", axis=0, tiled=True),
        lax.all_gather(down_weight, "shard", axis=0, tiled=True),
    )
    gain_full_two, gate_full, up_full, down_full = mlp_full
    gain_two = gain_full_two.astype(f32)
    inv_two = lax.rsqrt(jnp.mean(hidden_res * hidden_res, axis=-1, keepdims=True) + NORM_EPS)
    normed_two = (hidden_res * inv_two * gain_two).astype(bf16)
    gate_pre = jnp.dot(normed_two, gate_full, preferred_element_type=f32)
    up_pre = jnp.dot(normed_two, up_full, preferred_element_type=f32)
    sigmoid_gate = jax.nn.sigmoid(gate_pre)
    silu_gate = gate_pre * sigmoid_gate
    activation = (silu_gate * up_pre).astype(bf16)
    block_output = (hidden_res + jnp.dot(activation, down_full, preferred_element_type=f32)).astype(
        bf16
    )
    act_grad = jnp.einsum("td,fd->tf", cotangent, down_full, preferred_element_type=f32)
    gate_delta = (
        act_grad * up_pre * sigmoid_gate * (1.0 + gate_pre * (1.0 - sigmoid_gate))
    ).astype(bf16)
    up_delta = (act_grad * silu_gate).astype(bf16)
    normed_two_grad = jnp.einsum(
        "tf,df->td", gate_delta, gate_full, preferred_element_type=f32
    ) + jnp.einsum("tf,df->td", up_delta, up_full, preferred_element_type=f32)
    gain_two_grad = jnp.sum(normed_two_grad * hidden_res * inv_two, axis=0) * grad_scale
    own_rows = (
        lax.all_to_all(activation, "shard", split_axis=1, concat_axis=0, tiled=True),
        lax.all_to_all(normed_two, "shard", split_axis=1, concat_axis=0, tiled=True),
    )
    group_act, group_normed = own_rows
    group_rows = (
        lax.all_gather(cotangent, "shard", axis=0, tiled=True),
        lax.all_gather(gate_delta, "shard", axis=0, tiled=True),
        lax.all_gather(up_delta, "shard", axis=0, tiled=True),
    )
    group_cot, group_gate, group_up = group_rows
    down_part = (
        jnp.einsum("tf,td->fd", group_act, group_cot, preferred_element_type=f32) * grad_scale
    )
    gate_own = (
        jnp.einsum("td,tf->df", group_normed, group_gate, preferred_element_type=f32) * grad_scale
    )
    up_own = (
        jnp.einsum("td,tf->df", group_normed, group_up, preferred_element_type=f32) * grad_scale
    )
    gain_two_own = lax.psum_scatter(gain_two_grad, "shard", scatter_dimension=0, tiled=True)
    mlp_parts = (gain_two_own, gate_own, up_own)
    hidden_grad = cotangent.astype(f32) + inv_two * (
        gain_two * normed_two_grad
        - hidden_res
        * inv_two
        * inv_two
        * jnp.mean(gain_two * normed_two_grad * hidden_res, axis=-1, keepdims=True)
    )
    hidden_low = hidden_grad.astype(bf16)
    context_grad = jnp.einsum("td,ed->te", hidden_low, out_full, preferred_element_type=f32).astype(
        bf16
    )
    query_grad, key_grad, value_grad = attend_backward(
        queries, key_rot, values, logsum, context_grad
    )
    query_grad = unrotate(query_grad, cosine, sine_table).reshape(tok_count, q_width)
    key_grad = unrotate(key_grad, cosine, sine_table).reshape(tok_count, KV * HD)
    projected_grad = jnp.concatenate(
        [query_grad, key_grad, value_grad.reshape(tok_count, KV * HD)], axis=-1
    ).astype(bf16)
    normed_one_grad = jnp.einsum("tc,dc->td", projected_grad, qkv_full, preferred_element_type=f32)
    gain_one_grad = jnp.sum(normed_one_grad * xfloat * inv_one, axis=0) * grad_scale
    bias_grad = jnp.sum(projected_grad.astype(f32), axis=0) * grad_scale
    own_attn = (
        lax.all_to_all(context, "shard", split_axis=1, concat_axis=0, tiled=True),
        lax.all_to_all(normed_one, "shard", split_axis=1, concat_axis=0, tiled=True),
    )
    group_context, group_normed_one = own_attn
    group_rows = (
        lax.all_gather(hidden_low, "shard", axis=0, tiled=True),
        lax.all_gather(projected_grad, "shard", axis=0, tiled=True),
    )
    group_hidden, group_projected = group_rows
    out_own = (
        jnp.einsum("te,td->ed", group_context, group_hidden, preferred_element_type=f32)
        * grad_scale
    )
    qkv_part = (
        jnp.einsum("td,tc->dc", group_normed_one, group_projected, preferred_element_type=f32)
        * grad_scale
    )
    small_parts = (
        lax.psum_scatter(gain_one_grad, "shard", scatter_dimension=0, tiled=True),
        lax.psum_scatter(bias_grad, "shard", scatter_dimension=0, tiled=True),
    )
    attn_parts = (small_parts[0], qkv_part, small_parts[1], out_own)
    input_grad = hidden_grad + inv_one * (
        gain_one * normed_one_grad
        - xfloat
        * inv_one
        * inv_one
        * jnp.mean(gain_one * normed_one_grad * xfloat, axis=-1, keepdims=True)
    )
    summed = lax.psum(
        (
            attn_parts[0],
            attn_parts[1],
            attn_parts[2],
            attn_parts[3],
            mlp_parts[0],
            mlp_parts[1],
            mlp_parts[2],
            down_part,
        ),
        "replica",
    )
    attn_parts = (summed[0], summed[1], summed[2], summed[3])
    mlp_parts = (summed[4], summed[5], summed[6])
    down_part = summed[7]
    return (
        block_output,
        input_grad,
        attn_parts[0],
        attn_parts[1],
        attn_parts[2],
        attn_parts[3],
        mlp_parts[0],
        mlp_parts[1],
        mlp_parts[2],
        down_part,
    )


def solution(mesh):
    placed = (
        P(("replica", "shard"), None),
        P("shard"),
        P("shard", None),
        P("shard"),
        P("shard", None),
        P("shard"),
        P("shard", None),
        P("shard", None),
        P("shard", None),
        P(("replica", "shard"), None),
    )
    return jax.shard_map(
        per_device,
        mesh=mesh,
        in_specs=placed,
        out_specs=(
            P(("replica", "shard"), None),
            P(("replica", "shard"), None),
            P("shard"),
            P("shard", None),
            P("shard"),
            P("shard", None),
            P("shard"),
            P("shard", None),
            P("shard", None),
            P("shard", None),
        ),
        check_vma=False,
    )
```

profile of v0, /device:TPU:0, one launch (start us, length us, event | category | flops | bytes accessed | tf_op | source)
XLA Modules:
  0.0 2167.6 jit_solution(13757412810950889367)
XLA Ops:
  11.9 9.6 all-gather
  21.7 8.4 all-gather.1
  31.7 7.4 all-gather.2
  39.4 43.3 %all-gather.14.cloned.1.call-done = bf16[1536,2048]{1,0:T(8,128)(2,1)} async-done(((bf16[384,2048]{1,0:T(8,128)(2,1)}), bf16[1536,2048]{1,0:T(8,128)(2,1)}) %all-gather.14.cloned.1.call-update) | async-done | bytes 6291472 | tf_op jit(solution)/shard_map/all_gather | solution.py:144
  82.7 3.8 convolution_add_fusion.3
  92.8 48.7 %all-gather.16.cloned.1.call-done = bf16[1536,1536]{1,0:T(8,128)(2,1)} async-done(((bf16[384,1536]{1,0:T(8,128)(2,1)}), bf16[1536,1536]{1,0:T(8,128)(2,1)}) %all-gather.16.cloned.1.call-update) | async-done | bytes 4718608 | tf_op jit(solution)/shard_map/all_gather | solution.py:146
  141.5 3.2 multiply_reduce_fusion.2
  144.9 245.5 %all-gather.18.cloned.1.call-done = bf16[1536,8960]{1,0:T(8,128)(2,1)} async-done(((bf16[384,8960]{1,0:T(8,128)(2,1)}), bf16[1536,8960]{1,0:T(8,128)(2,1)}) %all-gather.18.cloned.1.call-update) | async-done | bytes 27525136 | tf_op jit(solution)/shard_map/all_gather | solution.py:166
  390.4 15.8 fusion.39
  406.3 232.9 %all-gather.20.cloned.1.call-done = bf16[1536,8960]{1,0:T(8,128)(2,1)} async-done(((bf16[384,8960]{1,0:T(8,128)(2,1)}), bf16[1536,8960]{1,0:T(8,128)(2,1)}) %all-gather.20.cloned.1.call-update) | async-done | bytes 27525136 | tf_op jit(solution)/shard_map/all_gather | solution.py:167
  639.2 15.8 fusion.40
  655.0 232.9 %all-gather.22.cloned.1.call-done = bf16[8960,1536]{1,0:T(8,128)(2,1)} async-done(((bf16[2240,1536]{1,0:T(8,128)(2,1)}), bf16[8960,1536]{1,0:T(8,128)(2,1)}) %all-gather.22.cloned.1.call-update) | async-done | bytes 27525136 | tf_op jit(solution)/shard_map/all_gather | solution.py:168
  887.9 18.2 multiply_convert_fusion
  906.1 15.8 fusion.41
  922.0 15.6 multiply_reduce_fusion
  938.7 4.8 convolution_convert_fusion
  945.9 2.9 convolution_bitcast_fusion.1
  950.2 3.0 fusion.11
  956.1 1.5 convert_reduce_fusion
  959.0 2.5 copy.84
  961.4 4.5 all-to-all-start.3
  965.9 1.8 copy.120
  967.7 1.9 copy.82
  969.6 1.8 copy.119
  971.4 22.8 %all-to-all-done.3 = bf16[128,4,2240]{0,2,1:T(8,128)(2,1)} async-done(((bf16[128,4,2240]{0,2,1:T(8,128)(2,1)}), bf16[128,4,2240]{0,2,1:T(8,128)(2,1)}, u32[]{:S(2)}, u32[]{:S(2)}) %all-to-all-start.3) | async-done | bytes 2293792 | tf_op jit(solution)/shard_map/all_to_all | solution.py:192
  994.2 4.1 all-to-all-start.1
  998.3 4.2 copy.85
  1002.6 11.1 convolution_multiply_fusion
  1013.6 4.1 all-to-all-start
  1017.8 3.7 convolution_multiply_fusion.3
  1021.5 3.1 all-to-all-done
  1024.6 4.1 all-to-all-start.2
  1029.0 4.9 convolution_multiply_fusion.4
  1033.9 3.0 all-to-all-done.2
  1036.8 79.6 %all-gather.28.cloned.1.call-done = bf16[512,8960]{1,0:T(8,128)(2,1)} async-done(((bf16[128,8960]{1,0:T(8,128)(2,1)}), bf16[512,8960]{1,0:T(8,128)(2,1)}) %all-gather.28.cloned.1.call-update) | async-done | bytes 9175056 | tf_op jit(solution)/shard_map/all_gather | solution.py:198
  1116.4 14.3 convolution_multiply_fusion.2
  1130.7 81.5 %all-gather.30.cloned.1.call-done = bf16[512,8960]{1,0:T(8,128)(2,1)} async-done(((bf16[128,8960]{1,0:T(8,128)(2,1)}), bf16[512,8960]{1,0:T(8,128)(2,1)}) %all-gather.30.cloned.1.call-update) | async-done | bytes 9175056 | tf_op jit(solution)/shard_map/all_gather | solution.py:199
  1212.2 12.7 convolution_multiply_fusion.1
  1227.4 6.1 fusion.22
  1233.5 16.0 all-reduce.5
  1250.4 15.8 all-reduce.3
  1266.2 2.8 fusion.18
  1269.0 11.9 fusion.2
  1280.9 841.1 %all-reduce.8.cloned.1.call-done = (f32[384,2048]{1,0:T(8,128)}, f32[384,1536]{1,0:T(8,128)}, f32[384,8960]{1,0:T(8,128)}, f32[384,8960]{1,0:T(8,128)}, f32[2240,1536]{1,0:T(8,128)}) async-done(((f32[384,2048]{1,0:T(8,128)}, f32[384,1536]{1,0:T(8,128)}, f32[384,8960]{1,0:T(8,128)}, f32[384,8960]{1,0:T(8,128)}, f32[2240,1536]{1,0:T(8,128)}), (f32[384,2048]{1,0:T(8,128)}, f32[384,1536]{1,0:T(8,128)}, ...) | async-done | bytes 46792720 | tf_op jit(solution)/shard_map/psum | solution.py:265
  2122.0 4.1 copy.126
  2127.5 11.0 copy.128
  2138.5 11.0 copy.129
  2149.4 11.5 copy.130
  (153 shorter events, 25.6 us)
Async XLA Ops:
  7.2 75.5 %all-gather.14.cloned.1.call-start = ((), (), s32[]{:S(2)}) async-start(), calls=%async_computation.4 | async-start | bytes 7864320 | tf_op jit(solution)/shard_map/all_gather | solution.py:144
  7.9 133.6 %all-gather.16.cloned.1.call-start = ((), (), s32[]{:S(2)}) async-start(), calls=%async_computation.5 | async-start | bytes 5898240 | tf_op jit(solution)/shard_map/all_gather | solution.py:146
  8.7 381.8 %all-gather.18.cloned.1.call-start = ((), (), s32[]{:S(2)}) async-start(), calls=%async_computation.6 | async-start | bytes 34406400 | tf_op jit(solution)/shard_map/all_gather | solution.py:166
  9.4 629.8 %all-gather.20.cloned.1.call-start = ((), (), s32[]{:S(2)}) async-start(), calls=%async_computation.7 | async-start | bytes 34406400 | tf_op jit(solution)/shard_map/all_gather | solution.py:167
  10.0 1.9 copy-start.34
  10.0 11.5 copy-start.2
  10.0 11.7 copy-start.33
  10.0 21.7 %copy-start.35 = (bf16[384]{0:T(512)(128)(2,1)S(1)}, bf16[384]{0:T(512)(128)(2,1)}, u32[]{:S(2)}) copy-start(bf16[384]{0:T(512)(128)(2,1)} %param.15) | copy-start | bytes 2308
  10.0 877.9 %all-gather.22.cloned.1.call-start = ((), (), s32[]{:S(2)}) async-start(), calls=%async_computation.8 | async-start | bytes 34406400 | tf_op jit(solution)/shard_map/all_gather | solution.py:168
  10.6 992.0 %all-gather.32.cloned.1.call-start = ((), (), s32[]{:S(2)}) async-start(), calls=%async_computation.13 | async-start | bytes 1966080 | tf_op jit(solution)/shard_map/all_gather | solution.py:197
  11.2 1006.6 %all-gather.26.cloned.1.call-start = ((), (), s32[]{:S(2)}) async-start(), calls=%async_computation.10 | async-start | bytes 1966080 | tf_op jit(solution)/shard_map/all_gather | solution.py:241
  21.7 61.1 %copy-start.29 = (f32[128]{0:T(128)}, f32[128]{0:T(128)S(1)}, u32[]{:S(2)}) copy-start(f32[128]{0:T(128)S(1)} %add_rsqrt_fusion.1) | copy-start | bytes 1540
  30.3 60.5 %copy-start.15 = (f32[128,64]{1,0:T(8,128)}, f32[128,64]{1,0:T(8,128)S(1)}, u32[]{:S(2)}) copy-start(f32[128,64]{1,0:T(8,128)S(1)} %get-tuple-element.86) | copy-start | bytes 98308
  39.4 47.1 %copy-start.5 = (bf16[128,1536]{1,0:T(8,128)(2,1)}, bf16[128,1536]{1,0:T(8,128)(2,1)S(1)}, u32[]{:S(2)}) copy-start(bf16[128,1536]{1,0:T(8,128)(2,1)S(1)} %fusion.14) | copy-start | bytes 1179652
  87.9 4.6 copy-start.23
  89.3 3.0 copy-start.11
  89.5 52.0 %copy-start.13 = (bf16[128,12,64]{2,0,1:T(8,128)(2,1)}, bf16[128,12,64]{2,0,1:T(8,128)(2,1)S(1)}, u32[]{:S(2)}) copy-start(bf16[128,12,64]{2,0,1:T(8,128)(2,1)S(1)} %copy.67) | copy-start | bytes 589828
  92.5 49.1 %copy-start.6 = (bf16[2,6,128,128]{2,3,1,0:T(8,128)(2,1)}, bf16[2,6,128,128]{2,3,1,0:T(8,128)(2,1)S(1)}, u32[]{:S(2)}) copy-start(bf16[2,6,128,128]{2,3,1,0:T(8,128)(2,1)S(1)} %exponential_convert_fusion) | copy-start | bytes 1179652
  92.5 313.8 %copy-start.17 = (bf16[128,2,128]{2,1,0:T(2,128)(2,1)}, bf16[128,2,128]{2,1,0:T(2,128)(2,1)S(1)}, u32[]{:S(2)}) copy-start(bf16[128,2,128]{2,1,0:T(2,128)(2,1)S(1)} %convert_element_type.75) | copy-start | bytes 196612
  92.8 52.0 %copy-start.7 = (bf16[2,128,6,128]{3,1,2,0:T(8,128)(2,1)}, bf16[2,128,6,128]{3,1,2,0:T(8,128)(2,1)S(1)}, u32[]{:S(2)}) copy-start(bf16[2,128,6,128]{3,1,2,0:T(8,128)(2,1)S(1)} %convolution_convert_fusion.1) | copy-start | bytes 1179652
  144.8 261.5 %copy-start.26 = (f32[128]{0:T(128)}, f32[128]{0:T(128)S(1)}, u32[]{:S(2)}) copy-start(f32[128]{0:T(128)S(1)} %add_rsqrt_fusion) | copy-start | bytes 1540
  144.9 494.3 %copy-start.4 = (bf16[128,1536]{1,0:T(8,128)(2,1)}, bf16[128,1536]{1,0:T(8,128)(2,1)S(1)}, u32[]{:S(2)}) copy-start(bf16[128,1536]{1,0:T(8,128)(2,1)S(1)} %multiply_convert_fusion.3) | copy-start | bytes 1179652
  906.1 15.8 copy-start
  922.0 15.6 copy-start.9
  922.0 15.6 copy-start.27
  937.5 8.4 copy-start.3
  937.5 7.3 copy-start.18
  937.6 8.4 copy-start.12
  937.6 8.4 copy-start.14
  938.6 10.3 copy-start.16
  938.7 11.6 copy-start.20
  938.7 11.6 copy-start.22
  938.7 90.3 %all-gather.24.cloned.1.call-start = ((), (), s32[]{:S(2)}) async-start(), calls=%async_computation.9 | async-start | bytes 2621440 | tf_op jit(solution)/shard_map/all_gather | solution.py:242
  944.8 5.4 copy-start.8
  953.3 5.7 copy-start.1
  957.6 158.8 %all-gather.28.cloned.1.call-start = ((), (), s32[]{:S(2)}) async-start(), calls=%async_computation.11 | async-start | bytes 11468800 | tf_op jit(solution)/shard_map/all_gather | solution.py:198
  958.4 253.8 %all-gather.30.cloned.1.call-start = ((), (), s32[]{:S(2)}) async-start(), calls=%async_computation.12 | async-start | bytes 11468800 | tf_op jit(solution)/shard_map/all_gather | solution.py:199
  961.4 32.7 %all-to-all-start.3 = ((bf16[128,4,2240]{0,2,1:T(8,128)(2,1)}), bf16[128,4,2240]{0,2,1:T(8,128)(2,1)}, u32[]{:S(2)}, u32[]{:S(2)}) async-start(bf16[128,4,2240]{0,2,1:T(8,128)(2,1)} %bitcast.101), calls=%async_computation.3 | async-start | bytes 4587520 | tf_op jit(solution)/shard_map/all_to_all | solution.py:192
  994.2 19.4 all-to-all-start.1
  1013.6 11.0 all-to-all-start
  1024.6 12.2 all-to-all-start.2
  1028.7 1093.3 %all-reduce.8.cloned.1.call-start = ((), (), s32[]{:S(2)}) async-start(), calls=%async_computation.14 | async-start | bytes 93585408 | tf_op jit(solution)/shard_map/psum | solution.py:265
  1224.9 2.5 copy-start.30
  1224.9 8.6 copy-start.25
  1224.9 8.6 copy-start.24
  1224.9 41.3 %copy-start.28 = (f32[128]{0:T(128)S(1)}, f32[128]{0:T(128)}, u32[]{:S(2)}) copy-start(f32[128]{0:T(128)} %copy-done.26) | copy-start | bytes 1540
  1224.9 41.3 %copy-start.32 = (f32[128]{0:T(128)S(1)}, f32[128]{0:T(128)}, u32[]{:S(2)}) copy-start(f32[128]{0:T(128)} %copy-done.31) | copy-start | bytes 1540
  2122.0 4.1 copy-start.10
  (4 other events, 4.5 us)
Sparse Core Ops, SparseCore 0:
  9.8 72.8 all-gather.13
  84.6 56.9 all-gather.15
  143.4 247.0 all-gather.17
  392.2 246.9 all-gather.19
  640.9 246.9 all-gather.21
  889.6 30.8 all-gather.31
  938.8 32.5 all-gather.25
  973.2 45.7 all-gather.23
  1021.5 94.9 all-gather.27
  1118.1 94.0 all-gather.29
  1225.0 896.9 all-reduce.7
where the time goes:
time: 2180 us; the launch traced here: 2170 us
  waiting for transfers between devices  1840 us (84%)
  matrix products  168 us (8%)
  local copies, waits for them, and re-layouts  59.5 us (3%)
  blocking collectives  57.1 us (3%)
    psum x1, waiting for transfers between devices, per_device(): lax.psum((attn_parts[0], attn_parts[1], attn_parts[2], attn_parts[3], mlp...  841 us
    all_gather x1, waiting for transfers between devices, per_device(): lax.all_gather(gate_weight, 'shard', axis=0, tiled=True)  246 us
    all_gather x1, waiting for transfers between devices, per_device(): lax.all_gather(up_weight, 'shard', axis=0, tiled=True)  233 us
    all_gather x1, waiting for transfers between devices, per_device(): lax.all_gather(down_weight, 'shard', axis=0, tiled=True)  233 us
    all_gather x1, waiting for transfers between devices, per_device(): lax.all_gather(up_delta, 'shard', axis=0, tiled=True)  81.5 us
    all_gather x1, waiting for transfers between devices, per_device(): lax.all_gather(gate_delta, 'shard', axis=0, tiled=True)  79.6 us
    all_gather x1, waiting for transfers between devices, per_device(): lax.all_gather(out_weight, 'shard', axis=0, tiled=True)  48.7 us
  transfers between devices with their start and end apart: 15, of which 11 were waited for; matrix products, arithmetic and copies ran while one was open for 9% of the time, Pallas kernels for 0%

commit v1 on v0

--- a/solution.py
+++ b/solution.py
@@ -1,8 +1,11 @@
+import functools
 import math
 
 import jax
 import jax.numpy as jnp
 from jax import lax
+from jax.experimental import pallas as pl
+from jax.experimental.pallas import tpu as pltpu
 from jax.sharding import PartitionSpec as P
 
 HEADS = 12
@@ -120,7 +123,7 @@
     return (query_grad.reshape(tok_count, HEADS, HD), key_grad, value_grad)
 
 
-def per_device(
+def general_device(
     block_input,
     attn_gain,
     qkv_weight,
@@ -292,6 +295,695 @@
     )
 
 
+MESH = pl.DeviceIdType.MESH
+VMEM_BYTES = 62 * 2**20
+WINDOW = 1152
+
+
+def place():
+    replica = lax.axis_index("replica")
+    shard = lax.axis_index("shard")
+    core = lax.rem(replica, 2)
+    return replica, shard, core
+
+
+def peer_of(shard, d):
+    across = lax.rem(lax.rem(shard, 2) + d % 2, 2)
+    up = lax.rem(shard // 2 + d // 2, 2)
+    return up * 2 + across
+
+
+def window_start(shard, core):
+    return ((shard * 35) // 2 + core * 9) * 128
+
+
+def remote(src, dst, send, recv, device):
+    return pltpu.make_async_remote_copy(
+        src_ref=src,
+        dst_ref=dst,
+        send_sem=send,
+        recv_sem=recv,
+        device_id=device,
+        device_id_type=MESH,
+    )
+
+
+def front_kernel(
+    wq, wo, wg, wu, cot, small, q_full, o_full, g_own, u_own, cot_all, small_all,
+    bq, bo, bg, bu, bc, bs, send, recv, fsend, frecv, local,
+):
+    replica, shard, core = place()
+    mate = (replica + 1 - 2 * core, shard)
+    half = 192
+
+    def rows(owner):
+        return pl.ds(pl.multiple_of(owner * 384, 384), 384)
+
+    def half_rows(owner, c):
+        return pl.ds(pl.multiple_of(owner * 384 + c * half, half), half)
+
+    def cols(target):
+        return pl.ds(pl.multiple_of(window_start(target, core), 128), WINDOW)
+
+    def block(owner, c):
+        return pl.ds(pl.multiple_of((c * 4 + owner) * 128, 128), 128)
+
+    mine = pl.ds(pl.multiple_of(core * half, half), half)
+    loads = [
+        (wq, bq, q_full.at[rows(shard)]),
+        (wo, bo, o_full.at[rows(shard)]),
+        (wg.at[:, cols(shard)], bg, g_own.at[rows(shard)]),
+        (wu.at[:, cols(shard)], bu, u_own.at[rows(shard)]),
+        (cot, bc, cot_all.at[block(shard, core)]),
+        (small, bs, small_all.at[shard]),
+    ]
+    items = [
+        (lambda t: small, lambda o: small_all.at[o], False),
+        (lambda t: wq.at[mine], lambda o: q_full.at[half_rows(o, core)], True),
+        (lambda t: wo.at[mine], lambda o: o_full.at[half_rows(o, core)], True),
+        (lambda t: cot, lambda o: cot_all.at[block(o, core)], True),
+        (lambda t: wg.at[:, cols(t)], lambda o: g_own.at[rows(o)], False),
+        (lambda t: wu.at[:, cols(t)], lambda o: u_own.at[rows(o)], False),
+    ]
+
+    def hop(i, d, t, o):
+        source, target, _ = items[i]
+        n = i * 3 + d - 1
+        return remote(source(t), target(o), send.at[n], recv.at[n], (replica, t))
+
+    def onward(i, d, ref):
+        n = i * 3 + d - 1
+        return remote(ref, ref, fsend.at[n], frecv.at[n], mate)
+
+    for i in range(len(items)):
+        for d in (3, 1, 2):
+            hop(i, d, peer_of(shard, d), shard).start()
+    own_block = remote(cot, cot_all.at[block(shard, core)], fsend.at[18], frecv.at[18], mate)
+    own_block.start()
+    for n, (src, buf, _) in enumerate(loads):
+        pltpu.make_async_copy(src, buf, local.at[n]).start()
+    for n, (src, buf, dst) in enumerate(loads):
+        pltpu.make_async_copy(src, buf, local.at[n]).wait()
+        pltpu.make_async_copy(buf, dst, local.at[n]).start()
+    for i, (_, target, passed) in enumerate(items):
+        for d in (3, 1, 2):
+            p = peer_of(shard, d)
+            hop(i, d, p, p).wait_recv()
+            if passed:
+                onward(i, d, target(p)).start()
+    for i, (_, target, passed) in enumerate(items):
+        for d in (3, 1, 2):
+            p = peer_of(shard, d)
+            hop(i, d, p, shard).wait_send()
+            if passed:
+                onward(i, d, target(p)).wait_send()
+    other = 1 - core
+    arrivals = {1: lambda o: q_full.at[half_rows(o, other)], 2: lambda o: o_full.at[half_rows(o, other)],
+                3: lambda o: cot_all.at[block(o, other)]}
+    for i, target in arrivals.items():
+        for d in (3, 1, 2):
+            onward(i, d, target(peer_of(shard, d))).wait_recv()
+    own_block.wait_send()
+    remote(cot, cot_all.at[block(shard, other)], fsend.at[18], frecv.at[18], mate).wait_recv()
+    for n, (src, buf, dst) in enumerate(loads):
+        pltpu.make_async_copy(buf, dst, local.at[n]).wait()
+
+
+def any_spec():
+    return pl.BlockSpec(memory_space=pl.ANY)
+
+
+def vmem_spec():
+    return pl.BlockSpec(memory_space=pltpu.VMEM)
+
+
+def params(**more):
+    return pltpu.CompilerParams(has_side_effects=True, vmem_limit_bytes=VMEM_BYTES, **more)
+
+
+def front(wq, wo, wg, wu, cot, small):
+    bf16 = jnp.bfloat16
+    shapes = [(1536, 2048), (1536, 1536), (1536, WINDOW), (1536, WINDOW), (1024, 1536), (4, 16, 512)]
+    bounce = [wq.shape, wo.shape, (384, WINDOW), (384, WINDOW), cot.shape, small.shape]
+    return pl.pallas_call(
+        front_kernel,
+        out_shape=[jax.ShapeDtypeStruct(s, bf16) for s in shapes],
+        in_specs=[any_spec()] * 6,
+        out_specs=[any_spec()] * 6,
+        scratch_shapes=[pltpu.VMEM(s, bf16) for s in bounce]
+        + [
+            pltpu.SemaphoreType.DMA((18,)),
+            pltpu.SemaphoreType.DMA((18,)),
+            pltpu.SemaphoreType.DMA((19,)),
+            pltpu.SemaphoreType.DMA((19,)),
+            pltpu.SemaphoreType.DMA((6,)),
+        ],
+        compiler_params=params(),
+    )(wq, wo, wg, wu, cot, small)
+
+
+def gather_kernel(x, out, send, recv, fsend, frecv, local):
+    replica, shard, core = place()
+    mate = (replica + 1 - 2 * core, shard)
+
+    def block(owner, c):
+        return out.at[pl.ds(pl.multiple_of((c * 4 + owner) * 128, 128), 128)]
+
+    for d in (3, 1, 2):
+        remote(x, block(shard, core), send.at[d], recv.at[d], (replica, peer_of(shard, d))).start()
+    remote(x, block(shard, core), fsend.at[0], frecv.at[0], mate).start()
+    own = pltpu.make_async_copy(x, block(shard, core), local)
+    own.start()
+    for d in (1, 2, 3):
+        p = peer_of(shard, d)
+        remote(x, block(p, core), send.at[d], recv.at[d], (replica, p)).wait_recv()
+        remote(block(p, core), block(p, core), fsend.at[d], frecv.at[d], mate).start()
+    own.wait()
+    for d in (1, 2, 3):
+        p = peer_of(shard, d)
+        remote(x, block(shard, core), send.at[d], recv.at[d], (replica, p)).wait_send()
+        remote(block(p, core), block(p, core), fsend.at[d], frecv.at[d], mate).wait_send()
+        remote(x, block(p, 1 - core), fsend.at[d], frecv.at[d], mate).wait_recv()
+    remote(x, block(shard, core), fsend.at[0], frecv.at[0], mate).wait_send()
+    remote(x, block(shard, 1 - core), fsend.at[0], frecv.at[0], mate).wait_recv()
+
+
+def plane_gather(x):
+    return pl.pallas_call(
+        gather_kernel,
+        out_shape=jax.ShapeDtypeStruct((x.shape[0] * 8, x.shape[1]), x.dtype),
+        in_specs=[vmem_spec()],
+        out_specs=vmem_spec(),
+        scratch_shapes=[pltpu.SemaphoreType.DMA((4,))] * 4 + [pltpu.SemaphoreType.DMA],
+        compiler_params=params(),
+    )(x)
+
+
+def scatter_kernel(pa, pb, oa, ob, held, sums, parts, csend, crecv, send, recv):
+    replica, shard, core = place()
+    mate = (replica + 1 - 2 * core, shard)
+    f32 = jnp.float32
+    inputs = (pa, pb)
+    outputs = (oa, ob)
+
+    def block(c, target):
+        return pl.ds(pl.multiple_of((c * 4 + target) * 128, 128), 128)
+
+    order = (3, 1, 2, 0)
+    for a in range(2):
+        for d in order:
+            t = peer_of(shard, d)
+            remote(inputs[a].at[block(1 - core, t)], held.at[a, d], csend.at[a * 4 + d], crecv.at[a * 4 + d], mate).start()
+
+    def summed(a, d):
+        t = peer_of(shard, d)
+        n = a * 4 + d
+        remote(inputs[a].at[block(core, t)], held.at[a, d], csend.at[n], crecv.at[n], mate).wait_recv()
+        return inputs[a][block(core, t), :].astype(f32) + held[a, d].astype(f32)
+
+    for a in range(2):
+        for d in (3, 1, 2):
+            sums[a, d - 1] = summed(a, d).astype(sums.dtype)
+            n = a * 3 + d - 1
+            remote(sums.at[a, d - 1], parts.at[a, d - 1], send.at[n], recv.at[n], (replica, peer_of(shard, d))).start()
+    for a in range(2):
+        outputs[a][...] = summed(a, 0)
+    for a in range(2):
+        for d in (1, 2, 3):
+            n = a * 3 + d - 1
+            remote(sums.at[a, d - 1], parts.at[a, d - 1], send.at[n], recv.at[n], (replica, peer_of(shard, d))).wait()
+            outputs[a][...] += parts[a, d - 1].astype(f32)
+    for a in range(2):
+        for d in order:
+            t = peer_of(shard, d)
+            n = a * 4 + d
+            remote(inputs[a].at[block(1 - core, t)], held.at[a, d], csend.at[n], crecv.at[n], mate).wait_send()
+
+
+def plane_scatter(pa, pb):
+    width = pa.shape[1]
+    bf16 = jnp.bfloat16
+    out = jax.ShapeDtypeStruct((128, width), jnp.float32)
+    return pl.pallas_call(
+        scatter_kernel,
+        out_shape=[out, out],
+        in_specs=[vmem_spec()] * 2,
+        out_specs=[vmem_spec()] * 2,
+        scratch_shapes=[
+            pltpu.VMEM((2, 4, 128, width), bf16),
+            pltpu.VMEM((2, 3, 128, width), bf16),
+            pltpu.VMEM((2, 3, 128, width), bf16),
+            pltpu.SemaphoreType.DMA((8,)),
+            pltpu.SemaphoreType.DMA((8,)),
+            pltpu.SemaphoreType.DMA((6,)),
+            pltpu.SemaphoreType.DMA((6,)),
+        ],
+        compiler_params=params(),
+    )(pa, pb)
+
+
+def attn_gather_kernel(ctx, nrm, hid, prj, ctx_all, nrm_all, hid_all, prj_all, send, recv, fsend, frecv, local):
+    replica, shard, core = place()
+    other = 1 - core
+    mate = (replica + 1 - 2 * core, shard)
+
+    def block(out, owner, c):
+        return out.at[pl.ds(pl.multiple_of((c * 4 + owner) * 128, 128), 128)]
+
+    def part(ref, index, width):
+        return ref.at[:, pl.ds(pl.multiple_of(index * width, width), width)]
+
+    def device(c, t):
+        return (replica - core + c, t)
+
+    wide = ((hid, hid_all, 768), (prj, prj_all, 1024))
+    narrow = ((ctx, ctx_all, 384), (nrm, nrm_all, 384))
+    def wide_copy(a, d, same, source_core, owner, t):
+        ref, out, width = wide[a]
+        c = core if same else other
+        n = (a * 4 + d) * 2 + (0 if same else 1)
+        return remote(part(ref, c, width), block(out, owner, source_core), send.at[n], recv.at[n], device(c, t))
+
+    def narrow_copy(a, d, owner, t):
+        ref, out, width = narrow[a]
+        n = 16 + a * 4 + d
+        return remote(part(ref, t, width), block(out, owner, core), send.at[n], recv.at[n], (replica, t))
+
+    def onward(a, d, source, owner, c):
+        _, out, _ = narrow[a]
+        n = a * 4 + d
+        return remote(source, block(out, owner, c), fsend.at[n], frecv.at[n], mate)
+
+    for d in (3, 1, 2, 0):
+        t = peer_of(shard, d)
+        for a in range(2):
+            if d:
+                wide_copy(a, d, True, core, shard, t).start()
+            wide_copy(a, d, False, core, shard, t).start()
+            if d:
+                narrow_copy(a, d, shard, t).start()
+            else:
+                ref, out, width = narrow[a]
+                onward(a, 0, part(ref, shard, width), shard, core).start()
+    locals_ = []
+    for a in range(2):
+        ref, out, width = narrow[a]
+        locals_.append(pltpu.make_async_copy(part(ref, shard, width), block(out, shard, core), local.at[a]))
+        ref, out, width = wide[a]
+        locals_.append(pltpu.make_async_copy(part(ref, core, width), block(out, shard, core), local.at[2 + a]))
+    for copy in locals_:
+        copy.start()
+    for d in (1, 2, 3):
+        p = peer_of(shard, d)
+        for a in range(2):
+            narrow_copy(a, d, p, p).wait_recv()
+            onward(a, d, block(narrow[a][1], p, core), p, core).start()
+    for copy in locals_:
+        copy.wait()
+    for d in (0, 1, 2, 3):
+        p = peer_of(shard, d)
+        for a in range(2):
+            if d:
+                wide_copy(a, d, True, core, p, p).wait_recv()
+                wide_copy(a, d, True, core, shard, p).wait_send()
+                narrow_copy(a, d, shard, p).wait_send()
+            wide_copy(a, d, False, other, p, p).wait_recv()
+            wide_copy(a, d, False, core, shard, p).wait_send()
+            onward(a, d, block(narrow[a][1], p, core), p, core).wait_send()
+            onward(a, d, block(narrow[a][1], p, other), p, other).wait_recv()
+
+
+def attn_gather(ctx, nrm, hid, prj):
+    bf16 = jnp.bfloat16
+    shapes = [(1024, 384), (1024, 384), (1024, 768), (1024, 1024)]
+    return pl.pallas_call(
+        attn_gather_kernel,
+        out_shape=[jax.ShapeDtypeStruct(s, bf16) for s in shapes],
+        in_specs=[vmem_spec()] * 4,
+        out_specs=[vmem_spec()] * 4,
+        scratch_shapes=[
+            pltpu.SemaphoreType.DMA((24,)),
+            pltpu.SemaphoreType.DMA((24,)),
+            pltpu.SemaphoreType.DMA((8,)),
+            pltpu.SemaphoreType.DMA((8,)),
+            pltpu.SemaphoreType.DMA((4,)),
+        ],
+        compiler_params=params(),
+    )(ctx, nrm, hid, prj)
+
+
+CHUNK = 128
+
+
+def reduce_kernel(
+    levels, pa, pd, pg, pu, fa, fd, fg, fu,
+    own_a, own_d, own_g, low_a, low_d, low_g, high_a, high_d, high_g,
+    xsend, xrecv, up_sem, down_sem, low_sem, high_sem, mate_send, mate_recv, out_sem, in_sem,
+):
+    replica, shard, core = place()
+    level = replica // 2
+    mate = (replica + 1 - 2 * core, shard)
+    above, below = (replica + 2, shard), (replica - 2, shard)
+    f32 = jnp.float32
+    sources = (pg, pu)
+
+    def exchange(a, d, p):
+        rows = pl.ds(pl.multiple_of(p * 384, 384), 384)
+        n = a * 4 + d
+        return remote(sources[a].at[rows], own_g.at[pl.ds(a * 1536 + d * 384, 384)], xsend.at[n], xrecv.at[n], (replica, p))
+
+    fills = [
+        pltpu.make_async_copy(pa, own_a, in_sem.at[0]),
+        pltpu.make_async_copy(pd, own_d, in_sem.at[1]),
+    ]
+    for a in range(2):
+        rows = pl.ds(pl.multiple_of(shard * 384, 384), 384)
+        fills.append(pltpu.make_async_copy(sources[a].at[rows], own_g.at[pl.ds(a * 1536, 384)], in_sem.at[2 + a]))
+    for copy in fills:
+        copy.start()
+    for a in range(2):
+        for d in (1, 2, 3):
+            exchange(a, d, peer_of(shard, d)).start()
+
+    chunks = []
+    for k in range(3):
+        at = pl.ds(k * CHUNK, CHUNK)
+        chunks.append((own_a, low_a, high_a, at, ("fill", 0), lambda c, at=at: fa.at[c, at]))
+    for k in range(9):
+        at = pl.ds(k * CHUNK, CHUNK)
+        chunks.append((own_d, low_d, high_d, at, ("fill", 1), lambda c, at=at: fd.at[c, at]))
+    for d in range(4):
+        for a in range(2):
+            for k in range(3):
+                at = pl.ds(a * 1536 + d * 384 + k * CHUNK, CHUNK)
+                dst = (fg, fu)[a]
+                source = peer_of(shard, d)
+                chunks.append((
+                    own_g, low_g, high_g, at, ("fill", 2 + a) if d == 0 else ("x", a, d),
+                    lambda c, k=k, dst=dst, source=source: dst.at[c, source, pl.ds(k * CHUNK, CHUNK)],
+                ))
+    total = len(chunks)
+    awaited = set()
+
+    def arrive(what):
+        if what in awaited:
+            return
+        awaited.add(what)
+        if what[0] == "fill":
+            fills[what[1]].wait()
+        else:
+            exchange(what[1], what[2], peer_of(shard, what[2])).wait_recv()
+
+    def up(k, ref):
+        own, low, high, at, _, _ = chunks[k]
+        return remote(ref.at[at], low.at[at], up_sem.at[k], low_sem.at[k], above)
+
+    def down(k, ref):
+        own, low, high, at, _, _ = chunks[k]
+        return remote(ref.at[at], high.at[at], down_sem.at[k], high_sem.at[k], below)
+
+    def add(k, *refs):
+        own, _, _, at, _, _ = chunks[k]
+        step = 32
+
+        def body(j, carry):
+            rows = pl.ds(pl.multiple_of(at.start + j * step, step), step)
+            value = own[rows, :].astype(f32)
+            for ref in refs:
+                value = value + ref[rows, :].astype(f32)
+            own[rows, :] = value.astype(own.dtype)
+            return carry
+
+        lax.fori_loop(0, CHUNK // step, body, 0)
+
+    def finish(k, ref):
+        _, _, _, at, _, dst = chunks[k]
+        pltpu.make_async_copy(ref.at[at], dst(core), out_sem.at[k]).start()
+        remote(ref.at[at], dst(core), mate_send.at[k], mate_recv.at[k], mate).start()
+
+    def root_of(k):
+        return levels // 2 - 1 + k % 2
+
+    def gather_step(k):
+        own, low, high, at, what, _ = chunks[k]
+        arrive(what)
+        root = root_of(k)
+
+        @pl.when(level < root)
+        def _():
+            if root > 1:
+
+                @pl.when(level > 0)
+                def _():
+                    up(k, own).wait_recv()
+                    add(k, low)
+
+            up(k, own).start()
+
+        @pl.when(level > root)
+        def _():
+            if root < levels - 2:
+
+                @pl.when(level < levels - 1)
+                def _():
+                    down(k, own).wait_recv()
+                    add(k, high)
+
+            down(k, own).start()
+
+    def root_step(k):
+        own, low, high, at, _, _ = chunks[k]
+
+        @pl.when(level == root_of(k))
+        def _():
+            up(k, own).wait_recv()
+            down(k, own).wait_recv()
+            add(k, low, high)
+            up(k, own).start()
+            down(k, own).start()
+            finish(k, own)
+
+    def spread_step(k):
+        own, low, high, at, _, _ = chunks[k]
+        root = root_of(k)
+
+        @pl.when(level < root)
+        def _():
+            down(k, own).wait_recv()
+            if root > 1:
+
+                @pl.when(level > 0)
+                def _():
+                    down(k, high).start()
+
+            finish(k, high)
+
+        @pl.when(level > root)
+        def _():
+            up(k, own).wait_recv()
+            if root < levels - 2:
+
+                @pl.when(level < levels - 1)
+                def _():
+                    up(k, low).start()
+
+            finish(k, low)
+
+    for t in range(total + 6):
+        if t < total:
+            gather_step(t)
+        if 0 <= t - 3 < total:
+            root_step(t - 3)
+        if 0 <= t - 6 < total:
+            spread_step(t - 6)
+    for a in range(2):
+        for d in (1, 2, 3):
+            exchange(a, d, peer_of(shard, d)).wait_send()
+    for k in range(total):
+        own, low, high, at, _, dst = chunks[k]
+
+        @pl.when(level < levels - 1)
+        def _():
+            up(k, own).wait_send()
+
+        @pl.when(level > 0)
+        def _():
+            down(k, own).wait_send()
+
+        pltpu.make_async_copy(own.at[at], dst(core), out_sem.at[k]).wait()
+        remote(own.at[at], dst(core), mate_send.at[k], mate_recv.at[k], mate).wait_send()
+        remote(own.at[at], dst(1 - core), mate_send.at[k], mate_recv.at[k], mate).wait_recv()
+
+
+def reduce_gradients(levels, pa, pd, pg, pu):
+    bf16 = jnp.bfloat16
+    shapes = [(2, 384, 1792), (2, WINDOW, 1536), (2, 4, 384, WINDOW), (2, 4, 384, WINDOW)]
+    buffers = [(384, 1792), (WINDOW, 1536), (3072, WINDOW)]
+    total = 36
+    dma = pltpu.SemaphoreType.DMA
+    return pl.pallas_call(
+        functools.partial(reduce_kernel, levels),
+        out_shape=[jax.ShapeDtypeStruct(s, bf16) for s in shapes],
+        in_specs=[any_spec()] * 4,
+        out_specs=[any_spec()] * 4,
+        scratch_shapes=[pltpu.VMEM(s, bf16) for s in buffers * 3]
+        + [dma((8,)), dma((8,))]
+        + [dma((total,))] * 7
+        + [dma((4,))],
+        compiler_params=params(),
+    )(pa, pd, pg, pu)
+
+
+def widen_kernel(x, out):
+    f32 = jnp.float32
+    for s in range(4):
+        for c in range(2):
+            first = (s * 35) // 2 + c * 9
+            joined = s % 2 == 1 and c == 0
+            rest = 1 if joined else 0
+            out[:, (first + rest) * 128 : (first + 9) * 128] = x[c, s][:, rest * 128 :].astype(f32)
+    for s in (1, 3):
+        first = (s * 35) // 2
+        out[:, first * 128 : (first + 1) * 128] = x[1, s - 1][:, 1024:].astype(f32) + x[0, s][:, :128].astype(f32)
+
+
+def widen(x):
+    rows = 32
+    return pl.pallas_call(
+        widen_kernel,
+        grid=(384 // rows,),
+        out_shape=jax.ShapeDtypeStruct((384, 8960), jnp.float32),
+        in_specs=[pl.BlockSpec((2, 4, rows, WINDOW), lambda i: (0, 0, i, 0))],
+        out_specs=pl.BlockSpec((rows, 8960), lambda i: (i, 0)),
+    )(x)
+
+
+def fast_device(
+    block_input,
+    attn_gain,
+    qkv_weight,
+    qkv_bias,
+    out_weight,
+    mlp_gain,
+    gate_weight,
+    up_weight,
+    down_weight,
+    cotangent,
+):
+    f32 = jnp.float32
+    bf16 = jnp.bfloat16
+    tok_count = block_input.shape[0]
+    levels = lax.axis_size("replica") // 2
+    grad_scale = 1.0 / math.sqrt(tok_count * lax.axis_size("replica") * lax.axis_size("shard"))
+    q_width = HEADS * HD
+    k_end = q_width + KV * HD
+    replica, shard, core = place()
+    cosine, sine_table = rope_tables(tok_count)
+    small = jnp.zeros((16, 512), bf16)
+    small = small.at[0, :384].set(attn_gain).at[1, :].set(qkv_bias).at[2, :384].set(mlp_gain)
+    qkv_full, out_full, gate_own, up_own, cot_all, small_all = front(
+        qkv_weight, out_weight, gate_weight, up_weight, cotangent, small
+    )
+    gain_one = small_all[:, 0, :384].reshape(-1).astype(f32)
+    bias = small_all[:, 1, :].reshape(-1).astype(f32)
+    gain_two = small_all[:, 2, :384].reshape(-1).astype(f32)
+
+    xfloat = block_input.astype(f32)
+    inv_one = lax.rsqrt(jnp.mean(xfloat * xfloat, axis=-1, keepdims=True) + NORM_EPS)
+    normed_one = (xfloat * inv_one * gain_one).astype(bf16)
+    projected = jnp.dot(normed_one, qkv_full, preferred_element_type=f32) + bias
+    queries = rotate(projected[:, :q_width].reshape(tok_count, HEADS, HD), cosine, sine_table).astype(bf16)
+    queries = queries.reshape(tok_count, KV, HEADS // KV, HD)
+    key_rot = rotate(projected[:, q_width:k_end].reshape(tok_count, KV, HD), cosine, sine_table).astype(bf16)
+    values = projected[:, k_end:].reshape(tok_count, KV, HD).astype(bf16)
+    context, logsum = attend_forward(queries, key_rot, values)
+    hidden_res = xfloat + jnp.dot(context, out_full, preferred_element_type=f32)
+    inv_two = lax.rsqrt(jnp.mean(hidden_res * hidden_res, axis=-1, keepdims=True) + NORM_EPS)
+    normed_two = (hidden_res * inv_two * gain_two).astype(bf16)
+
+    normed_all = plane_gather(normed_two)
+    first = window_start(shard, core)
+    column = first + jnp.arange(WINDOW)
+    owned = (column >= shard * 2240) & (column < (shard + 1) * 2240)
+    padded = jnp.pad(down_weight, ((64, 64), (0, 0)))
+    down_own = lax.dynamic_slice_in_dim(padded, first - shard * 2240 + 64, WINDOW, 0)
+    gate_pre = jnp.dot(normed_all, gate_own, preferred_element_type=f32)
+    up_pre = jnp.dot(normed_all, up_own, preferred_element_type=f32)
+    sigmoid_gate = jax.nn.sigmoid(gate_pre)
+    silu_gate = gate_pre * sigmoid_gate
+    act_grad = jnp.einsum("td,fd->tf", cot_all, down_own, preferred_element_type=f32)
+    activation = jnp.where(owned, silu_gate * up_pre, 0.0).astype(bf16)
+    gate_delta = jnp.where(
+        owned, act_grad * up_pre * sigmoid_gate * (1.0 + gate_pre * (1.0 - sigmoid_gate)), 0.0
+    ).astype(bf16)
+    up_delta = jnp.where(owned, act_grad * silu_gate, 0.0).astype(bf16)
+    down_out = jnp.dot(activation, down_own, preferred_element_type=f32).astype(bf16)
+    back = (
+        jnp.einsum("tf,df->td", gate_delta, gate_own, preferred_element_type=f32)
+        + jnp.einsum("tf,df->td", up_delta, up_own, preferred_element_type=f32)
+    ).astype(bf16)
+    gate_part = (jnp.einsum("td,tf->df", normed_all, gate_delta, preferred_element_type=f32) * grad_scale).astype(bf16)
+    up_part = (jnp.einsum("td,tf->df", normed_all, up_delta, preferred_element_type=f32) * grad_scale).astype(bf16)
+    down_part = (jnp.einsum("tf,td->fd", activation, cot_all, preferred_element_type=f32) * grad_scale).astype(bf16)
+
+    down_sum, normed_two_grad = plane_scatter(down_out, back)
+    block_output = (hidden_res + down_sum).astype(bf16)
+    gain_two_grad = jnp.sum(normed_two_grad * hidden_res * inv_two, axis=0) * grad_scale
+    hidden_grad = cotangent.astype(f32) + inv_two * (
+        gain_two * normed_two_grad
+        - hidden_res
+        * inv_two
+        * inv_two
+        * jnp.mean(gain_two * normed_two_grad * hidden_res, axis=-1, keepdims=True)
+    )
+    hidden_low = hidden_grad.astype(bf16)
+    context_grad = jnp.einsum("td,ed->te", hidden_low, out_full, preferred_element_type=f32).astype(bf16)
+    query_grad, key_grad, value_grad = attend_backward(queries, key_rot, values, logsum, context_grad)
+    query_grad = unrotate(query_grad, cosine, sine_table).reshape(tok_count, q_width)
+    key_grad = unrotate(key_grad, cosine, sine_table).reshape(tok_count, KV * HD)
+    projected_grad = jnp.concatenate(
+        [query_grad, key_grad, value_grad.reshape(tok_count, KV * HD)], axis=-1
+    ).astype(bf16)
+    normed_one_grad = jnp.einsum("tc,dc->td", projected_grad, qkv_full, preferred_element_type=f32)
+    gain_one_grad = jnp.sum(normed_one_grad * xfloat * inv_one, axis=0) * grad_scale
+    bias_grad = jnp.sum(projected_grad.astype(f32), axis=0) * grad_scale
+    input_grad = hidden_grad + inv_one * (
+        gain_one * normed_one_grad
+        - xfloat
+        * inv_one
+        * inv_one
+        * jnp.mean(gain_one * normed_one_grad * xfloat, axis=-1, keepdims=True)
+    )
+    vectors = lax.psum(jnp.concatenate([gain_one_grad, bias_grad, gain_two_grad]), ("replica", "shard"))
+    gain_one_own = lax.dynamic_slice_in_dim(vectors, shard * 384, 384)
+    bias_own = lax.dynamic_slice_in_dim(vectors, 1536 + shard * 512, 512)
+    gain_two_own = lax.dynamic_slice_in_dim(vectors, 3584 + shard * 384, 384)
+
+    ctx_rows, normed_rows, hidden_rows, projected_rows = attn_gather(context, normed_one, hidden_low, projected_grad)
+    qkv_part = jnp.einsum("td,tc->dc", normed_rows, projected_rows, preferred_element_type=f32)
+    out_part = jnp.einsum("te,td->ed", ctx_rows, hidden_rows, preferred_element_type=f32)
+    attn_part = (jnp.concatenate([qkv_part, out_part], axis=1) * grad_scale).astype(bf16)
+
+    sum_attn, sum_down, sum_gate, sum_up = reduce_gradients(levels, attn_part, down_part, gate_part, up_part)
+    qkv_grad = jnp.concatenate([sum_attn[0, :, :1024], sum_attn[1, :, :1024]], axis=1).astype(f32)
+    out_grad = jnp.concatenate([sum_attn[0, :, 1024:], sum_attn[1, :, 1024:]], axis=1).astype(f32)
+    down_grad = lax.dynamic_slice_in_dim(
+        sum_down.reshape(2 * WINDOW, 1536), lax.rem(shard, 2) * 64, 2240, 0
+    ).astype(f32)
+    return (
+        block_output,
+        input_grad,
+        gain_one_own,
+        qkv_grad,
+        bias_own,
+        out_grad,
+        gain_two_own,
+        widen(sum_gate),
+        widen(sum_up),
+        down_grad,
+    )
+
+
 def solution(mesh):
     placed = (
         P(("replica", "shard"), None),
@@ -305,6 +997,8 @@
         P("shard", None),
         P(("replica", "shard"), None),
     )
+    fits = mesh.shape["shard"] == 4 and mesh.shape["replica"] % 2 == 0 and mesh.shape["replica"] >= 8
+    per_device = fast_device if fits else general_device
     return jax.shard_map(
         per_device,
         mesh=mesh,

time: 2180 us -> 960 us (0.44)
  waiting for transfers between devices: 1840 us -> 0 us
  Pallas kernels: 0 us -> 790 us
  matrix products: 168 us -> 83.2 us
  local copies, waits for them, and re-layouts: 59.5 us -> 11.6 us
    all_gather x10 -> x0, waiting for transfers between devices: 964 us -> none  [the longest x1 246 us: per_device(): lax.all_gather(gate_weight, 'shard', axis=0, tiled=True)]
    psum x1 -> x0, waiting for transfers between devices: 841 us -> none  [per_device(): lax.psum((attn_parts[0], attn_parts[1], attn_parts[2], attn_parts[3], mlp...]
    pallas_call x0 -> x7, Pallas kernels: none -> 790 us  [the longest x1 467 us: reduce_gradients(): pl.pallas_call(functools.partial(reduce_kernel, levels), out_shape=[jax.S...]
    dot_general x15, matrix products: 158 us -> 77.3 us  [the longest x1 9.41 us: fast_device(): jnp.einsum('td,fd->tf', cot_all, down_own, preferred_element_type=f32)]
    unnamed x86 -> x98, local copies, waits for them, and re-layouts: 41.1 us -> 2.43 us
    all_to_all x4 -> x0, waiting for transfers between devices: 28.8 us -> none  [the longest x1 22.8 us: per_device(): lax.all_to_all(activation, 'shard', split_axis=1, concat_axis=0, tiled=True)]
    all_gather x3 -> x0, blocking collectives: 25.4 us -> none  [the longest x1 9.56 us: per_device(): lax.all_gather(attn_gain, 'shard', axis=0, tiled=True)]
    psum x1, blocking collectives: 15.8 us -> 39.8 us  [fast_device(): lax.psum(jnp.concatenate([gain_one_grad, bias_grad, gain_two_grad]), ('re...]
  transfers between devices with their start and end apart: 15 -> 0, of which waited for: 11 -> 0; matrix products, arithmetic and copies ran while one was open for 9% -> 0% of each run, Pallas kernels for 0% -> 0%
where the time goes in v1:
time: 960 us; the launch traced here: 954 us
  Pallas kernels  790 us (82%)
  matrix products  83.2 us (9%)
  blocking collectives  39.8 us (4%)
  other arithmetic  27.3 us (3%)
  local copies, waits for them, and re-layouts  11.6 us (1%)
    pallas_call x1, Pallas kernels, reduce_gradients(): pl.pallas_call(functools.partial(reduce_kernel, levels), out_shape=[jax.S...  467 us
    pallas_call x1, Pallas kernels, front(): pl.pallas_call(front_kernel, out_shape=[jax.ShapeDtypeStruct(s, bf16) for...  164 us
    pallas_call x1, Pallas kernels, attn_gather(): pl.pallas_call(attn_gather_kernel, out_shape=[jax.ShapeDtypeStruct(s, bf1...  60.8 us
    pallas_call x1, Pallas kernels, plane_scatter(): pl.pallas_call(scatter_kernel, out_shape=[out, out], in_specs=[vmem_spec(...  48 us
    psum x1, blocking collectives, fast_device(): lax.psum(jnp.concatenate([gain_one_grad, bias_grad, gain_two_grad]), ('re...  39.8 us
    pallas_call x1, Pallas kernels, plane_gather(): pl.pallas_call(gather_kernel, out_shape=jax.ShapeDtypeStruct((x.shape[0]...  29.6 us
    pallas_call x2, Pallas kernels, widen(): pl.pallas_call(widen_kernel, grid=(384 // rows,), out_shape=jax.ShapeDtyp...  21.8 us

profile of v1, /device:TPU:0, one launch (start us, length us, event | category | flops | bytes accessed | tf_op | source)
XLA Modules:
  0.0 954.3 jit_solution(4475227644205695638)
XLA Ops:
  0.7 1.2 fusion.23
  1.9 0.6 fusion.35
  2.5 0.7 reshape.240
  3.1 0.7 reshape.242
  3.8 0.7 reshape.241
  4.8 0.6 iota_compare_fusion
  5.9 163.6 %shard_map.177 = (bf16[1536,2048]{1,0:T(8,128)(2,1)}, bf16[1536,1536]{1,0:T(8,128)(2,1)}, bf16[1536,1152]{1,0:T(8,128)(2,1)}, bf16[1536,1152]{1,0:T(8,128)(2,1)}...) custom-call(bf16[384,2048]{1,0:T(8,128)(2,1)} %wq.1, bf16[384,1536]{1,0:T(8,128)(2,1)} %wo.1, ...), custom_call_target="tpu_custom_call" | custom-call | tf_op jit(solution)/shard_map/pallas_call | solution.py:428
  169.5 0.8 slice_convert_fusion.1
  170.3 0.9 convert_reduce_fusion.1
  171.8 3.9 convolution_add_fusion.1
  178.2 1.0 copy.61.ctx
  179.2 3.2 multiply_reduce_fusion.2
  182.9 0.9 multiply_convert_fusion.x
  183.8 29.6 %shard_map.178 = bf16[1024,1536]{1,0:T(8,128)(2,1)} custom-call(bf16[128,1536]{1,0:T(8,128)(2,1)} %multiply_convert_fusion.x), custom_call_target="tpu_custom_call" | custom-call | tf_op jit(solution)/shard_map/pallas_call | solution.py:472
  213.4 7.3 fusion.52
  220.8 5.8 fusion.51
  226.7 9.4 select_convert_fusion
  236.1 5.4 fusion.1.pd
  241.5 5.8 convolution_convert_fusion.pa
  247.3 4.3 fusion.53
  251.6 5.7 add_convert_fusion.pb
  257.3 48.0 %shard_map.179 = (f32[128,1536]{1,0:T(8,128)}, f32[128,1536]{1,0:T(8,128)}) custom-call(bf16[1024,1536]{1,0:T(8,128)(2,1)} %convolution_convert_fusion.pa, bf16[1024,1536]{1,0:T(8,128)(2,1)} %add_convert_fusion.pb), custom_call_target="tpu_custom_call" | custom-call | tf_op jit(solution)/shard_map/pallas_call | solution.py:527
  305.3 2.0 multiply_reduce_fusion
  307.8 1.4 fusion.47.hid
  309.2 0.8 copy-done.6
  310.0 4.0 convolution_convert_fusion.1
  314.7 1.1 convolution_bitcast_fusion
  315.8 1.9 convolution_bitcast_fusion.1
  317.8 1.8 fusion.15
  320.4 5.4 fusion.26
  325.8 39.8 %psum.7 = f32[5120]{0:T(1024)S(1)} all-reduce(f32[5120]{0:T(1024)S(1)} %pad_maximum_fusion.5), channel_id=1, replica_groups=mesh['replica'=8,'shard'=4] {'replica','shard'}, use_global_device_ids=true, to_apply=%region_10.11 | all-reduce | flops 5120 | bytes 40960 | tf_op jit(solution)/shard_map/psum | solution.py:957
  365.6 2.7 fusion.22
  368.3 0.7 dynamic_slice.32
  369.0 0.7 fusion.49
  369.6 7.6 fusion.3.pu
  377.2 5.7 fusion.2.pg
  382.9 60.8 %shard_map.180 = (bf16[1024,384]{1,0:T(8,128)(2,1)}, bf16[1024,384]{1,0:T(8,128)(2,1)}, bf16[1024,768]{1,0:T(8,128)(2,1)}, bf16[1024,1024]{1,0:T(8,128)(2,1)}) custom-call(bf16[128,1536]{1,0:T(8,128)(2,1)} %copy.61.ctx, bf16[128,1536]{1,0:T(8,128)(2,1)} %copy-done.2, bf16[128,1536]{1,0:T(8,128)(2,1)} %copy-done.6, bf16[128,2048]{1,0:T(8,128)(2,1)} %copy-done.3), custom_call_target="tpu_custom_call" | custom-call | tf_op jit(solution)/shard_map/pallas_call | solution.py:619
  443.8 3.0 fusion.54
  446.8 0.8 fusion.55
  447.6 1.2 fusion.5.pa
  448.9 466.5 %shard_map.181 = (bf16[2,384,1792]{2,1,0:T(8,128)(2,1)}, bf16[2,1152,1536]{2,1,0:T(8,128)(2,1)}, bf16[2,4,384,1152]{3,2,1,0:T(8,128)(2,1)}, bf16[2,4,384,1152]{3,2,1,0:T(8,128)(2,1)}) custom-call(bf16[384,1792]{1,0:T(8,128)(2,1)} %fusion.5.pa, bf16[1152,1536]{1,0:T(8,128)(2,1)} %fusion.1.pd, bf16[1536,1152]{1,0:T(8,128)(2,1)} %fusion.2.pg, ...), custom_call_target="tpu_custom_call" | custom-call | tf_op jit(solution)/shard_map/pallas_call | solution.py:824
  915.4 1.3 slice_bitcast_fusion.3
  916.7 1.5 slice_bitcast_fusion.1
  918.2 1.7 maximum_convert_fusion.1
  919.9 2.0 maximum_convert_fusion
  922.0 10.9 %shard_map.182 = f32[384,8960]{1,0:T(8,128)} custom-call(bf16[2,4,384,1152]{3,2,1,0:T(8,128)(2,1)} %get-tuple-element.120.x), custom_call_target="tpu_custom_call" | custom-call | tf_op jit(solution)/shard_map/pallas_call | solution.py:852
  932.9 10.1 %dynamic-slice_convert_fusion = f32[2240,1536]{1,0:T(8,128)} fusion(bf16[2304,1536]{1,0:T(8,128)(2,1)} %bitcast.89, s32[]{:T(128)S(6)} %select_n.46), kind=kLoop, calls=%fused_computation.8 | loop fusion | flops 3440640 | bytes 20643844 | tf_op jit(solution)/shard_map/convert_element_type | solution.py:972
  942.9 10.9 %shard_map.183 = f32[384,8960]{1,0:T(8,128)} custom-call(bf16[2,4,384,1152]{3,2,1,0:T(8,128)(2,1)} %get-tuple-element.121.x), custom_call_target="tpu_custom_call" | custom-call | tf_op jit(solution)/shard_map/pallas_call | solution.py:852
  (140 shorter events, 6.0 us)
Async XLA Ops:
  1.8 169.3 %copy-start.36 = (f32[128]{0:T(128)}, f32[128]{0:T(128)S(1)}, u32[]{:S(2)}) copy-start(f32[128]{0:T(128)S(1)} %add_rsqrt_fusion.1) | copy-start | bytes 1540
  4.8 1.1 copy-start.32
  5.7 170.9 %copy-start.14 = (f32[128,64]{1,0:T(8,128)}, f32[128,64]{1,0:T(8,128)S(1)}, u32[]{:S(2)}) copy-start(f32[128,64]{1,0:T(8,128)S(1)} %get-tuple-element.153) | copy-start | bytes 98308
  5.7 170.4 %copy-start.23 = (f32[128,64]{0,1:T(8,128)}, f32[128,64]{0,1:T(8,128)S(1)}, u32[]{:S(2)}) copy-start(f32[128,64]{0,1:T(8,128)S(1)} %copy.43) | copy-start | bytes 98308
  5.9 170.3 %copy-start.25 = (f32[128,64]{0,1:T(8,128)}, f32[128,64]{0,1:T(8,128)S(1)}, u32[]{:S(2)}) copy-start(f32[128,64]{0,1:T(8,128)S(1)} %copy.44) | copy-start | bytes 98308
  5.9 165.3 %copy-start = (bf16[128,1536]{1,0:T(8,128)(2,1)S(1)}, bf16[128,1536]{1,0:T(8,128)(2,1)}, u32[]{:S(2)}) copy-start(bf16[128,1536]{1,0:T(8,128)(2,1)} %param.16) | copy-start | bytes 1179652
  171.2 11.3 %copy-start.27 = (f32[1536]{0:T(1024)}, f32[1536]{0:T(1024)S(1)}, u32[]{:S(2)}) copy-start(f32[1536]{0:T(1024)S(1)} %reshape.253) | copy-start | bytes 18436
  171.2 0.6 copy-start.29
  171.8 3.9 copy-start.2
  175.8 2.1 copy-start.17
  175.8 1.4 copy-start.31
  176.6 5.8 copy-start.19
  176.6 5.8 copy-start.21
  176.9 0.8 copy-start.10
  177.1 5.3 copy-start.12
  182.4 0.5 copy-start.34
  213.4 7.4 copy-start.7
  213.4 7.4 copy-start.42
  213.4 13.2 %slice-start = ((s8[6881280]{0:T(1024)(128)(4,1)}), s8[4194304]{0:T(1024)(128)(4,1)S(1)}, s32[]{:S(2)}) async-start(s8[6881280]{0:T(1024)(128)(4,1)} %bitcast.105), calls=%async_computation | async-start | bytes 8388608
  220.8 5.9 copy-start.40
  220.8 5.8 slice-start.1
  220.8 5.8 copy-start.43
  241.5 5.8 copy-start.44
  247.3 4.3 copy-start.41
  247.3 4.3 copy-start.46
  257.3 50.5 %copy-start.4 = (bf16[128,1536]{1,0:T(8,128)(2,1)S(1)}, bf16[128,1536]{1,0:T(8,128)(2,1)}, u32[]{:S(2)}) copy-start(bf16[128,1536]{1,0:T(8,128)(2,1)} %cot.1) | copy-start | bytes 1179652
  309.2 0.8 copy-start.6
  310.0 4.7 copy-start.18
  310.0 5.9 copy-start.11
  310.0 5.9 copy-start.13
  314.0 3.7 copy-start.20
  314.0 3.7 copy-start.22
  314.1 5.5 copy-start.15
  314.1 5.8 copy-start.24
  314.1 5.8 copy-start.26
  315.8 4.5 copy-start.30
  320.3 5.5 copy-start.3
  320.3 5.5 copy-start.33
  320.3 45.3 %copy-start.1 = (f32[128,1536]{1,0:T(8,128)S(1)}, f32[128,1536]{1,0:T(8,128)}, u32[]{:S(2)}) copy-start(f32[128,1536]{1,0:T(8,128)} %get-tuple-element.114) | copy-start | bytes 2359300
  320.3 45.3 %copy-start.5 = (bf16[128,1536]{1,0:T(8,128)(2,1)S(1)}, bf16[128,1536]{1,0:T(8,128)(2,1)}, u32[]{:S(2)}) copy-start(bf16[128,1536]{1,0:T(8,128)(2,1)} %cot.1) | copy-start | bytes 1179652
  320.4 45.3 %copy-start.28 = (f32[1536]{0:T(1024)S(1)}, f32[1536]{0:T(1024)}, u32[]{:S(2)}) copy-start(f32[1536]{0:T(1024)} %copy-done.27) | copy-start | bytes 18436
  320.4 45.3 %copy-start.35 = (f32[128]{0:T(128)S(1)}, f32[128]{0:T(128)}, u32[]{:S(2)}) copy-start(f32[128]{0:T(128)} %copy-done.34) | copy-start | bytes 1540
  320.4 45.3 %copy-start.37 = (f32[128]{0:T(128)S(1)}, f32[128]{0:T(128)}, u32[]{:S(2)}) copy-start(f32[128]{0:T(128)} %copy-done.36) | copy-start | bytes 1540
  320.4 45.3 %copy-start.39 = (f32[128]{0:T(128)S(1)}, f32[128]{0:T(128)}, u32[]{:S(2)}) copy-start(f32[128]{0:T(128)} %copy-done.38) | copy-start | bytes 1540
  365.6 4.0 copy-start.8
  369.6 7.6 copy-start.45
  443.8 3.0 copy-start.9
  443.8 3.0 copy-start.16
  (1 other events, 0.5 us)

commit v2 on v1

--- a/solution.py
+++ b/solution.py
@@ -330,25 +330,26 @@
 
 def front_kernel(
     wq, wo, wg, wu, cot, small, q_full, o_full, g_own, u_own, cot_all, small_all,
-    bq, bo, bg, bu, bc, bs, send, recv, fsend, frecv, local,
+    bq, bo, bg, bu, bc, bs, send, recv, fsend, frecv, zsend, zrecv, local,
 ):
     replica, shard, core = place()
+    other = 1 - core
     mate = (replica + 1 - 2 * core, shard)
-    half = 192
+    odd = lax.rem(replica // 2, 2)
+    pair = (replica + 2 - 4 * odd, shard)
+
+    def span(start, size):
+        return pl.ds(pl.multiple_of(start, 16), size)
+
+    def cols(target):
+        return pl.ds(pl.multiple_of(window_start(target, core), 128), WINDOW)
+
+    def block(owner, c):
+        return pl.ds(pl.multiple_of((c * 4 + owner) * 128, 128), 128)
 
     def rows(owner):
         return pl.ds(pl.multiple_of(owner * 384, 384), 384)
 
-    def half_rows(owner, c):
-        return pl.ds(pl.multiple_of(owner * 384 + c * half, half), half)
-
-    def cols(target):
-        return pl.ds(pl.multiple_of(window_start(target, core), 128), WINDOW)
-
-    def block(owner, c):
-        return pl.ds(pl.multiple_of((c * 4 + owner) * 128, 128), 128)
-
-    mine = pl.ds(pl.multiple_of(core * half, half), half)
     loads = [
         (wq, bq, q_full.at[rows(shard)]),
         (wo, bo, o_full.at[rows(shard)]),
@@ -357,54 +358,107 @@
         (cot, bc, cot_all.at[block(shard, core)]),
         (small, bs, small_all.at[shard]),
     ]
-    items = [
-        (lambda t: small, lambda o: small_all.at[o], False),
-        (lambda t: wq.at[mine], lambda o: q_full.at[half_rows(o, core)], True),
-        (lambda t: wo.at[mine], lambda o: o_full.at[half_rows(o, core)], True),
-        (lambda t: cot, lambda o: cot_all.at[block(o, core)], True),
-        (lambda t: wg.at[:, cols(t)], lambda o: g_own.at[rows(o)], False),
-        (lambda t: wu.at[:, cols(t)], lambda o: u_own.at[rows(o)], False),
+    weights = [
+        (lambda t: wq, q_full, 192, 80, True),
+        (lambda t: wo, o_full, 192, 80, True),
+        (lambda t: wg.at[:, cols(t)], g_own, 384, 176, False),
+        (lambda t: wu.at[:, cols(t)], u_own, 384, 176, False),
     ]
 
+    def base(i, c):
+        return c * 192 if weights[i][4] else 0
+
     def hop(i, d, t, o):
-        source, target, _ = items[i]
+        source, out, size, shared, _ = weights[i]
+        first = base(i, core) + odd * shared
         n = i * 3 + d - 1
-        return remote(source(t), target(o), send.at[n], recv.at[n], (replica, t))
-
-    def onward(i, d, ref):
+        return remote(
+            source(t).at[span(first, size - shared)], out.at[span(o * 384 + first, size - shared)],
+            send.at[n], recv.at[n], (replica, t),
+        )
+
+    def across(i, d, o, whose):
+        _, out, size, shared, _ = weights[i]
+        ref = out.at[span(o * 384 + base(i, core) + whose * (size - shared), shared)]
         n = i * 3 + d - 1
+        return remote(ref, ref, zsend.at[n], zrecv.at[n], pair)
+
+    def onward(i, d, o, c, shared_part):
+        _, out, size, shared, _ = weights[i]
+        first = o * 384 + base(i, c) + ((1 - odd) * (size - shared) if shared_part else odd * shared)
+        ref = out.at[span(first, shared if shared_part else size - shared)]
+        n = i * 3 + d - 1 + (6 if shared_part else 0)
         return remote(ref, ref, fsend.at[n], frecv.at[n], mate)
 
-    for i in range(len(items)):
-        for d in (3, 1, 2):
+    def cot_hop(d, t, o):
+        return remote(cot, cot_all.at[block(o, core)], send.at[11 + d], recv.at[11 + d], (replica, t))
+
+    def cot_onward(d, o, c):
+        ref = cot_all.at[block(o, c)] if d else cot
+        return remote(ref, cot_all.at[block(o, c)], fsend.at[12 + d], frecv.at[12 + d], mate)
+
+    def small_hop(d, t, o):
+        return remote(small, small_all.at[o], send.at[14 + d], recv.at[14 + d], (replica, t))
+
+    order = (3, 1, 2)
+    for d in order:
+        small_hop(d, peer_of(shard, d), shard).start()
+    for i in range(4):
+        if i == 2:
+            for d in order:
+                cot_hop(d, peer_of(shard, d), shard).start()
+        for d in order:
             hop(i, d, peer_of(shard, d), shard).start()
-    own_block = remote(cot, cot_all.at[block(shard, core)], fsend.at[18], frecv.at[18], mate)
-    own_block.start()
+    cot_onward(0, shard, core).start()
     for n, (src, buf, _) in enumerate(loads):
         pltpu.make_async_copy(src, buf, local.at[n]).start()
     for n, (src, buf, dst) in enumerate(loads):
         pltpu.make_async_copy(src, buf, local.at[n]).wait()
         pltpu.make_async_copy(buf, dst, local.at[n]).start()
-    for i, (_, target, passed) in enumerate(items):
-        for d in (3, 1, 2):
+
+    def take(i):
+        for d in order:
             p = peer_of(shard, d)
             hop(i, d, p, p).wait_recv()
-            if passed:
-                onward(i, d, target(p)).start()
-    for i, (_, target, passed) in enumerate(items):
-        for d in (3, 1, 2):
+            across(i, d, p, odd).start()
+            if weights[i][4]:
+                onward(i, d, p, core, False).start()
+
+    def take_shared(i):
+        for d in order:
             p = peer_of(shard, d)
+            across(i, d, p, 1 - odd).wait_recv()
+            if weights[i][4]:
+                onward(i, d, p, core, True).start()
+
+    take(0)
+    take(1)
+    for d in order:
+        p = peer_of(shard, d)
+        cot_hop(d, p, p).wait_recv()
+        cot_onward(d, p, core).start()
+    take_shared(0)
+    take_shared(1)
+    take(2)
+    take(3)
+    take_shared(2)
+    take_shared(3)
+    for d in order:
+        p = peer_of(shard, d)
+        small_hop(d, p, p).wait_recv()
+        small_hop(d, p, shard).wait_send()
+        cot_hop(d, p, shard).wait_send()
+        cot_onward(d, p, core).wait_send()
+        cot_onward(d, p, other).wait_recv()
+        for i in range(4):
             hop(i, d, p, shard).wait_send()
-            if passed:
-                onward(i, d, target(p)).wait_send()
-    other = 1 - core
-    arrivals = {1: lambda o: q_full.at[half_rows(o, other)], 2: lambda o: o_full.at[half_rows(o, other)],
-                3: lambda o: cot_all.at[block(o, other)]}
-    for i, target in arrivals.items():
-        for d in (3, 1, 2):
-            onward(i, d, target(peer_of(shard, d))).wait_recv()
-    own_block.wait_send()
-    remote(cot, cot_all.at[block(shard, other)], fsend.at[18], frecv.at[18], mate).wait_recv()
+            across(i, d, p, odd).wait_send()
+            if weights[i][4]:
+                for part in (False, True):
+                    onward(i, d, p, core, part).wait_send()
+                    onward(i, d, p, other, part).wait_recv()
+    cot_onward(0, shard, core).wait_send()
+    cot_onward(0, shard, other).wait_recv()
     for n, (src, buf, dst) in enumerate(loads):
         pltpu.make_async_copy(buf, dst, local.at[n]).wait()
 
@@ -434,8 +488,10 @@
         + [
             pltpu.SemaphoreType.DMA((18,)),
             pltpu.SemaphoreType.DMA((18,)),
-            pltpu.SemaphoreType.DMA((19,)),
-            pltpu.SemaphoreType.DMA((19,)),
+            pltpu.SemaphoreType.DMA((16,)),
+            pltpu.SemaphoreType.DMA((16,)),
+            pltpu.SemaphoreType.DMA((12,)),
+            pltpu.SemaphoreType.DMA((12,)),
             pltpu.SemaphoreType.DMA((6,)),
         ],
         compiler_params=params(),
@@ -683,12 +739,13 @@
                     lambda c, k=k, dst=dst, source=source: dst.at[c, source, pl.ds(k * CHUNK, CHUNK)],
                 ))
     total = len(chunks)
-    awaited = set()
-
-    def arrive(what):
-        if what in awaited:
+    awaited = (set(), set())
+    end = (level == 0) | (level == levels - 1)
+
+    def arrive(what, seen):
+        if what in seen:
             return
-        awaited.add(what)
+        seen.add(what)
         if what[0] == "fill":
             fills[what[1]].wait()
         else:
@@ -724,32 +781,44 @@
     def root_of(k):
         return levels // 2 - 1 + k % 2
 
+    def end_gather(k):
+        own = chunks[k][0]
+
+        @pl.when(end)
+        def _():
+            arrive(chunks[k][4], awaited[0])
+
+        @pl.when(level == 0)
+        def _():
+            up(k, own).start()
+
+        @pl.when(level == levels - 1)
+        def _():
+            down(k, own).start()
+
     def gather_step(k):
         own, low, high, at, what, _ = chunks[k]
-        arrive(what)
         root = root_of(k)
 
-        @pl.when(level < root)
+        @pl.when(~end)
         def _():
-            if root > 1:
-
-                @pl.when(level > 0)
-                def _():
-                    up(k, own).wait_recv()
-                    add(k, low)
-
-            up(k, own).start()
-
-        @pl.when(level > root)
-        def _():
-            if root < levels - 2:
-
-                @pl.when(level < levels - 1)
-                def _():
-                    down(k, own).wait_recv()
-                    add(k, high)
-
-            down(k, own).start()
+            arrive(what, awaited[1])
+
+        if root > 1:
+
+            @pl.when((level > 0) & (level < root))
+            def _():
+                up(k, own).wait_recv()
+                add(k, low)
+                up(k, own).start()
+
+        if root < levels - 2:
+
+            @pl.when((level < levels - 1) & (level > root))
+            def _():
+                down(k, own).wait_recv()
+                add(k, high)
+                down(k, own).start()
 
     def root_step(k):
         own, low, high, at, _, _ = chunks[k]
@@ -767,35 +836,40 @@
         own, low, high, at, _, _ = chunks[k]
         root = root_of(k)
 
-        @pl.when(level < root)
+        if root > 1:
+
+            @pl.when((level > 0) & (level < root))
+            def _():
+                down(k, own).wait_recv()
+                down(k, high).start()
+                finish(k, high)
+
+        if root < levels - 2:
+
+            @pl.when((level < levels - 1) & (level > root))
+            def _():
+                up(k, own).wait_recv()
+                up(k, low).start()
+                finish(k, low)
+
+    def end_spread(k):
+        own, low, high, at, _, _ = chunks[k]
+
+        @pl.when(level == 0)
         def _():
             down(k, own).wait_recv()
-            if root > 1:
-
-                @pl.when(level > 0)
-                def _():
-                    down(k, high).start()
-
             finish(k, high)
 
-        @pl.when(level > root)
+        @pl.when(level == levels - 1)
         def _():
             up(k, own).wait_recv()
-            if root < levels - 2:
-
-                @pl.when(level < levels - 1)
-                def _():
-                    up(k, low).start()
-
             finish(k, low)
 
-    for t in range(total + 6):
-        if t < total:
-            gather_step(t)
-        if 0 <= t - 3 < total:
-            root_step(t - 3)
-        if 0 <= t - 6 < total:
-            spread_step(t - 6)
+    stages = ((end_gather, 0), (gather_step, 4), (root_step, 7), (spread_step, 10), (end_spread, 14))
+    for t in range(total + stages[-1][1]):
+        for stage, lag in stages:
+            if 0 <= t - lag < total:
+                stage(t - lag)
     for a in range(2):
         for d in (1, 2, 3):
             exchange(a, d, peer_of(shard, d)).wait_send()
@@ -997,7 +1071,7 @@
         P("shard", None),
         P(("replica", "shard"), None),
     )
-    fits = mesh.shape["shard"] == 4 and mesh.shape["replica"] % 2 == 0 and mesh.shape["replica"] >= 8
+    fits = mesh.shape["shard"] == 4 and mesh.shape["replica"] % 4 == 0
     per_device = fast_device if fits else general_device
     return jax.shard_map(
         per_device,

time: 960 us -> 782 us (0.81)
  Pallas kernels: 790 us -> 612 us
    pallas_call x1, Pallas kernels: 467 us -> 323 us  [reduce_gradients(): pl.pallas_call(functools.partial(reduce_kernel, levels), out_shape=[jax.S...]
    pallas_call x1, Pallas kernels: 164 us -> 130 us  [front(): pl.pallas_call(front_kernel, out_shape=[jax.ShapeDtypeStruct(s, bf16) for...]
where the time goes in v2:
time: 782 us; the launch traced here: 776 us
  Pallas kernels  612 us (78%)
  matrix products  83.2 us (11%)
  blocking collectives  39.8 us (5%)
  other arithmetic  27.3 us (3%)
  local copies, waits for them, and re-layouts  11.6 us (1%)
    pallas_call x1, Pallas kernels, reduce_gradients(): pl.pallas_call(functools.partial(reduce_kernel, levels), out_shape=[jax.S...  323 us
    pallas_call x1, Pallas kernels, front(): pl.pallas_call(front_kernel, out_shape=[jax.ShapeDtypeStruct(s, bf16) for...  130 us
    pallas_call x1, Pallas kernels, attn_gather(): pl.pallas_call(attn_gather_kernel, out_shape=[jax.ShapeDtypeStruct(s, bf1...  60.9 us
    pallas_call x1, Pallas kernels, plane_scatter(): pl.pallas_call(scatter_kernel, out_shape=[out, out], in_specs=[vmem_spec(...  48 us
    psum x1, blocking collectives, fast_device(): lax.psum(jnp.concatenate([gain_one_grad, bias_grad, gain_two_grad]), ('re...  39.8 us
    pallas_call x1, Pallas kernels, plane_gather(): pl.pallas_call(gather_kernel, out_shape=jax.ShapeDtypeStruct((x.shape[0]...  28.7 us
    pallas_call x2, Pallas kernels, widen(): pl.pallas_call(widen_kernel, grid=(384 // rows,), out_shape=jax.ShapeDtyp...  21.8 us

profile of v2, /device:TPU:0, one launch (start us, length us, event | category | flops | bytes accessed | tf_op | source)
XLA Modules:
  0.0 775.5 jit_solution(5635711007453006971)
XLA Ops:
  0.7 1.2 fusion.23
  1.9 0.6 fusion.35
  2.5 0.7 reshape.240
  3.1 0.7 reshape.242
  3.8 0.7 reshape.241
  4.8 0.6 iota_compare_fusion
  5.9 129.5 %shard_map.177 = (bf16[1536,2048]{1,0:T(8,128)(2,1)}, bf16[1536,1536]{1,0:T(8,128)(2,1)}, bf16[1536,1152]{1,0:T(8,128)(2,1)}, bf16[1536,1152]{1,0:T(8,128)(2,1)}...) custom-call(bf16[384,2048]{1,0:T(8,128)(2,1)} %wq.1, bf16[384,1536]{1,0:T(8,128)(2,1)} %wo.1, ...), custom_call_target="tpu_custom_call" | custom-call | tf_op jit(solution)/shard_map/pallas_call | solution.py:482
  135.4 0.8 slice_convert_fusion.1
  136.2 0.9 convert_reduce_fusion.1
  137.7 3.9 convolution_add_fusion.1
  144.1 1.0 copy.61.ctx
  145.1 3.2 multiply_reduce_fusion.2
  148.8 0.9 multiply_convert_fusion.x
  149.7 28.7 %shard_map.178 = bf16[1024,1536]{1,0:T(8,128)(2,1)} custom-call(bf16[128,1536]{1,0:T(8,128)(2,1)} %multiply_convert_fusion.x), custom_call_target="tpu_custom_call" | custom-call | tf_op jit(solution)/shard_map/pallas_call | solution.py:528
  178.5 7.3 fusion.52
  185.8 5.8 fusion.51
  191.7 9.4 %select_convert_fusion = (bf16[1024,1152]{1,0:T(8,128)(2,1)}, bf16[1024,1152]{1,0:T(8,128)(2,1)}, bf16[1024,1152]{1,0:T(8,128)(2,1)S(1)}) fusion(pred[1152]{0:T(1024)(128)(4,1)S(1)} %copy-done.40, f32[1024,1152]{1,0:T(8,128)} %fusion.51, f32[1024,1152]{1,0:T(8,128)S(1)} %fusion.52, bf16[1024,1536]{1,0:T(8,128)(2,1)S(1)} %copy-done.43, s32[]{:T(128)S(6)} %select_n.40, ...), kind=kOutput, calls=%fused_computation.10 | convolution fusion | flops 3645112320 | bytes 26543236 | tf_op jit(solution)/shard_map/td,fd->tf/dot_general | solution.py:988
  201.1 5.4 fusion.1.pd
  206.5 5.8 convolution_convert_fusion.pa
  212.3 4.3 fusion.53
  216.6 5.7 add_convert_fusion.pb
  222.3 48.0 %shard_map.179 = (f32[128,1536]{1,0:T(8,128)}, f32[128,1536]{1,0:T(8,128)}) custom-call(bf16[1024,1536]{1,0:T(8,128)(2,1)} %convolution_convert_fusion.pa, bf16[1024,1536]{1,0:T(8,128)(2,1)} %add_convert_fusion.pb), custom_call_target="tpu_custom_call" | custom-call | tf_op jit(solution)/shard_map/pallas_call | solution.py:583
  270.3 2.0 multiply_reduce_fusion
  272.8 1.4 fusion.47.hid
  274.2 0.8 copy-done.6
  275.0 4.1 convolution_convert_fusion.1
  279.7 1.1 convolution_bitcast_fusion
  280.9 1.9 convolution_bitcast_fusion.1
  282.8 1.8 fusion.15
  285.4 5.4 fusion.26
  290.8 39.8 %psum.7 = f32[5120]{0:T(1024)S(1)} all-reduce(f32[5120]{0:T(1024)S(1)} %pad_maximum_fusion.5), channel_id=1, replica_groups=mesh['replica'=8,'shard'=4] {'replica','shard'}, use_global_device_ids=true, to_apply=%region_10.11 | all-reduce | flops 5120 | bytes 40960 | tf_op jit(solution)/shard_map/psum | solution.py:1031
  330.7 2.7 fusion.22
  333.3 0.7 dynamic_slice.32
  334.0 0.7 fusion.49
  334.7 7.6 fusion.3.pu
  342.2 5.7 fusion.2.pg
  348.0 60.9 %shard_map.180 = (bf16[1024,384]{1,0:T(8,128)(2,1)}, bf16[1024,384]{1,0:T(8,128)(2,1)}, bf16[1024,768]{1,0:T(8,128)(2,1)}, bf16[1024,1024]{1,0:T(8,128)(2,1)}) custom-call(bf16[128,1536]{1,0:T(8,128)(2,1)} %copy.61.ctx, bf16[128,1536]{1,0:T(8,128)(2,1)} %copy-done.2, bf16[128,1536]{1,0:T(8,128)(2,1)} %copy-done.6, bf16[128,2048]{1,0:T(8,128)(2,1)} %copy-done.3), custom_call_target="tpu_custom_call" | custom-call | tf_op jit(solution)/shard_map/pallas_call | solution.py:675
  408.9 3.0 fusion.54
  411.9 0.8 fusion.55
  412.7 1.2 fusion.5.pa
  413.9 322.7 %shard_map.181 = (bf16[2,384,1792]{2,1,0:T(8,128)(2,1)}, bf16[2,1152,1536]{2,1,0:T(8,128)(2,1)}, bf16[2,4,384,1152]{3,2,1,0:T(8,128)(2,1)}, bf16[2,4,384,1152]{3,2,1,0:T(8,128)(2,1)}) custom-call(bf16[384,1792]{1,0:T(8,128)(2,1)} %fusion.5.pa, bf16[1152,1536]{1,0:T(8,128)(2,1)} %fusion.1.pd, bf16[1536,1152]{1,0:T(8,128)(2,1)} %fusion.2.pg, ...), custom_call_target="tpu_custom_call" | custom-call | tf_op jit(solution)/shard_map/pallas_call | solution.py:898
  736.6 1.3 slice_bitcast_fusion.3
  737.9 1.5 slice_bitcast_fusion.1
  739.4 1.7 maximum_convert_fusion.1
  741.1 2.0 maximum_convert_fusion
  743.2 10.9 %shard_map.182 = f32[384,8960]{1,0:T(8,128)} custom-call(bf16[2,4,384,1152]{3,2,1,0:T(8,128)(2,1)} %get-tuple-element.120.x), custom_call_target="tpu_custom_call" | custom-call | tf_op jit(solution)/shard_map/pallas_call | solution.py:926
  754.1 10.1 %dynamic-slice_convert_fusion = f32[2240,1536]{1,0:T(8,128)} fusion(bf16[2304,1536]{1,0:T(8,128)(2,1)} %bitcast.89, s32[]{:T(128)S(6)} %select_n.46), kind=kLoop, calls=%fused_computation.8 | loop fusion | flops 3440640 | bytes 20643844 | tf_op jit(solution)/shard_map/convert_element_type | solution.py:1046
  764.1 10.9 %shard_map.183 = f32[384,8960]{1,0:T(8,128)} custom-call(bf16[2,4,384,1152]{3,2,1,0:T(8,128)(2,1)} %get-tuple-element.121.x), custom_call_target="tpu_custom_call" | custom-call | tf_op jit(solution)/shard_map/pallas_call | solution.py:926
  (140 shorter events, 6.0 us)
Async XLA Ops:
  1.8 135.2 %copy-start.36 = (f32[128]{0:T(128)}, f32[128]{0:T(128)S(1)}, u32[]{:S(2)}) copy-start(f32[128]{0:T(128)S(1)} %add_rsqrt_fusion.1) | copy-start | bytes 1540
  4.8 1.1 copy-start.32
  5.7 136.8 %copy-start.14 = (f32[128,64]{1,0:T(8,128)}, f32[128,64]{1,0:T(8,128)S(1)}, u32[]{:S(2)}) copy-start(f32[128,64]{1,0:T(8,128)S(1)} %get-tuple-element.153) | copy-start | bytes 98308
  5.7 136.3 %copy-start.23 = (f32[128,64]{0,1:T(8,128)}, f32[128,64]{0,1:T(8,128)S(1)}, u32[]{:S(2)}) copy-start(f32[128,64]{0,1:T(8,128)S(1)} %copy.43) | copy-start | bytes 98308
  5.9 136.2 %copy-start.25 = (f32[128,64]{0,1:T(8,128)}, f32[128,64]{0,1:T(8,128)S(1)}, u32[]{:S(2)}) copy-start(f32[128,64]{0,1:T(8,128)S(1)} %copy.44) | copy-start | bytes 98308
  5.9 131.2 %copy-start = (bf16[128,1536]{1,0:T(8,128)(2,1)S(1)}, bf16[128,1536]{1,0:T(8,128)(2,1)}, u32[]{:S(2)}) copy-start(bf16[128,1536]{1,0:T(8,128)(2,1)} %param.16) | copy-start | bytes 1179652
  137.1 11.3 %copy-start.27 = (f32[1536]{0:T(1024)}, f32[1536]{0:T(1024)S(1)}, u32[]{:S(2)}) copy-start(f32[1536]{0:T(1024)S(1)} %reshape.253) | copy-start | bytes 18436
  137.1 0.6 copy-start.29
  137.7 3.9 copy-start.2
  141.7 2.1 copy-start.17
  141.7 1.4 copy-start.31
  142.5 5.8 copy-start.19
  142.5 5.8 copy-start.21
  142.8 0.8 copy-start.10
  143.0 5.3 copy-start.12
  148.3 0.5 copy-start.34
  178.4 7.4 copy-start.7
  178.4 7.4 copy-start.42
  178.4 13.2 %slice-start = ((s8[6881280]{0:T(1024)(128)(4,1)}), s8[4194304]{0:T(1024)(128)(4,1)S(1)}, s32[]{:S(2)}) async-start(s8[6881280]{0:T(1024)(128)(4,1)} %bitcast.105), calls=%async_computation | async-start | bytes 8388608
  185.8 5.9 copy-start.40
  185.8 5.8 slice-start.1
  185.8 5.8 copy-start.43
  206.5 5.8 copy-start.44
  212.3 4.3 copy-start.41
  212.3 4.3 copy-start.46
  222.3 50.5 %copy-start.4 = (bf16[128,1536]{1,0:T(8,128)(2,1)S(1)}, bf16[128,1536]{1,0:T(8,128)(2,1)}, u32[]{:S(2)}) copy-start(bf16[128,1536]{1,0:T(8,128)(2,1)} %cot.1) | copy-start | bytes 1179652
  274.2 0.8 copy-start.6
  275.0 4.7 copy-start.18
  275.0 5.9 copy-start.11
  275.0 5.9 copy-start.13
  279.0 3.7 copy-start.20
  279.1 3.7 copy-start.22
  279.1 5.5 copy-start.15
  279.1 5.8 copy-start.24
  279.1 5.8 copy-start.26
  280.9 4.5 copy-start.30
  285.3 5.5 copy-start.3
  285.3 5.5 copy-start.33
  285.3 45.3 %copy-start.1 = (f32[128,1536]{1,0:T(8,128)S(1)}, f32[128,1536]{1,0:T(8,128)}, u32[]{:S(2)}) copy-start(f32[128,1536]{1,0:T(8,128)} %get-tuple-element.114) | copy-start | bytes 2359300
  285.4 45.3 %copy-start.5 = (bf16[128,1536]{1,0:T(8,128)(2,1)S(1)}, bf16[128,1536]{1,0:T(8,128)(2,1)}, u32[]{:S(2)}) copy-start(bf16[128,1536]{1,0:T(8,128)(2,1)} %cot.1) | copy-start | bytes 1179652
  285.4 45.3 %copy-start.28 = (f32[1536]{0:T(1024)S(1)}, f32[1536]{0:T(1024)}, u32[]{:S(2)}) copy-start(f32[1536]{0:T(1024)} %copy-done.27) | copy-start | bytes 18436
  285.4 45.3 %copy-start.35 = (f32[128]{0:T(128)S(1)}, f32[128]{0:T(128)}, u32[]{:S(2)}) copy-start(f32[128]{0:T(128)} %copy-done.34) | copy-start | bytes 1540
  285.4 45.3 %copy-start.37 = (f32[128]{0:T(128)S(1)}, f32[128]{0:T(128)}, u32[]{:S(2)}) copy-start(f32[128]{0:T(128)} %copy-done.36) | copy-start | bytes 1540
  285.4 45.3 %copy-start.39 = (f32[128]{0:T(128)S(1)}, f32[128]{0:T(128)}, u32[]{:S(2)}) copy-start(f32[128]{0:T(128)} %copy-done.38) | copy-start | bytes 1540
  330.6 4.0 copy-start.8
  334.7 7.6 copy-start.45
  408.8 3.0 copy-start.9
  408.8 3.0 copy-start.16
  (1 other events, 0.5 us)

commit v3 on v2

--- a/solution.py
+++ b/solution.py
@@ -535,215 +535,327 @@
     )(x)
 
 
-def scatter_kernel(pa, pb, oa, ob, held, sums, parts, csend, crecv, send, recv):
+CHUNK = 128
+SCORE_SCALE = 1.0 / math.sqrt(HD)
+
+
+def dot_nt(a, b):
+    return lax.dot_general(a, b, (((1,), (1,)), ((), ())), preferred_element_type=jnp.float32)
+
+
+def dot_tn(a, b):
+    return lax.dot_general(a, b, (((0,), (0,)), ((), ())), preferred_element_type=jnp.float32)
+
+
+def row_loop(rows, step, body, init):
+    return lax.fori_loop(0, rows // step, lambda j, c: body(pl.ds(pl.multiple_of(j * step, step), step), c), init)
+
+
+def backward_kernel(levels, grad_scale, names, *refs):
+    v = dict(zip(names, refs))
     replica, shard, core = place()
+    other = 1 - core
+    level = replica // 2
     mate = (replica + 1 - 2 * core, shard)
+    above, below = (replica + 2, shard), (replica - 2, shard)
     f32 = jnp.float32
-    inputs = (pa, pb)
-    outputs = (oa, ob)
-
-    def block(c, target):
-        return pl.ds(pl.multiple_of((c * 4 + target) * 128, 128), 128)
-
-    order = (3, 1, 2, 0)
+    bf16 = jnp.bfloat16
+    order = (3, 1, 2)
+    own_a, own_d, own_g = v["own_a"], v["own_d"], v["own_g"]
+    sources = (v["pg"], v["pu"])
+
+    def tokens(owner, c):
+        return pl.ds(pl.multiple_of((c * 4 + owner) * 128, 128), 128)
+
+    def exchange(a, d, p):
+        rows = pl.ds(pl.multiple_of(p * 384, 384), 384)
+        n = a * 4 + d
+        return remote(
+            sources[a].at[rows], own_g.at[pl.ds(a * 1536 + d * 384, 384)],
+            v["xsend"].at[n], v["xrecv"].at[n], (replica, p),
+        )
+
+    fills = [
+        None,
+        pltpu.make_async_copy(v["pd"], own_d, v["in_sem"].at[1]),
+    ]
     for a in range(2):
-        for d in order:
-            t = peer_of(shard, d)
-            remote(inputs[a].at[block(1 - core, t)], held.at[a, d], csend.at[a * 4 + d], crecv.at[a * 4 + d], mate).start()
-
-    def summed(a, d):
+        rows = pl.ds(pl.multiple_of(shard * 384, 384), 384)
+        fills.append(
+            pltpu.make_async_copy(sources[a].at[rows], own_g.at[pl.ds(a * 1536, 384)], v["in_sem"].at[2 + a])
+        )
+
+    partial = (v["p_back"], v["p_out"])
+    held, kept, parts = v["held"], v["kept"], v["parts"]
+
+    def to_mate(a, d):
         t = peer_of(shard, d)
         n = a * 4 + d
-        remote(inputs[a].at[block(core, t)], held.at[a, d], csend.at[n], crecv.at[n], mate).wait_recv()
-        return inputs[a][block(core, t), :].astype(f32) + held[a, d].astype(f32)
-
-    for a in range(2):
-        for d in (3, 1, 2):
-            sums[a, d - 1] = summed(a, d).astype(sums.dtype)
-            n = a * 3 + d - 1
-            remote(sums.at[a, d - 1], parts.at[a, d - 1], send.at[n], recv.at[n], (replica, peer_of(shard, d))).start()
-    for a in range(2):
-        outputs[a][...] = summed(a, 0)
-    for a in range(2):
+        return remote(partial[a].at[tokens(t, other)], held.at[a, d],
+                      v["csend"].at[n], v["crecv"].at[n], mate)
+
+    def keep(a, d):
+        return pltpu.make_async_copy(partial[a].at[tokens(peer_of(shard, d), core)], kept.at[a, d], v["keep_sem"].at[a * 4 + d])
+
+    def to_owner(a, d):
+        n = a * 3 + d - 1
+        return remote(kept.at[a, d], parts.at[a, d - 1], v["psend"].at[n], v["precv"].at[n], (replica, peer_of(shard, d)))
+
+    def pair_sums(a):
+        for d in order:
+            to_mate(a, d).wait_recv()
+            keep(a, d).wait()
+
+            def body(rows, carry):
+                kept[a, d, rows, :] = (kept[a, d, rows, :].astype(f32) + held[a, d, rows, :].astype(f32)).astype(bf16)
+                return carry
+
+            row_loop(128, 32, body, 0)
+            to_owner(a, d).start()
+
+    def collect(a):
+        to_mate(a, 0).wait_recv()
+        keep(a, 0).wait()
+        for d in order:
+            to_owner(a, d).wait_recv()
+
+    def full_sum(a, rows):
+        total = kept[a, 0, rows, :].astype(f32) + held[a, 0, rows, :].astype(f32)
         for d in (1, 2, 3):
-            n = a * 3 + d - 1
-            remote(sums.at[a, d - 1], parts.at[a, d - 1], send.at[n], recv.at[n], (replica, peer_of(shard, d))).wait()
-            outputs[a][...] += parts[a, d - 1].astype(f32)
-    for a in range(2):
-        for d in order:
-            t = peer_of(shard, d)
-            n = a * 4 + d
-            remote(inputs[a].at[block(1 - core, t)], held.at[a, d], csend.at[n], crecv.at[n], mate).wait_send()
-
-
-def plane_scatter(pa, pb):
-    width = pa.shape[1]
-    bf16 = jnp.bfloat16
-    out = jax.ShapeDtypeStruct((128, width), jnp.float32)
-    return pl.pallas_call(
-        scatter_kernel,
-        out_shape=[out, out],
-        in_specs=[vmem_spec()] * 2,
-        out_specs=[vmem_spec()] * 2,
-        scratch_shapes=[
-            pltpu.VMEM((2, 4, 128, width), bf16),
-            pltpu.VMEM((2, 3, 128, width), bf16),
-            pltpu.VMEM((2, 3, 128, width), bf16),
-            pltpu.SemaphoreType.DMA((8,)),
-            pltpu.SemaphoreType.DMA((8,)),
-            pltpu.SemaphoreType.DMA((6,)),
-            pltpu.SemaphoreType.DMA((6,)),
-        ],
-        compiler_params=params(),
-    )(pa, pb)
-
-
-def attn_gather_kernel(ctx, nrm, hid, prj, ctx_all, nrm_all, hid_all, prj_all, send, recv, fsend, frecv, local):
-    replica, shard, core = place()
-    other = 1 - core
-    mate = (replica + 1 - 2 * core, shard)
+            total = total + parts[a, d - 1, rows, :].astype(f32)
+        return total
+
+    wide = ((v["hid"], v["hid_all"], 768), (v["prj"], v["prj_all"], 1024))
+    narrow = ((v["ctx"], v["ctx_all"], 384), (v["nrm"], v["nrm_all"], 384))
 
     def block(out, owner, c):
-        return out.at[pl.ds(pl.multiple_of((c * 4 + owner) * 128, 128), 128)]
-
-    def part(ref, index, width):
+        return out.at[tokens(owner, c)]
+
+    def columns(ref, index, width):
         return ref.at[:, pl.ds(pl.multiple_of(index * width, width), width)]
 
-    def device(c, t):
-        return (replica - core + c, t)
-
-    wide = ((hid, hid_all, 768), (prj, prj_all, 1024))
-    narrow = ((ctx, ctx_all, 384), (nrm, nrm_all, 384))
     def wide_copy(a, d, same, source_core, owner, t):
         ref, out, width = wide[a]
         c = core if same else other
         n = (a * 4 + d) * 2 + (0 if same else 1)
-        return remote(part(ref, c, width), block(out, owner, source_core), send.at[n], recv.at[n], device(c, t))
+        return remote(
+            columns(ref, c, width), block(out, owner, source_core), v["gsend"].at[n], v["grecv"].at[n],
+            (replica - core + c, t),
+        )
 
     def narrow_copy(a, d, owner, t):
         ref, out, width = narrow[a]
         n = 16 + a * 4 + d
-        return remote(part(ref, t, width), block(out, owner, core), send.at[n], recv.at[n], (replica, t))
+        return remote(columns(ref, t, width), block(out, owner, core), v["gsend"].at[n], v["grecv"].at[n], (replica, t))
 
     def onward(a, d, source, owner, c):
-        _, out, _ = narrow[a]
+        out = narrow[a][1]
         n = a * 4 + d
-        return remote(source, block(out, owner, c), fsend.at[n], frecv.at[n], mate)
-
-    for d in (3, 1, 2, 0):
-        t = peer_of(shard, d)
+        return remote(source, block(out, owner, c), v["fsend"].at[n], v["frecv"].at[n], mate)
+
+    def own_narrow(a):
+        ref, out, width = narrow[a]
+        return pltpu.make_async_copy(columns(ref, shard, width), block(out, shard, core), v["local"].at[a])
+
+    def own_wide(a):
+        ref, out, width = wide[a]
+        return pltpu.make_async_copy(columns(ref, core, width), block(out, shard, core), v["local"].at[2 + a])
+
+    wbuf = v["wbuf"]
+    load_out = pltpu.make_async_copy(v["wo"], wbuf.at[:, pl.ds(0, 1536)], v["local"].at[4])
+    load_qkv = pltpu.make_async_copy(v["wq"], wbuf, v["local"].at[5])
+
+    def stage_sums():
+        pair_sums(0)
+        for d in order:
+            for a in range(2):
+                narrow_copy(a, d, shard, peer_of(shard, d)).start()
+        for d in (1, 2, 3):
+            for a in range(2):
+                exchange(a, d, peer_of(shard, d)).start()
+
+    def stage_hidden():
+        collect(0)
+        gain = v["gain_two"][...]
+
+        def body(rows, total):
+            grad = full_sum(0, rows)
+            hidden = v["hidden"][rows, :]
+            inv = lax.rsqrt(jnp.mean(hidden * hidden, axis=-1, keepdims=True) + NORM_EPS)
+            scaled = gain * grad
+            out = v["cot"][rows, :].astype(f32) + inv * (
+                scaled - hidden * inv * inv * jnp.mean(scaled * hidden, axis=-1, keepdims=True)
+            )
+            v["hgrad"][rows, :] = out
+            v["hid"][rows, :] = out.astype(bf16)
+            return total + jnp.sum(grad * hidden * inv, axis=0, keepdims=True)
+
+        v["row_two"][...] = row_loop(128, 16, body, jnp.zeros((1, 1536), f32)) * grad_scale
+        for d in (0,) + order:
+            if d:
+                wide_copy(0, d, True, core, shard, peer_of(shard, d)).start()
+            wide_copy(0, d, False, core, shard, peer_of(shard, d)).start()
+        own_wide(0).start()
+
+    def stage_context():
+        load_out.wait()
+        for e in range(4):
+            cols = pl.ds(e * 384, 384)
+            v["cgrad"][:, cols] = dot_nt(v["hid"][...], wbuf[cols, 0:1536]).astype(bf16)
+        load_qkv.start()
+
+    def unrotated(x):
+        return x * v["cos"][...] + pltpu.roll(x, HD // 2, 1) * v["sin"][...]
+
+    def stage_heads(g):
+        keys = v["key"][:, g * HD : (g + 1) * HD]
+        values = v["val"][:, g * HD : (g + 1) * HD]
+        causal = lax.broadcasted_iota(jnp.int32, (128, 128), 0) >= lax.broadcasted_iota(jnp.int32, (128, 128), 1)
+        key_grad = jnp.zeros((128, HD), f32)
+        value_grad = jnp.zeros((128, HD), f32)
+        for h in range(g * (HEADS // KV), (g + 1) * (HEADS // KV)):
+            at = slice(h * HD, (h + 1) * HD)
+            query = v["qry"][:, at]
+            grad = v["cgrad"][:, at]
+            scores = jnp.where(causal, dot_nt(query, keys) * SCORE_SCALE, -1e30)
+            probs = jnp.exp(scores - v["lse"][:, h : h + 1]).astype(bf16)
+            wide_probs = probs.astype(f32)
+            prob_grad = dot_nt(grad, values)
+            delta = jnp.sum(wide_probs * prob_grad, axis=-1, keepdims=True)
+            score_grad = (wide_probs * (prob_grad - delta) * SCORE_SCALE).astype(bf16)
+            v["prj"][:, at] = unrotated(jnp.dot(score_grad, keys, preferred_element_type=f32)).astype(bf16)
+            key_grad = key_grad + dot_tn(score_grad, query)
+            value_grad = value_grad + dot_tn(probs, grad)
+        first = HEADS * HD + g * HD
+        v["prj"][:, first : first + HD] = unrotated(key_grad).astype(bf16)
+        first = first + KV * HD
+        v["prj"][:, first : first + HD] = value_grad.astype(bf16)
+
+    def stage_send_projected():
+        for d in (0,) + order:
+            if d:
+                wide_copy(1, d, True, core, shard, peer_of(shard, d)).start()
+            wide_copy(1, d, False, core, shard, peer_of(shard, d)).start()
+        own_wide(1).start()
+
+    def stage_normed():
+        load_qkv.wait()
+        for e in range(4):
+            cols = pl.ds(e * 384, 384)
+            v["ngrad"][:, cols] = dot_nt(v["prj"][...], wbuf[cols, :])
+
+    vec, vin, vall = v["vec"], v["vin"], v["vall"]
+    replicas = 2 * levels
+
+    def vec_hop(d):
+        return remote(vec.at[peer_of(shard, d)], vin.at[d - 1], v["vsend"].at[d - 1], v["vrecv"].at[d - 1],
+                      (replica, peer_of(shard, d)))
+
+    def vec_spread(j, slot):
+        target = lax.rem(replica + j, replicas)
+        return remote(v["vsum"], vall.at[slot], v["vsend"].at[2 + j], v["vrecv"].at[2 + j], (target, shard))
+
+    def stage_input():
+        gain = v["gain_one"][...]
+
+        def body(rows, totals):
+            total, bias = totals
+            x = v["x"][rows, :].astype(f32)
+            grad = v["ngrad"][rows, :]
+            inv = lax.rsqrt(jnp.mean(x * x, axis=-1, keepdims=True) + NORM_EPS)
+            scaled = gain * grad
+            v["input_grad"][rows, :] = v["hgrad"][rows, :] + inv * (
+                scaled - x * inv * inv * jnp.mean(scaled * x, axis=-1, keepdims=True)
+            )
+            return (
+                total + jnp.sum(grad * x * inv, axis=0, keepdims=True),
+                bias + jnp.sum(v["prj"][rows, :].astype(f32), axis=0, keepdims=True),
+            )
+
+        row_one, row_bias = row_loop(128, 16, body, (jnp.zeros((1, 1536), f32), jnp.zeros((1, 2048), f32)))
+        row_one = row_one * grad_scale
+        row_bias = row_bias * grad_scale
+        row_two = v["row_two"][...]
+        for s in range(4):
+            vec[s, :, 0:384] = jnp.broadcast_to(row_one[:, s * 384 : (s + 1) * 384], (8, 384))
+            vec[s, :, 384:896] = jnp.broadcast_to(row_bias[:, s * 512 : (s + 1) * 512], (8, 512))
+            vec[s, :, 896:1280] = jnp.broadcast_to(row_two[:, s * 384 : (s + 1) * 384], (8, 384))
+        for d in order:
+            vec_hop(d).start()
+
+    def stage_vec():
+        total = vec[shard]
+        for d in (1, 2, 3):
+            vec_hop(d).wait_recv()
+            total = total + vin[d - 1]
+        v["vsum"][...] = total
+        for j in range(1, replicas):
+            vec_spread(j, replica).start()
+        pair_sums(1)
+
+    def stage_vec_out():
+        vall[replica] = v["vsum"][...]
+        for j in range(1, replicas):
+            vec_spread(j, lax.rem(replica + replicas - j, replicas)).wait_recv()
+        total = vall[0]
+        for j in range(1, replicas):
+            total = total + vall[j]
+        v["vec_out"][...] = total
+
+    def stage_output():
+        collect(1)
+
+        def body(rows, carry):
+            v["block_out"][rows, :] = (v["hidden"][rows, :] + full_sum(1, rows)).astype(bf16)
+            return carry
+
+        row_loop(128, 32, body, 0)
+
+    def stage_relay():
+        for d in order:
+            p = peer_of(shard, d)
+            for a in range(2):
+                narrow_copy(a, d, p, p).wait_recv()
+                onward(a, d, block(narrow[a][1], p, core), p, core).start()
+
+    def stage_attention_parts():
         for a in range(2):
-            if d:
-                wide_copy(a, d, True, core, shard, t).start()
-            wide_copy(a, d, False, core, shard, t).start()
-            if d:
-                narrow_copy(a, d, shard, t).start()
-            else:
-                ref, out, width = narrow[a]
-                onward(a, 0, part(ref, shard, width), shard, core).start()
-    locals_ = []
-    for a in range(2):
-        ref, out, width = narrow[a]
-        locals_.append(pltpu.make_async_copy(part(ref, shard, width), block(out, shard, core), local.at[a]))
-        ref, out, width = wide[a]
-        locals_.append(pltpu.make_async_copy(part(ref, core, width), block(out, shard, core), local.at[2 + a]))
-    for copy in locals_:
-        copy.start()
-    for d in (1, 2, 3):
-        p = peer_of(shard, d)
-        for a in range(2):
-            narrow_copy(a, d, p, p).wait_recv()
-            onward(a, d, block(narrow[a][1], p, core), p, core).start()
-    for copy in locals_:
-        copy.wait()
-    for d in (0, 1, 2, 3):
-        p = peer_of(shard, d)
-        for a in range(2):
-            if d:
-                wide_copy(a, d, True, core, p, p).wait_recv()
-                wide_copy(a, d, True, core, shard, p).wait_send()
-                narrow_copy(a, d, shard, p).wait_send()
-            wide_copy(a, d, False, other, p, p).wait_recv()
-            wide_copy(a, d, False, core, shard, p).wait_send()
-            onward(a, d, block(narrow[a][1], p, core), p, core).wait_send()
-            onward(a, d, block(narrow[a][1], p, other), p, other).wait_recv()
-
-
-def attn_gather(ctx, nrm, hid, prj):
-    bf16 = jnp.bfloat16
-    shapes = [(1024, 384), (1024, 384), (1024, 768), (1024, 1024)]
-    return pl.pallas_call(
-        attn_gather_kernel,
-        out_shape=[jax.ShapeDtypeStruct(s, bf16) for s in shapes],
-        in_specs=[vmem_spec()] * 4,
-        out_specs=[vmem_spec()] * 4,
-        scratch_shapes=[
-            pltpu.SemaphoreType.DMA((24,)),
-            pltpu.SemaphoreType.DMA((24,)),
-            pltpu.SemaphoreType.DMA((8,)),
-            pltpu.SemaphoreType.DMA((8,)),
-            pltpu.SemaphoreType.DMA((4,)),
-        ],
-        compiler_params=params(),
-    )(ctx, nrm, hid, prj)
-
-
-CHUNK = 128
-
-
-def reduce_kernel(
-    levels, pa, pd, pg, pu, fa, fd, fg, fu,
-    own_a, own_d, own_g, low_a, low_d, low_g, high_a, high_d, high_g,
-    xsend, xrecv, up_sem, down_sem, low_sem, high_sem, mate_send, mate_recv, out_sem, in_sem,
-):
-    replica, shard, core = place()
-    level = replica // 2
-    mate = (replica + 1 - 2 * core, shard)
-    above, below = (replica + 2, shard), (replica - 2, shard)
-    f32 = jnp.float32
-    sources = (pg, pu)
-
-    def exchange(a, d, p):
-        rows = pl.ds(pl.multiple_of(p * 384, 384), 384)
-        n = a * 4 + d
-        return remote(sources[a].at[rows], own_g.at[pl.ds(a * 1536 + d * 384, 384)], xsend.at[n], xrecv.at[n], (replica, p))
-
-    fills = [
-        pltpu.make_async_copy(pa, own_a, in_sem.at[0]),
-        pltpu.make_async_copy(pd, own_d, in_sem.at[1]),
-    ]
-    for a in range(2):
-        rows = pl.ds(pl.multiple_of(shard * 384, 384), 384)
-        fills.append(pltpu.make_async_copy(sources[a].at[rows], own_g.at[pl.ds(a * 1536, 384)], in_sem.at[2 + a]))
-    for copy in fills:
-        copy.start()
-    for a in range(2):
-        for d in (1, 2, 3):
-            exchange(a, d, peer_of(shard, d)).start()
+            own_narrow(a).wait()
+            own_wide(a).wait()
+            for d in (0, 1, 2, 3):
+                p = peer_of(shard, d)
+                if d:
+                    wide_copy(a, d, True, core, p, p).wait_recv()
+                wide_copy(a, d, False, other, p, p).wait_recv()
+                onward(a, d, block(narrow[a][1], p, other), p, other).wait_recv()
+        for j in range(3):
+            at = pl.ds(j * 128, 128)
+            own_a[at, 0:1024] = (dot_tn(v["nrm_all"][:, at], v["prj_all"][...]) * grad_scale).astype(bf16)
+            own_a[at, 1024:1792] = (dot_tn(v["ctx_all"][:, at], v["hid_all"][...]) * grad_scale).astype(bf16)
 
     chunks = []
-    for k in range(3):
-        at = pl.ds(k * CHUNK, CHUNK)
-        chunks.append((own_a, low_a, high_a, at, ("fill", 0), lambda c, at=at: fa.at[c, at]))
     for k in range(9):
         at = pl.ds(k * CHUNK, CHUNK)
-        chunks.append((own_d, low_d, high_d, at, ("fill", 1), lambda c, at=at: fd.at[c, at]))
+        chunks.append((own_d, v["low_d"], v["high_d"], at, ("fill", 1), lambda c, at=at: v["fd"].at[c, at]))
     for d in range(4):
         for a in range(2):
             for k in range(3):
                 at = pl.ds(a * 1536 + d * 384 + k * CHUNK, CHUNK)
-                dst = (fg, fu)[a]
+                dst = (v["fg"], v["fu"])[a]
                 source = peer_of(shard, d)
                 chunks.append((
-                    own_g, low_g, high_g, at, ("fill", 2 + a) if d == 0 else ("x", a, d),
+                    own_g, v["low_g"], v["high_g"], at, ("fill", 2 + a) if d == 0 else ("x", a, d),
                     lambda c, k=k, dst=dst, source=source: dst.at[c, source, pl.ds(k * CHUNK, CHUNK)],
                 ))
+    for k in range(3):
+        at = pl.ds(k * CHUNK, CHUNK)
+        chunks.append((own_a, v["low_a"], v["high_a"], at, ("none",), lambda c, at=at: v["fa"].at[c, at]))
     total = len(chunks)
     awaited = (set(), set())
     end = (level == 0) | (level == levels - 1)
 
     def arrive(what, seen):
-        if what in seen:
+        if what in seen or what[0] == "none":
             return
         seen.add(what)
         if what[0] == "fill":
@@ -753,11 +865,11 @@
 
     def up(k, ref):
         own, low, high, at, _, _ = chunks[k]
-        return remote(ref.at[at], low.at[at], up_sem.at[k], low_sem.at[k], above)
+        return remote(ref.at[at], low.at[at], v["up_sem"].at[k], v["low_sem"].at[k], above)
 
     def down(k, ref):
         own, low, high, at, _, _ = chunks[k]
-        return remote(ref.at[at], high.at[at], down_sem.at[k], high_sem.at[k], below)
+        return remote(ref.at[at], high.at[at], v["down_sem"].at[k], v["high_sem"].at[k], below)
 
     def add(k, *refs):
         own, _, _, at, _, _ = chunks[k]
@@ -775,8 +887,8 @@
 
     def finish(k, ref):
         _, _, _, at, _, dst = chunks[k]
-        pltpu.make_async_copy(ref.at[at], dst(core), out_sem.at[k]).start()
-        remote(ref.at[at], dst(core), mate_send.at[k], mate_recv.at[k], mate).start()
+        pltpu.make_async_copy(ref.at[at], dst(core), v["out_sem"].at[k]).start()
+        remote(ref.at[at], dst(core), v["mate_send"].at[k], v["mate_recv"].at[k], mate).start()
 
     def root_of(k):
         return levels // 2 - 1 + k % 2
@@ -865,11 +977,37 @@
             up(k, own).wait_recv()
             finish(k, low)
 
+    for a in range(2):
+        for d in order + (0,):
+            to_mate(a, d).start()
+            keep(a, d).start()
+    for copy in fills[1:]:
+        copy.start()
+    load_out.start()
+    for a in range(2):
+        own_narrow(a).start()
+        onward(a, 0, columns(narrow[a][0], shard, 384), shard, core).start()
+    beside = {
+        0: [stage_sums],
+        3: [stage_hidden],
+        4: [stage_context],
+        5: [functools.partial(stage_heads, 0)],
+        6: [functools.partial(stage_heads, 1), stage_send_projected],
+        7: [stage_normed],
+        8: [stage_input],
+        10: [stage_vec],
+        12: [stage_relay],
+        14: [stage_vec_out],
+        24: [stage_output],
+        27: [stage_attention_parts],
+    }
     stages = ((end_gather, 0), (gather_step, 4), (root_step, 7), (spread_step, 10), (end_spread, 14))
     for t in range(total + stages[-1][1]):
         for stage, lag in stages:
             if 0 <= t - lag < total:
                 stage(t - lag)
+        for stage in beside.get(t, ()):
+            stage()
     for a in range(2):
         for d in (1, 2, 3):
             exchange(a, d, peer_of(shard, d)).wait_send()
@@ -884,28 +1022,79 @@
         def _():
             down(k, own).wait_send()
 
-        pltpu.make_async_copy(own.at[at], dst(core), out_sem.at[k]).wait()
-        remote(own.at[at], dst(core), mate_send.at[k], mate_recv.at[k], mate).wait_send()
-        remote(own.at[at], dst(1 - core), mate_send.at[k], mate_recv.at[k], mate).wait_recv()
-
-
-def reduce_gradients(levels, pa, pd, pg, pu):
+        pltpu.make_async_copy(own.at[at], dst(core), v["out_sem"].at[k]).wait()
+        remote(own.at[at], dst(core), v["mate_send"].at[k], v["mate_recv"].at[k], mate).wait_send()
+        remote(own.at[at], dst(1 - core), v["mate_send"].at[k], v["mate_recv"].at[k], mate).wait_recv()
+    for a in range(2):
+        for d in (0, 1, 2, 3):
+            p = peer_of(shard, d)
+            to_mate(a, d).wait_send()
+            wide_copy(a, d, False, core, shard, p).wait_send()
+            onward(a, d, block(narrow[a][1], p, core), p, core).wait_send()
+            if d:
+                to_owner(a, d).wait_send()
+                wide_copy(a, d, True, core, shard, p).wait_send()
+                narrow_copy(a, d, shard, p).wait_send()
+    for d in order:
+        vec_hop(d).wait_send()
+    for j in range(1, replicas):
+        vec_spread(j, replica).wait_send()
+
+
+def backward(levels, grad_scale, **given):
     bf16 = jnp.bfloat16
-    shapes = [(2, 384, 1792), (2, WINDOW, 1536), (2, 4, 384, WINDOW), (2, 4, 384, WINDOW)]
-    buffers = [(384, 1792), (WINDOW, 1536), (3072, WINDOW)]
-    total = 36
+    f32 = jnp.float32
     dma = pltpu.SemaphoreType.DMA
+    in_hbm = ("pd", "pg", "pu", "p_back", "p_out", "wo", "wq")
+    outs = {
+        "fa": ((2, 384, 1792), bf16, any_spec()),
+        "fd": ((2, WINDOW, 1536), bf16, any_spec()),
+        "fg": ((2, 4, 384, WINDOW), bf16, any_spec()),
+        "fu": ((2, 4, 384, WINDOW), bf16, any_spec()),
+        "block_out": ((128, 1536), bf16, vmem_spec()),
+        "input_grad": ((128, 1536), f32, vmem_spec()),
+        "vec_out": ((8, 1280), f32, vmem_spec()),
+    }
+    scratch = {}
+    for where in ("own", "low", "high"):
+        scratch[where + "_a"] = pltpu.VMEM((384, 1792), bf16)
+        scratch[where + "_d"] = pltpu.VMEM((WINDOW, 1536), bf16)
+        scratch[where + "_g"] = pltpu.VMEM((3072, WINDOW), bf16)
+    scratch |= {
+        "held": pltpu.VMEM((2, 4, 128, 1536), bf16),
+        "kept": pltpu.VMEM((2, 4, 128, 1536), bf16),
+        "parts": pltpu.VMEM((2, 3, 128, 1536), bf16),
+        "wbuf": pltpu.VMEM((1536, 2048), bf16),
+        "hgrad": pltpu.VMEM((128, 1536), f32),
+        "ngrad": pltpu.VMEM((128, 1536), f32),
+        "hid": pltpu.VMEM((128, 1536), bf16),
+        "cgrad": pltpu.VMEM((128, 1536), bf16),
+        "prj": pltpu.VMEM((128, 2048), bf16),
+        "ctx_all": pltpu.VMEM((1024, 384), bf16),
+        "nrm_all": pltpu.VMEM((1024, 384), bf16),
+        "hid_all": pltpu.VMEM((1024, 768), bf16),
+        "prj_all": pltpu.VMEM((1024, 1024), bf16),
+        "row_two": pltpu.VMEM((1, 1536), f32),
+        "vec": pltpu.VMEM((4, 8, 1280), f32),
+        "vin": pltpu.VMEM((3, 8, 1280), f32),
+        "vsum": pltpu.VMEM((8, 1280), f32),
+        "vall": pltpu.VMEM((2 * levels, 8, 1280), f32),
+    }
+    counts = {
+        "xsend": 8, "xrecv": 8, "csend": 8, "crecv": 8, "keep_sem": 8, "psend": 6, "precv": 6, "gsend": 24, "grecv": 24,
+        "fsend": 8, "frecv": 8, "local": 6, "in_sem": 4, "vsend": 2 + 2 * levels, "vrecv": 2 + 2 * levels,
+    }
+    for name in ("up_sem", "down_sem", "low_sem", "high_sem", "mate_send", "mate_recv", "out_sem"):
+        counts[name] = 36
+    scratch |= {name: dma((n,)) for name, n in counts.items()}
     return pl.pallas_call(
-        functools.partial(reduce_kernel, levels),
-        out_shape=[jax.ShapeDtypeStruct(s, bf16) for s in shapes],
-        in_specs=[any_spec()] * 4,
-        out_specs=[any_spec()] * 4,
-        scratch_shapes=[pltpu.VMEM(s, bf16) for s in buffers * 3]
-        + [dma((8,)), dma((8,))]
-        + [dma((total,))] * 7
-        + [dma((4,))],
-        compiler_params=params(),
-    )(pa, pd, pg, pu)
+        functools.partial(backward_kernel, levels, grad_scale, (*given, *outs, *scratch)),
+        out_shape=[jax.ShapeDtypeStruct(s, dt) for s, dt, _ in outs.values()],
+        in_specs=[any_spec() if name in in_hbm else vmem_spec() for name in given],
+        out_specs=[spec for _, _, spec in outs.values()],
+        scratch_shapes=list(scratch.values()),
+        compiler_params=pltpu.CompilerParams(has_side_effects=True, vmem_limit_bytes=67043328),
+    )(*given.values())
 
 
 def widen_kernel(x, out):
@@ -1000,45 +1189,32 @@
     up_part = (jnp.einsum("td,tf->df", normed_all, up_delta, preferred_element_type=f32) * grad_scale).astype(bf16)
     down_part = (jnp.einsum("tf,td->fd", activation, cot_all, preferred_element_type=f32) * grad_scale).astype(bf16)
 
-    down_sum, normed_two_grad = plane_scatter(down_out, back)
-    block_output = (hidden_res + down_sum).astype(bf16)
-    gain_two_grad = jnp.sum(normed_two_grad * hidden_res * inv_two, axis=0) * grad_scale
-    hidden_grad = cotangent.astype(f32) + inv_two * (
-        gain_two * normed_two_grad
-        - hidden_res
-        * inv_two
-        * inv_two
-        * jnp.mean(gain_two * normed_two_grad * hidden_res, axis=-1, keepdims=True)
-    )
-    hidden_low = hidden_grad.astype(bf16)
-    context_grad = jnp.einsum("td,ed->te", hidden_low, out_full, preferred_element_type=f32).astype(bf16)
-    query_grad, key_grad, value_grad = attend_backward(queries, key_rot, values, logsum, context_grad)
-    query_grad = unrotate(query_grad, cosine, sine_table).reshape(tok_count, q_width)
-    key_grad = unrotate(key_grad, cosine, sine_table).reshape(tok_count, KV * HD)
-    projected_grad = jnp.concatenate(
-        [query_grad, key_grad, value_grad.reshape(tok_count, KV * HD)], axis=-1
-    ).astype(bf16)
-    normed_one_grad = jnp.einsum("tc,dc->td", projected_grad, qkv_full, preferred_element_type=f32)
-    gain_one_grad = jnp.sum(normed_one_grad * xfloat * inv_one, axis=0) * grad_scale
-    bias_grad = jnp.sum(projected_grad.astype(f32), axis=0) * grad_scale
-    input_grad = hidden_grad + inv_one * (
-        gain_one * normed_one_grad
-        - xfloat
-        * inv_one
-        * inv_one
-        * jnp.mean(gain_one * normed_one_grad * xfloat, axis=-1, keepdims=True)
-    )
-    vectors = lax.psum(jnp.concatenate([gain_one_grad, bias_grad, gain_two_grad]), ("replica", "shard"))
-    gain_one_own = lax.dynamic_slice_in_dim(vectors, shard * 384, 384)
-    bias_own = lax.dynamic_slice_in_dim(vectors, 1536 + shard * 512, 512)
-    gain_two_own = lax.dynamic_slice_in_dim(vectors, 3584 + shard * 384, 384)
-
-    ctx_rows, normed_rows, hidden_rows, projected_rows = attn_gather(context, normed_one, hidden_low, projected_grad)
-    qkv_part = jnp.einsum("td,tc->dc", normed_rows, projected_rows, preferred_element_type=f32)
-    out_part = jnp.einsum("te,td->ed", ctx_rows, hidden_rows, preferred_element_type=f32)
-    attn_part = (jnp.concatenate([qkv_part, out_part], axis=1) * grad_scale).astype(bf16)
-
-    sum_attn, sum_down, sum_gate, sum_up = reduce_gradients(levels, attn_part, down_part, gate_part, up_part)
+    sums = logsum.reshape(HEADS, tok_count).T
+    sum_attn, sum_down, sum_gate, sum_up, block_output, input_grad, vectors = backward(
+        levels,
+        grad_scale,
+        pd=down_part,
+        pg=gate_part,
+        pu=up_part,
+        p_back=back,
+        p_out=down_out,
+        wo=out_full,
+        wq=qkv_full,
+        hidden=hidden_res,
+        x=block_input,
+        cot=cotangent,
+        gain_one=gain_one[None, :],
+        gain_two=gain_two[None, :],
+        ctx=context,
+        nrm=normed_one,
+        qry=queries.reshape(tok_count, q_width),
+        key=key_rot.reshape(tok_count, KV * HD),
+        val=values.reshape(tok_count, KV * HD),
+        lse=jnp.pad(sums, ((0, 0), (0, HD - HEADS))),
+        cos=jnp.concatenate([cosine[:, 0], cosine[:, 0]], axis=1),
+        sin=jnp.concatenate([sine_table[:, 0], -sine_table[:, 0]], axis=1),
+    )
+    gain_one_own, bias_own, gain_two_own = vectors[0, :384], vectors[0, 384:896], vectors[0, 896:]
     qkv_grad = jnp.concatenate([sum_attn[0, :, :1024], sum_attn[1, :, :1024]], axis=1).astype(f32)
     out_grad = jnp.concatenate([sum_attn[0, :, 1024:], sum_attn[1, :, 1024:]], axis=1).astype(f32)
     down_grad = lax.dynamic_slice_in_dim(

time: 782 us -> 694 us (0.89)
  blocking collectives: 39.8 us -> 0 us
  Pallas kernels: 612 us -> 588 us
  matrix products: 83.2 us -> 65.4 us
  other arithmetic: 27.3 us -> 18.2 us
    psum x1 -> x0, blocking collectives: 39.8 us -> none  [fast_device(): lax.psum(jnp.concatenate([gain_one_grad, bias_grad, gain_two_grad]), ('re...]
    pallas_call x3 -> x1, Pallas kernels: 432 us -> 408 us  [backward(): pl.pallas_call(functools.partial(backward_kernel, levels, grad_scale, (*g...]
    dot_general x8 -> x0, matrix products: 18.3 us -> none  [the longest x1 5.38 us: fast_device(): jnp.einsum('tc,dc->td', projected_grad, qkv_full, preferred_element_type=...]
where the time goes in v3:
time: 694 us; the launch traced here: 688 us
  Pallas kernels  588 us (85%)
  matrix products  65.4 us (9%)
  other arithmetic  18.2 us (3%)
  local copies, waits for them, and re-layouts  14.6 us (2%)
    pallas_call x1, Pallas kernels, backward(): pl.pallas_call(functools.partial(backward_kernel, levels, grad_scale, (*g...  408 us
    pallas_call x1, Pallas kernels, front(): pl.pallas_call(front_kernel, out_shape=[jax.ShapeDtypeStruct(s, bf16) for...  130 us
    pallas_call x1, Pallas kernels, plane_gather(): pl.pallas_call(gather_kernel, out_shape=jax.ShapeDtypeStruct((x.shape[0]...  28.8 us
    pallas_call x2, Pallas kernels, widen(): pl.pallas_call(widen_kernel, grid=(384 // rows,), out_shape=jax.ShapeDtyp...  21.9 us

profile of v3, /device:TPU:0, one launch (start us, length us, event | category | flops | bytes accessed | tf_op | source)
XLA Modules:
  0.0 688.0 jit_solution(17869623389035641940)
XLA Ops:
  0.7 1.2 fusion.7
  1.9 0.7 reshape.239
  2.6 0.7 reshape.241
  3.2 0.7 reshape.240
  4.0 0.2 scatter.14.small
  4.2 0.3 fusion.17
  4.6 0.8 pad_maximum_fusion.1
  5.4 129.5 %shard_map.177 = (bf16[1536,2048]{1,0:T(8,128)(2,1)}, bf16[1536,1536]{1,0:T(8,128)(2,1)}, bf16[1536,1152]{1,0:T(8,128)(2,1)}, bf16[1536,1152]{1,0:T(8,128)(2,1)}...) custom-call(bf16[384,2048]{1,0:T(8,128)(2,1)} %wq.1, bf16[384,1536]{1,0:T(8,128)(2,1)} %wo.1, ...), custom_call_target="tpu_custom_call" | custom-call | tf_op jit(solution)/shard_map/pallas_call | solution.py:482
  135.0 0.8 slice_convert_fusion.1
  135.7 1.4 slice_convert_fusion.2
  137.1 0.9 fusion.27
  138.0 0.2 fusion.9.refs_13_
  138.2 3.9 convolution_add_fusion.1
  142.4 0.3 copy.32
  142.8 0.2 fusion.28
  143.1 0.7 copy_bitcast_fusion.refs_15_
  143.8 0.9 copy.42.refs_14_
  144.8 0.2 copy.35
  145.0 0.2 copy.36
  145.3 0.4 fusion.29
  145.8 0.3 convolution_convert_fusion.1
  146.3 0.6 pad.19.refs_17_
  146.9 0.9 copy.41.refs_12_
  147.8 3.2 multiply_reduce_fusion
  151.1 0.9 copy-done
  151.9 0.9 multiply_convert_fusion.x
  152.8 28.8 %shard_map.178 = bf16[1024,1536]{1,0:T(8,128)(2,1)} custom-call(bf16[128,1536]{1,0:T(8,128)(2,1)} %multiply_convert_fusion.x), custom_call_target="tpu_custom_call" | custom-call | tf_op jit(solution)/shard_map/pallas_call | solution.py:528
  181.6 7.3 %fusion.32 = f32[1024,1152]{1,0:T(8,128)S(1)} fusion(bf16[1024,1536]{1,0:T(8,128)(2,1)} %shard_map.178, bf16[1536,1152]{1,0:T(8,128)(2,1)} %get-tuple-element.81), kind=kOutput, calls=%fused_computation.81 | convolution fusion | flops 3623878656 | bytes 11403264 | tf_op jit(solution)/shard_map/dot_general | solution.py:1174
  189.0 5.8 fusion.31
  194.8 9.8 %select_convert_fusion = (bf16[1024,1152]{1,0:T(8,128)(2,1)}, bf16[1024,1152]{1,0:T(8,128)(2,1)}, bf16[1024,1152]{1,0:T(8,128)(2,1)}) fusion(pred[1152]{0:T(1024)(128)(4,1)S(1)} %fusion.20, f32[1024,1152]{1,0:T(8,128)} %fusion.31, f32[1024,1152]{1,0:T(8,128)S(1)} %fusion.32, bf16[1024,1536]{1,0:T(8,128)(2,1)S(1)} %copy-done.10, s32[]{:T(128)S(6)} %select_n.29, ...), kind=kOutput, calls=%fused_computation.9 | convolution fusion | flops 3645112320 | bytes 26543236 | tf_op jit(solution)/shard_map/td,fd->tf/dot_general | solution.py:1177
  204.6 7.2 %fusion.refs_0_ = bf16[1152,1536]{1,0:T(8,128)(2,1)} fusion(bf16[1024,1152]{1,0:T(8,128)(2,1)} %get-tuple-element.96, bf16[1024,1536]{1,0:T(8,128)(2,1)S(1)} %copy-done.10), kind=kOutput, calls=%fused_computation.3 | convolution fusion | flops 3627417600 | bytes 9043968 | tf_op jit(solution)/shard_map/tf,td->fd/dot_general | solution.py:1190
  211.8 6.0 convolution_convert_fusion.refs_4_
  217.8 4.3 fusion.33
  222.1 5.7 add_convert_fusion.refs_3_
  227.8 5.8 fusion.2.refs_2_
  233.6 5.7 fusion.1.refs_1_
  239.3 408.2 %shard_map.179 = (bf16[2,384,1792]{2,1,0:T(8,128)(2,1)}, bf16[2,1152,1536]{2,1,0:T(8,128)(2,1)}, bf16[2,4,384,1152]{3,2,1,0:T(8,128)(2,1)}, bf16[2,4,384,1152]{3...) custom-call(bf16[1152,1536]{1,0:T(8,128)(2,1)} %fusion.refs_0_, ...), custom_call_target="tpu_custom_call" | custom-call | tf_op jit(solution)/shard_map/pallas_call | solution.py:1090
  647.5 1.3 slice.114
  648.8 1.3 slice_reduce_fusion
  650.1 1.5 slice_bitcast_fusion.3
  651.6 1.6 slice_bitcast_fusion.1
  653.2 1.7 maximum_convert_fusion.1
  654.9 2.0 maximum_convert_fusion
  657.0 7.1 %dynamic-slice_convert_fusion = f32[2240,1536]{1,0:T(8,128)} fusion(bf16[2304,1536]{1,0:T(8,128)(2,1)S(1)} %bitcast.65, s32[]{:T(128)S(6)} %select_n.32), kind=kLoop, calls=%fused_computation.7 | loop fusion | flops 3440640 | bytes 20643844 | tf_op jit(solution)/shard_map/convert_element_type | solution.py:1222
  664.1 10.9 %shard_map.180 = f32[384,8960]{1,0:T(8,128)} custom-call(bf16[2,4,384,1152]{3,2,1,0:T(8,128)(2,1)} %get-tuple-element.87.x), custom_call_target="tpu_custom_call" | custom-call | tf_op jit(solution)/shard_map/pallas_call | solution.py:1115
  675.0 11.0 %shard_map.181 = f32[384,8960]{1,0:T(8,128)} custom-call(bf16[2,4,384,1152]{3,2,1,0:T(8,128)(2,1)} %get-tuple-element.88.x), custom_call_target="tpu_custom_call" | custom-call | tf_op jit(solution)/shard_map/pallas_call | solution.py:1115
  686.0 0.7 copy.59
  686.7 0.9 copy.60
  (60 shorter events, 1.0 us)
Async XLA Ops:
  4.2 1.2 copy-start.7
  5.4 132.6 %copy-start.1 = (bf16[128,1536]{1,0:T(8,128)(2,1)S(1)}, bf16[128,1536]{1,0:T(8,128)(2,1)}, u32[]{:S(2)}) copy-start(bf16[128,1536]{1,0:T(8,128)(2,1)} %refs_8_.1) | copy-start | bytes 1179652
  138.2 3.9 copy-start.2
  142.2 1.7 copy-start.5
  151.0 0.9 copy-start
  181.6 7.4 %copy-start.3 = (bf16[1024,1536]{1,0:T(8,128)(2,1)S(1)}, bf16[1024,1536]{1,0:T(8,128)(2,1)}, u32[]{:S(2)}) copy-start(bf16[1024,1536]{1,0:T(8,128)(2,1)} %shard_map.178) | copy-start | bytes 9437188
  181.6 7.4 %copy-start.9 = (bf16[1536,1152]{1,0:T(8,128)(2,1)S(1)}, bf16[1536,1152]{1,0:T(8,128)(2,1)}, u32[]{:S(2)}) copy-start(bf16[1536,1152]{1,0:T(8,128)(2,1)} %get-tuple-element.80) | copy-start | bytes 10616836
  181.6 13.2 %slice-start.2 = ((s8[6881280]{0:T(1024)(128)(4,1)}), s8[4194304]{0:T(1024)(128)(4,1)S(1)}, s32[]{:S(2)}) async-start(s8[6881280]{0:T(1024)(128)(4,1)} %bitcast.78), calls=%async_computation.2 | async-start | bytes 8388608
  189.0 5.8 slice-start.3
  189.0 5.8 copy-start.10
  204.6 7.2 %copy-start.11 = (bf16[1024,1152]{1,0:T(8,128)(2,1)S(1)}, bf16[1024,1152]{1,0:T(8,128)(2,1)}, u32[]{:S(2)}) copy-start(bf16[1024,1152]{1,0:T(8,128)(2,1)} %get-tuple-element.96) | copy-start | bytes 7077892
  211.8 6.0 copy-start.12
  217.8 4.3 copy-start.8
  217.8 4.3 copy-start.13
  650.1 6.9 slice-start
  653.2 3.7 slice-start.1
  675.0 11.0 %copy-start.6 = (bf16[128,1536]{1,0:T(8,128)(2,1)S(1)}, bf16[128,1536]{1,0:T(8,128)(2,1)}, u32[]{:S(2)}) copy-start(bf16[128,1536]{1,0:T(8,128)(2,1)} %get-tuple-element.128) | copy-start | bytes 1179652
  675.0 11.8 %copy-start.4 = (f32[128,1536]{1,0:T(8,128)S(1)}, f32[128,1536]{1,0:T(8,128)}, u32[]{:S(2)}) copy-start(f32[128,1536]{1,0:T(8,128)} %get-tuple-element.129) | copy-start | bytes 2359300

commit v4 on v3

--- a/solution.py
+++ b/solution.py
@@ -536,7 +536,14 @@
 
 
 CHUNK = 128
+DOWN_CHUNKS = (64, 64) + (128,) * 8
+ATTENTION_CHUNKS = (64, 64, 64, 64, 32, 32, 32, 32)
+CHUNKS = len(DOWN_CHUNKS) + 24 + len(ATTENTION_CHUNKS)
 SCORE_SCALE = 1.0 / math.sqrt(HD)
+
+
+def row_spans(sizes):
+    return [pl.ds(sum(sizes[:k]), size) for k, size in enumerate(sizes)]
 
 
 def dot_nt(a, b):
@@ -707,13 +714,14 @@
     def unrotated(x):
         return x * v["cos"][...] + pltpu.roll(x, HD // 2, 1) * v["sin"][...]
 
-    def stage_heads(g):
+    def stage_heads(g, part):
         keys = v["key"][:, g * HD : (g + 1) * HD]
         values = v["val"][:, g * HD : (g + 1) * HD]
         causal = lax.broadcasted_iota(jnp.int32, (128, 128), 0) >= lax.broadcasted_iota(jnp.int32, (128, 128), 1)
-        key_grad = jnp.zeros((128, HD), f32)
-        value_grad = jnp.zeros((128, HD), f32)
-        for h in range(g * (HEADS // KV), (g + 1) * (HEADS // KV)):
+        key_grad = jnp.zeros((128, HD), f32) if part == 0 else v["kv_sum"][0]
+        value_grad = jnp.zeros((128, HD), f32) if part == 0 else v["kv_sum"][1]
+        first_head = g * (HEADS // KV) + part * 2
+        for h in range(first_head, first_head + 2):
             at = slice(h * HD, (h + 1) * HD)
             query = v["qry"][:, at]
             grad = v["cgrad"][:, at]
@@ -726,6 +734,10 @@
             v["prj"][:, at] = unrotated(jnp.dot(score_grad, keys, preferred_element_type=f32)).astype(bf16)
             key_grad = key_grad + dot_tn(score_grad, query)
             value_grad = value_grad + dot_tn(probs, grad)
+        if part < 2:
+            v["kv_sum"][0] = key_grad
+            v["kv_sum"][1] = value_grad
+            return
         first = HEADS * HD + g * HD
         v["prj"][:, first : first + HD] = unrotated(key_grad).astype(bf16)
         first = first + KV * HD
@@ -738,9 +750,10 @@
             wide_copy(1, d, False, core, shard, peer_of(shard, d)).start()
         own_wide(1).start()
 
-    def stage_normed():
-        load_qkv.wait()
-        for e in range(4):
+    def stage_normed(part):
+        if part == 0:
+            load_qkv.wait()
+        for e in (2 * part, 2 * part + 1):
             cols = pl.ds(e * 384, 384)
             v["ngrad"][:, cols] = dot_nt(v["prj"][...], wbuf[cols, :])
 
@@ -818,7 +831,7 @@
                 narrow_copy(a, d, p, p).wait_recv()
                 onward(a, d, block(narrow[a][1], p, core), p, core).start()
 
-    def stage_attention_parts():
+    def stage_gathered():
         for a in range(2):
             own_narrow(a).wait()
             own_wide(a).wait()
@@ -828,14 +841,14 @@
                     wide_copy(a, d, True, core, p, p).wait_recv()
                 wide_copy(a, d, False, other, p, p).wait_recv()
                 onward(a, d, block(narrow[a][1], p, other), p, other).wait_recv()
-        for j in range(3):
-            at = pl.ds(j * 128, 128)
-            own_a[at, 0:1024] = (dot_tn(v["nrm_all"][:, at], v["prj_all"][...]) * grad_scale).astype(bf16)
-            own_a[at, 1024:1792] = (dot_tn(v["ctx_all"][:, at], v["hid_all"][...]) * grad_scale).astype(bf16)
+
+    def stage_attention_parts(j):
+        at = pl.ds(j * 128, 128)
+        own_a[at, 0:1024] = (dot_tn(v["nrm_all"][:, at], v["prj_all"][...]) * grad_scale).astype(bf16)
+        own_a[at, 1024:1792] = (dot_tn(v["ctx_all"][:, at], v["hid_all"][...]) * grad_scale).astype(bf16)
 
     chunks = []
-    for k in range(9):
-        at = pl.ds(k * CHUNK, CHUNK)
+    for at in row_spans(DOWN_CHUNKS):
         chunks.append((own_d, v["low_d"], v["high_d"], at, ("fill", 1), lambda c, at=at: v["fd"].at[c, at]))
     for d in range(4):
         for a in range(2):
@@ -847,8 +860,7 @@
                     own_g, v["low_g"], v["high_g"], at, ("fill", 2 + a) if d == 0 else ("x", a, d),
                     lambda c, k=k, dst=dst, source=source: dst.at[c, source, pl.ds(k * CHUNK, CHUNK)],
                 ))
-    for k in range(3):
-        at = pl.ds(k * CHUNK, CHUNK)
+    for at in row_spans(ATTENTION_CHUNKS):
         chunks.append((own_a, v["low_a"], v["high_a"], at, ("none",), lambda c, at=at: v["fa"].at[c, at]))
     total = len(chunks)
     awaited = (set(), set())
@@ -883,7 +895,7 @@
             own[rows, :] = value.astype(own.dtype)
             return carry
 
-        lax.fori_loop(0, CHUNK // step, body, 0)
+        lax.fori_loop(0, at.size // step, body, 0)
 
     def finish(k, ref):
         _, _, _, at, _, dst = chunks[k]
@@ -989,19 +1001,25 @@
         onward(a, 0, columns(narrow[a][0], shard, 384), shard, core).start()
     beside = {
         0: [stage_sums],
-        3: [stage_hidden],
-        4: [stage_context],
-        5: [functools.partial(stage_heads, 0)],
-        6: [functools.partial(stage_heads, 1), stage_send_projected],
-        7: [stage_normed],
-        8: [stage_input],
-        10: [stage_vec],
-        12: [stage_relay],
-        14: [stage_vec_out],
-        24: [stage_output],
-        27: [stage_attention_parts],
+        11: [stage_hidden],
+        12: [stage_context],
+        13: [functools.partial(stage_heads, 0, 0)],
+        14: [functools.partial(stage_heads, 0, 1), stage_relay],
+        15: [functools.partial(stage_heads, 0, 2)],
+        16: [functools.partial(stage_heads, 1, 0)],
+        17: [functools.partial(stage_heads, 1, 1)],
+        18: [functools.partial(stage_heads, 1, 2), stage_send_projected],
+        19: [functools.partial(stage_normed, 0)],
+        20: [functools.partial(stage_normed, 1)],
+        21: [stage_input],
+        22: [stage_vec],
+        25: [stage_vec_out],
+        29: [stage_output],
+        30: [stage_gathered, functools.partial(stage_attention_parts, 0)],
+        31: [functools.partial(stage_attention_parts, 1)],
+        32: [functools.partial(stage_attention_parts, 2)],
     }
-    stages = ((end_gather, 0), (gather_step, 4), (root_step, 7), (spread_step, 10), (end_spread, 14))
+    stages = ((end_gather, 0), (gather_step, 6), (root_step, 10), (spread_step, 14), (end_spread, 20))
     for t in range(total + stages[-1][1]):
         for stage, lag in stages:
             if 0 <= t - lag < total:
@@ -1075,6 +1093,7 @@
         "hid_all": pltpu.VMEM((1024, 768), bf16),
         "prj_all": pltpu.VMEM((1024, 1024), bf16),
         "row_two": pltpu.VMEM((1, 1536), f32),
+        "kv_sum": pltpu.VMEM((2, 128, HD), f32),
         "vec": pltpu.VMEM((4, 8, 1280), f32),
         "vin": pltpu.VMEM((3, 8, 1280), f32),
         "vsum": pltpu.VMEM((8, 1280), f32),
@@ -1085,7 +1104,7 @@
         "fsend": 8, "frecv": 8, "local": 6, "in_sem": 4, "vsend": 2 + 2 * levels, "vrecv": 2 + 2 * levels,
     }
     for name in ("up_sem", "down_sem", "low_sem", "high_sem", "mate_send", "mate_recv", "out_sem"):
-        counts[name] = 36
+        counts[name] = CHUNKS
     scratch |= {name: dma((n,)) for name, n in counts.items()}
     return pl.pallas_call(
         functools.partial(backward_kernel, levels, grad_scale, (*given, *outs, *scratch)),
@@ -1097,28 +1116,28 @@
     )(*given.values())
 
 
-def widen_kernel(x, out):
+def widen_kernel(x_gate, x_up, out_gate, out_up):
     f32 = jnp.float32
-    for s in range(4):
-        for c in range(2):
-            first = (s * 35) // 2 + c * 9
-            joined = s % 2 == 1 and c == 0
-            rest = 1 if joined else 0
-            out[:, (first + rest) * 128 : (first + 9) * 128] = x[c, s][:, rest * 128 :].astype(f32)
-    for s in (1, 3):
-        first = (s * 35) // 2
-        out[:, first * 128 : (first + 1) * 128] = x[1, s - 1][:, 1024:].astype(f32) + x[0, s][:, :128].astype(f32)
-
-
-def widen(x):
+    for x, out in ((x_gate, out_gate), (x_up, out_up)):
+        for s in range(4):
+            for c in range(2):
+                first = (s * 35) // 2 + c * 9
+                rest = 1 if s % 2 == 1 and c == 0 else 0
+                out[:, (first + rest) * 128 : (first + 9) * 128] = x[c, s][:, rest * 128 :].astype(f32)
+        for s in (1, 3):
+            first = (s * 35) // 2
+            out[:, first * 128 : (first + 1) * 128] = x[1, s - 1][:, 1024:].astype(f32) + x[0, s][:, :128].astype(f32)
+
+
+def widen(*sums):
     rows = 32
     return pl.pallas_call(
         widen_kernel,
         grid=(384 // rows,),
-        out_shape=jax.ShapeDtypeStruct((384, 8960), jnp.float32),
-        in_specs=[pl.BlockSpec((2, 4, rows, WINDOW), lambda i: (0, 0, i, 0))],
-        out_specs=pl.BlockSpec((rows, 8960), lambda i: (i, 0)),
-    )(x)
+        out_shape=[jax.ShapeDtypeStruct((384, 8960), jnp.float32)] * 2,
+        in_specs=[pl.BlockSpec((2, 4, rows, WINDOW), lambda i: (0, 0, i, 0))] * 2,
+        out_specs=[pl.BlockSpec((rows, 8960), lambda i: (i, 0))] * 2,
+    )(*sums)
 
 
 def fast_device(
@@ -1220,6 +1239,7 @@
     down_grad = lax.dynamic_slice_in_dim(
         sum_down.reshape(2 * WINDOW, 1536), lax.rem(shard, 2) * 64, 2240, 0
     ).astype(f32)
+    gate_grad, up_grad = widen(sum_gate, sum_up)
     return (
         block_output,
         input_grad,
@@ -1228,8 +1248,8 @@
         bias_own,
         out_grad,
         gain_two_own,
-        widen(sum_gate),
-        widen(sum_up),
+        gate_grad,
+        up_grad,
         down_grad,
     )
 

time: 694 us -> 627 us (0.903)
  Pallas kernels: 588 us -> 519 us
    pallas_call x1, Pallas kernels: 408 us -> 345 us  [backward(): pl.pallas_call(functools.partial(backward_kernel, levels, grad_scale, (*g...]
    pallas_call x2 -> x1, Pallas kernels: 21.9 us -> 15.7 us  [widen(): pl.pallas_call(widen_kernel, grid=(384 // rows,), out_shape=[jax.ShapeDty...]
where the time goes in v4:
time: 627 us; the launch traced here: 622 us
  Pallas kernels  519 us (83%)
  matrix products  66.7 us (11%)
  other arithmetic  22.2 us (4%)
  local copies, waits for them, and re-layouts  12.2 us (2%)
    pallas_call x1, Pallas kernels, backward(): pl.pallas_call(functools.partial(backward_kernel, levels, grad_scale, (*g...  345 us
    pallas_call x1, Pallas kernels, front(): pl.pallas_call(front_kernel, out_shape=[jax.ShapeDtypeStruct(s, bf16) for...  130 us
    pallas_call x1, Pallas kernels, plane_gather(): pl.pallas_call(gather_kernel, out_shape=jax.ShapeDtypeStruct((x.shape[0]...  28.8 us
    pallas_call x1, Pallas kernels, widen(): pl.pallas_call(widen_kernel, grid=(384 // rows,), out_shape=[jax.ShapeDty...  15.7 us

profile of v4, /device:TPU:0, one launch (start us, length us, event | category | flops | bytes accessed | tf_op | source)
XLA Modules:
  0.0 621.5 jit_solution(11006002024988738932)
XLA Ops:
  0.6 0.7 reshape.239
  1.3 0.7 reshape.240
  2.0 0.7 reshape.241
  2.9 0.6 copy-done.16
  3.5 129.5 %shard_map.177 = (bf16[1536,2048]{1,0:T(8,128)(2,1)}, bf16[1536,1536]{1,0:T(8,128)(2,1)}, bf16[1536,1152]{1,0:T(8,128)(2,1)}, bf16[1536,1152]{1,0:T(8,128)(2,1)}...) custom-call(bf16[384,2048]{1,0:T(8,128)(2,1)} %wq.1, bf16[384,1536]{1,0:T(8,128)(2,1)} %wo.1, ...), custom_call_target="tpu_custom_call" | custom-call | tf_op jit(solution)/shard_map/pallas_call | solution.py:482
  133.0 1.4 fusion.27
  134.4 0.2 fusion.7
  134.6 0.2 fusion.9.refs_13_
  134.8 0.8 slice_convert_fusion.1
  135.6 3.8 convolution_add_fusion.1
  139.5 0.2 fusion.28
  139.7 0.9 fusion.17
  140.6 0.7 multiply_subtract_fusion
  141.3 0.3 copy.32
  141.7 0.1 subtract_convert_fusion
  141.9 0.2 copy.35
  142.1 0.2 copy.36
  142.4 1.3 fusion.29
  144.0 0.3 convolution_convert_fusion.1
  144.3 3.2 multiply_reduce_fusion
  147.6 0.8 copy-done
  148.4 0.9 multiply_convert_fusion.x
  149.3 28.8 %shard_map.178 = bf16[1024,1536]{1,0:T(8,128)(2,1)} custom-call(bf16[128,1536]{1,0:T(8,128)(2,1)} %multiply_convert_fusion.x), custom_call_target="tpu_custom_call" | custom-call | tf_op jit(solution)/shard_map/pallas_call | solution.py:528
  178.1 9.5 %fusion.32 = f32[1024,1152]{1,0:T(8,128)} fusion(bf16[1024,1536]{1,0:T(8,128)(2,1)} %shard_map.178, bf16[1536,1152]{1,0:T(8,128)(2,1)} %get-tuple-element.83), kind=kOutput, calls=%fused_computation.81 | convolution fusion | flops 3623878656 | bytes 11403264 | tf_op jit(solution)/shard_map/dot_general | solution.py:1193
  187.6 5.8 fusion.31
  193.4 10.1 %select_convert_fusion = (bf16[1024,1152]{1,0:T(8,128)(2,1)S(1)}, bf16[1024,1152]{1,0:T(8,128)(2,1)S(1)}, bf16[1024,1152]{1,0:T(8,128)(2,1)S(1)}) fusion(pred[1152]{0:T(1024)(128)(4,1)S(1)} %fusion.20, f32[1024,1152]{1,0:T(8,128)} %fusion.31, f32[1024,1152]{1,0:T(8,128)} %fusion.32, bf16[1024,1536]{1,0:T(8,128)(2,1)} %get-tuple-element.84, ...), kind=kOutput, calls=%fused_computation.9 | convolution fusion | flops 3645112320 | bytes 26543236 | tf_op jit(solution)/shard_map/td,fd->tf/dot_general | solution.py:1196
  203.6 4.3 fusion.33
  207.9 5.7 add_convert_fusion.refs_3_
  213.6 5.9 fusion.2.refs_2_
  219.5 5.7 fusion.1.refs_1_
  225.2 5.4 fusion.refs_0_
  230.7 5.7 convolution_convert_fusion.refs_4_
  236.3 0.9 copy.41.refs_12_
  237.4 0.6 pad.19.refs_17_
  238.0 0.7 copy_bitcast_fusion.refs_15_
  238.8 0.9 copy.42.refs_14_
  239.7 0.8 pad_maximum_fusion.1
  240.5 1.4 slice_convert_fusion.2
  241.9 344.9 %shard_map.179 = (bf16[2,384,1792]{2,1,0:T(8,128)(2,1)}, bf16[2,1152,1536]{2,1,0:T(8,128)(2,1)}, bf16[2,4,384,1152]{3,2,1,0:T(8,128)(2,1)}, bf16[2,4,384,1152]{3...) custom-call(bf16[1152,1536]{1,0:T(8,128)(2,1)} %fusion.refs_0_, ...), custom_call_target="tpu_custom_call" | custom-call | tf_op jit(solution)/shard_map/pallas_call | solution.py:1109
  586.8 15.7 %shard_map.180 = (f32[384,8960]{1,0:T(8,128)}, f32[384,8960]{1,0:T(8,128)}) custom-call(bf16[2,4,384,1152]{3,2,1,0:T(8,128)(2,1)} %get-tuple-element.89.x_gate, bf16[2,4,384,1152]{3,2,1,0:T(8,128)(2,1)} %get-tuple-element.90.x_up), custom_call_target="tpu_custom_call" | custom-call | tf_op jit(solution)/shard_map/pallas_call | solution.py:1134
  602.5 10.2 %dynamic-slice_convert_fusion = f32[2240,1536]{1,0:T(8,128)} fusion(bf16[2304,1536]{1,0:T(8,128)(2,1)} %bitcast.63, s32[]{:T(128)S(6)} %select_n.32), kind=kLoop, calls=%fused_computation.7 | loop fusion | flops 3440640 | bytes 20643844 | tf_op jit(solution)/shard_map/convert_element_type | solution.py:1241
  612.8 1.7 maximum_convert_fusion.1
  614.5 0.2 slice_bitcast_fusion.1
  614.8 2.0 maximum_convert_fusion
  616.8 1.3 slice_reduce_fusion
  618.1 1.3 slice.114
  619.4 0.7 copy.59
  620.2 0.9 copy.60
  (70 shorter events, 1.1 us)
Async XLA Ops:
  2.9 0.6 copy-start.16
  3.5 131.0 %copy-start.1 = (bf16[128,1536]{1,0:T(8,128)(2,1)S(1)}, bf16[128,1536]{1,0:T(8,128)(2,1)}, u32[]{:S(2)}) copy-start(bf16[128,1536]{1,0:T(8,128)(2,1)} %refs_8_.1) | copy-start | bytes 1179652
  134.8 4.6 copy-start.2
  140.6 3.1 copy-start.6
  143.9 3.7 copy-start.14
  143.9 3.7 copy-start.9
  144.0 3.6 copy-start.17
  147.6 0.9 copy-start
  178.1 9.5 %copy-start.3 = (bf16[1024,1536]{1,0:T(8,128)(2,1)S(1)}, bf16[1024,1536]{1,0:T(8,128)(2,1)}, u32[]{:S(2)}) copy-start(bf16[1024,1536]{1,0:T(8,128)(2,1)} %shard_map.178) | copy-start | bytes 9437188
  178.1 9.5 %copy-start.19 = (bf16[1536,1152]{1,0:T(8,128)(2,1)S(1)}, bf16[1536,1152]{1,0:T(8,128)(2,1)}, u32[]{:S(2)}) copy-start(bf16[1536,1152]{1,0:T(8,128)(2,1)} %get-tuple-element.82) | copy-start | bytes 10616836
  193.4 10.2 %copy-start.20 = (bf16[1536,1152]{1,0:T(8,128)(2,1)S(1)}, bf16[1536,1152]{1,0:T(8,128)(2,1)}, u32[]{:S(2)}) copy-start(bf16[1536,1152]{1,0:T(8,128)(2,1)} %get-tuple-element.82) | copy-start | bytes 10616836
  203.6 4.3 copy-start.18
  207.9 5.7 copy-start.4
  213.6 17.0 %slice-start = ((s8[6881280]{0:T(1024)(128)(4,1)}), s8[4194304]{0:T(1024)(128)(4,1)S(1)}, s32[]{:S(2)}) async-start(s8[6881280]{0:T(1024)(128)(4,1)} %bitcast.76), calls=%async_computation | async-start | bytes 8388608
  219.5 5.7 copy-start.21
  219.5 11.1 %slice-start.1 = ((s8[6881280]{0:T(1024)(128)(4,1)}), s8[2686976]{0:T(1024)(128)(4,1)S(1)}, s32[]{:S(2)}) async-start(s8[6881280]{0:T(1024)(128)(4,1)} %bitcast.76), calls=%async_computation.1 | async-start | bytes 5373952
  230.6 6.7 %copy-start.15 = (f32[2,6,128]{2,1,0:T(8,128)S(1)}, f32[2,6,128]{2,1,0:T(8,128)}, u32[]{:S(2)}) copy-start(f32[2,6,128]{2,1,0:T(8,128)} %copy-done.14) | copy-start | bytes 18436
  230.6 7.4 %copy-start.10 = (bf16[128,2,64]{2,0,1:T(8,128)(2,1)S(1)}, bf16[128,2,64]{2,0,1:T(8,128)(2,1)}, u32[]{:S(2)}) copy-start(bf16[128,2,64]{2,0,1:T(8,128)(2,1)} %get-tuple-element.107) | copy-start | bytes 98308
  230.6 7.4 %copy-start.11 = (bf16[128,2,64]{2,0,1:T(8,128)(2,1)S(1)}, bf16[128,2,64]{2,0,1:T(8,128)(2,1)}, u32[]{:S(2)}) copy-start(bf16[128,2,64]{2,0,1:T(8,128)(2,1)} %get-tuple-element.108) | copy-start | bytes 98308
  230.6 9.1 %copy-start.7 = (f32[128,64]{1,0:T(8,128)S(1)}, f32[128,64]{1,0:T(8,128)}, u32[]{:S(2)}) copy-start(f32[128,64]{1,0:T(8,128)} %copy-done.6) | copy-start | bytes 98308
  230.6 9.1 %copy-start.13 = (f32[128,64]{1,0:T(8,128)S(1)}, f32[128,64]{1,0:T(8,128)}, u32[]{:S(2)}) copy-start(f32[128,64]{1,0:T(8,128)} %get-tuple-element.113) | copy-start | bytes 98308
  602.5 10.2 %copy-start.5 = (bf16[2,384,1792]{2,1,0:T(8,128)(2,1)S(1)}, bf16[2,384,1792]{2,1,0:T(8,128)(2,1)}, u32[]{:S(2)}) copy-start(bf16[2,384,1792]{2,1,0:T(8,128)(2,1)} %get-tuple-element.88) | copy-start | bytes 8257540
  614.5 4.9 copy-start.12
  614.7 5.4 copy-start.8

commit v5 on v4

--- a/solution.py
+++ b/solution.py
@@ -328,42 +328,77 @@
     )
 
 
-def front_kernel(
-    wq, wo, wg, wu, cot, small, q_full, o_full, g_own, u_own, cot_all, small_all,
-    bq, bo, bg, bu, bc, bs, send, recv, fsend, frecv, zsend, zrecv, local,
-):
+def any_spec():
+    return pl.BlockSpec(memory_space=pl.ANY)
+
+
+def vmem_spec():
+    return pl.BlockSpec(memory_space=pltpu.VMEM)
+
+
+def params(**more):
+    return pltpu.CompilerParams(has_side_effects=True, vmem_limit_bytes=VMEM_BYTES, **more)
+
+
+CHUNK = 128
+DOWN_CHUNKS = (64, 64) + (128,) * 8
+ATTENTION_CHUNKS = (64, 64, 64, 64, 32, 32, 32, 32)
+CHUNKS = len(DOWN_CHUNKS) + 24 + len(ATTENTION_CHUNKS)
+SCORE_SCALE = 1.0 / math.sqrt(HD)
+
+
+def row_spans(sizes):
+    return [pl.ds(sum(sizes[:k]), size) for k, size in enumerate(sizes)]
+
+
+def dot_nt(a, b):
+    return lax.dot_general(a, b, (((1,), (1,)), ((), ())), preferred_element_type=jnp.float32)
+
+
+def dot_tn(a, b):
+    return lax.dot_general(a, b, (((0,), (0,)), ((), ())), preferred_element_type=jnp.float32)
+
+
+def row_loop(rows, step, body, init):
+    return lax.fori_loop(0, rows // step, lambda j, c: body(pl.ds(pl.multiple_of(j * step, step), step), c), init)
+
+
+TILES = ((0, 640, 192), (640, 512, 160))
+
+
+def forward_kernel(grad_scale, names, *refs):
+    v = dict(zip(names, refs))
+    f32 = jnp.float32
+    bf16 = jnp.bfloat16
     replica, shard, core = place()
     other = 1 - core
     mate = (replica + 1 - 2 * core, shard)
     odd = lax.rem(replica // 2, 2)
     pair = (replica + 2 - 4 * odd, shard)
+    order = (3, 1, 2)
+    first_unit = window_start(shard, core)
+    q_buf, o_buf, g_buf, u_buf, d_buf = v["q_buf"], v["o_buf"], v["g_buf"], v["u_buf"], v["d_buf"]
+    n_all, cot_all, small_all = v["n_all"], v["cot_all"], v["small_all"]
 
     def span(start, size):
         return pl.ds(pl.multiple_of(start, 16), size)
 
-    def cols(target):
-        return pl.ds(pl.multiple_of(window_start(target, core), 128), WINDOW)
-
-    def block(owner, c):
+    def units(target, offset, width):
+        return pl.ds(pl.multiple_of(window_start(target, core) + offset, 128), width)
+
+    def tokens(owner, c):
         return pl.ds(pl.multiple_of((c * 4 + owner) * 128, 128), 128)
 
-    def rows(owner):
-        return pl.ds(pl.multiple_of(owner * 384, 384), 384)
-
-    loads = [
-        (wq, bq, q_full.at[rows(shard)]),
-        (wo, bo, o_full.at[rows(shard)]),
-        (wg.at[:, cols(shard)], bg, g_own.at[rows(shard)]),
-        (wu.at[:, cols(shard)], bu, u_own.at[rows(shard)]),
-        (cot, bc, cot_all.at[block(shard, core)]),
-        (small, bs, small_all.at[shard]),
+    weights = [
+        (lambda t: v["wq"], q_buf, 192, 80, True),
+        (lambda t: v["wo"], o_buf, 192, 80, True),
     ]
-    weights = [
-        (lambda t: wq, q_full, 192, 80, True),
-        (lambda t: wo, o_full, 192, 80, True),
-        (lambda t: wg.at[:, cols(t)], g_own, 384, 176, False),
-        (lambda t: wu.at[:, cols(t)], u_own, 384, 176, False),
-    ]
+    for offset, width, shared in TILES:
+        for name, buf in (("wg", g_buf), ("wu", u_buf)):
+            weights.append((
+                lambda t, name=name, offset=offset, width=width: v[name].at[:, units(t, offset, width)],
+                buf.at[:, pl.ds(offset, width)], 384, shared, False,
+            ))
 
     def base(i, c):
         return c * 192 if weights[i][4] else 0
@@ -374,55 +409,63 @@
         n = i * 3 + d - 1
         return remote(
             source(t).at[span(first, size - shared)], out.at[span(o * 384 + first, size - shared)],
-            send.at[n], recv.at[n], (replica, t),
+            v["send"].at[n], v["recv"].at[n], (replica, t),
         )
 
     def across(i, d, o, whose):
         _, out, size, shared, _ = weights[i]
         ref = out.at[span(o * 384 + base(i, core) + whose * (size - shared), shared)]
         n = i * 3 + d - 1
-        return remote(ref, ref, zsend.at[n], zrecv.at[n], pair)
+        return remote(ref, ref, v["zsend"].at[n], v["zrecv"].at[n], pair)
 
     def onward(i, d, o, c, shared_part):
         _, out, size, shared, _ = weights[i]
         first = o * 384 + base(i, c) + ((1 - odd) * (size - shared) if shared_part else odd * shared)
         ref = out.at[span(first, shared if shared_part else size - shared)]
         n = i * 3 + d - 1 + (6 if shared_part else 0)
-        return remote(ref, ref, fsend.at[n], frecv.at[n], mate)
-
-    def cot_hop(d, t, o):
-        return remote(cot, cot_all.at[block(o, core)], send.at[11 + d], recv.at[11 + d], (replica, t))
-
-    def cot_onward(d, o, c):
-        ref = cot_all.at[block(o, c)] if d else cot
-        return remote(ref, cot_all.at[block(o, c)], fsend.at[12 + d], frecv.at[12 + d], mate)
+        return remote(ref, ref, v["fsend"].at[n], v["frecv"].at[n], mate)
+
+    row_sets = (cot_all, n_all)
+
+    def row_hop(a, d, t, o):
+        n = 18 + a * 3 + d - 1
+        return remote(row_sets[a].at[tokens(shard, core)], row_sets[a].at[tokens(o, core)], v["send"].at[n], v["recv"].at[n],
+                      (replica, t))
+
+    def row_onward(a, d, o, c):
+        n = 12 + a * 4 + d
+        ref = row_sets[a].at[tokens(o, c)]
+        return remote(ref, ref, v["fsend"].at[n], v["frecv"].at[n], mate)
 
     def small_hop(d, t, o):
-        return remote(small, small_all.at[o], send.at[14 + d], recv.at[14 + d], (replica, t))
-
-    order = (3, 1, 2)
-    for d in order:
-        small_hop(d, peer_of(shard, d), shard).start()
-    for i in range(4):
-        if i == 2:
-            for d in order:
-                cot_hop(d, peer_of(shard, d), shard).start()
+        n = 24 + d - 1
+        return remote(v["small"], small_all.at[o], v["send"].at[n], v["recv"].at[n], (replica, t))
+
+    def send_rows(a):
+        for d in order:
+            row_hop(a, d, peer_of(shard, d), shard).start()
+        row_onward(a, 0, shard, core).start()
+
+    def take_rows(a):
+        for d in order:
+            p = peer_of(shard, d)
+            row_hop(a, d, p, p).wait_recv()
+            row_onward(a, d, p, core).start()
+
+    def have_rows(a):
+        for d in (0,) + order:
+            row_onward(a, d, peer_of(shard, d), other).wait_recv()
+
+    def send_weight(i):
         for d in order:
             hop(i, d, peer_of(shard, d), shard).start()
-    cot_onward(0, shard, core).start()
-    for n, (src, buf, _) in enumerate(loads):
-        pltpu.make_async_copy(src, buf, local.at[n]).start()
-    for n, (src, buf, dst) in enumerate(loads):
-        pltpu.make_async_copy(src, buf, local.at[n]).wait()
-        pltpu.make_async_copy(buf, dst, local.at[n]).start()
-
-    def take(i):
-        for d in order:
-            p = peer_of(shard, d)
-            hop(i, d, p, p).wait_recv()
-            across(i, d, p, odd).start()
-            if weights[i][4]:
-                onward(i, d, p, core, False).start()
+
+    def take(i, d):
+        p = peer_of(shard, d)
+        hop(i, d, p, p).wait_recv()
+        across(i, d, p, odd).start()
+        if weights[i][4]:
+            onward(i, d, p, core, False).start()
 
     def take_shared(i):
         for d in order:
@@ -431,131 +474,320 @@
             if weights[i][4]:
                 onward(i, d, p, core, True).start()
 
-    take(0)
-    take(1)
+    def have_other_half(i):
+        for d in order:
+            for part in (False, True):
+                onward(i, d, peer_of(shard, d), other, part).wait_recv()
+
+    rows = span(shard * 384, 384)
+    loads = [
+        pltpu.make_async_copy(v["cot"], cot_all.at[tokens(shard, core)], v["local"].at[0]),
+        pltpu.make_async_copy(v["wq"], q_buf.at[rows], v["local"].at[1]),
+        pltpu.make_async_copy(v["wo"], o_buf.at[rows], v["local"].at[2]),
+        pltpu.make_async_copy(v["wg"].at[:, units(shard, 0, WINDOW)], g_buf.at[rows], v["local"].at[3]),
+        pltpu.make_async_copy(v["wu"].at[:, units(shard, 0, WINDOW)], u_buf.at[rows], v["local"].at[4]),
+    ]
+    odd_chip = lax.rem(shard, 2)
+    inside = odd_chip == core
+    loads.append(pltpu.make_async_copy(
+        v["wd"].at[span((1152 - 64 * odd_chip) * core, 1088)],
+        d_buf.at[span(odd_chip * (1 - core) * 64, 1088)], v["local"].at[5],
+    ))
+
     for d in order:
-        p = peer_of(shard, d)
-        cot_hop(d, p, p).wait_recv()
-        cot_onward(d, p, core).start()
-    take_shared(0)
-    take_shared(1)
-    take(2)
-    take(3)
-    take_shared(2)
-    take_shared(3)
+        small_hop(d, peer_of(shard, d), shard).start()
+    send_weight(0)
+    send_weight(1)
+    for copy in loads:
+        copy.start()
+    rest = pltpu.make_async_copy(
+        v["wd"].at[span((2176 - 1088) * core + 1088, 64)], d_buf.at[pl.ds(1088, 64)], v["local"].at[6]
+    )
+
+    @pl.when(inside)
+    def _():
+        rest.start()
+
+    @pl.when(~inside)
+    def _():
+        d_buf[span(1088 - 1088 * odd_chip, 64), :] = jnp.zeros((64, 1536), bf16)
+
+    loads[0].wait()
+    send_rows(0)
+    send_weight(2)
+    send_weight(3)
+
+    small_all[shard] = v["small"][...]
     for d in order:
         p = peer_of(shard, d)
         small_hop(d, p, p).wait_recv()
-        small_hop(d, p, shard).wait_send()
-        cot_hop(d, p, shard).wait_send()
-        cot_onward(d, p, core).wait_send()
-        cot_onward(d, p, other).wait_recv()
-        for i in range(4):
+
+    def gathered(row, width):
+        return jnp.concatenate([small_all[s, row : row + 1, 0:width].astype(f32) for s in range(4)], axis=1)
+
+    gain_one = gathered(0, 384)
+
+    def norm_body(at, carry):
+        x = v["x"][at, :].astype(f32)
+        inv = lax.rsqrt(jnp.mean(x * x, axis=-1, keepdims=True) + NORM_EPS)
+        v["nrm"][at, :] = (x * inv * gain_one).astype(bf16)
+        return carry
+
+    row_loop(128, 16, norm_body, 0)
+    for copy in loads[1:]:
+        copy.wait()
+
+    @pl.when(inside)
+    def _():
+        rest.wait()
+
+    for i in (0, 1):
+        for d in order:
+            take(i, d)
+    take_shared(0)
+    have_other_half(0)
+    keep_q = pltpu.make_async_copy(q_buf, v["q_full"], v["local"].at[7])
+    keep_q.start()
+    bias = gathered(1, 512)
+
+    def rotated(x):
+        return x * v["cos"][...] + pltpu.roll(x, HD // 2, 1) * v["sin"][...]
+
+    def project(head, out, at, turn):
+        cols = slice(head * HD, (head + 1) * HD)
+        x = v["prj"][:, cols] + bias[:, cols]
+        out[:, at * HD : (at + 1) * HD] = (rotated(x) if turn else x).astype(bf16)
+
+    for n in range(4):
+        v["prj"][:, n * 512 : (n + 1) * 512] = jnp.dot(
+            v["nrm"][...], q_buf[:, n * 512 : (n + 1) * 512], preferred_element_type=f32
+        )
+    take_shared(1)
+    for h in range(HEADS):
+        project(h, v["qry"], h, True)
+    for g in range(KV):
+        project(HEADS + g, v["key"], g, True)
+        project(HEADS + KV + g, v["val"], g, False)
+    causal = lax.broadcasted_iota(jnp.int32, (128, 128), 0) >= lax.broadcasted_iota(jnp.int32, (128, 128), 1)
+    v["lse"][...] = jnp.zeros((128, HD), f32)
+    for h in range(HEADS):
+        g = h // (HEADS // KV)
+        at = slice(h * HD, (h + 1) * HD)
+        scores = dot_nt(v["qry"][:, at], v["key"][:, g * HD : (g + 1) * HD]) * SCORE_SCALE
+        scores = jnp.where(causal, scores, -1e30)
+        row_max = jnp.max(scores, axis=-1, keepdims=True)
+        logsum = row_max + jnp.log(jnp.sum(jnp.exp(scores - row_max), axis=-1, keepdims=True))
+        v["lse"][:, h : h + 1] = logsum
+        probs = jnp.exp(scores - logsum).astype(bf16)
+        v["ctx"][:, at] = jnp.dot(probs, v["val"][:, g * HD : (g + 1) * HD], preferred_element_type=f32).astype(bf16)
+    have_other_half(1)
+    keep_o = pltpu.make_async_copy(o_buf, v["o_full"], v["local"].at[8])
+    keep_o.start()
+    for n in range(3):
+        cols = slice(n * 512, (n + 1) * 512)
+        v["hidden"][:, cols] = v["x"][:, cols].astype(f32) + jnp.dot(
+            v["ctx"][...], o_buf[:, cols], preferred_element_type=f32
+        )
+    gain_two = gathered(2, 384)
+    v["gains"][0:1, :] = gain_one
+    v["gains"][1:2, :] = gain_two
+
+    def norm_two(j, carry):
+        at = pl.ds(pl.multiple_of(j * 16, 16), 16)
+        hidden = v["hidden"][at, :]
+        inv = lax.rsqrt(jnp.mean(hidden * hidden, axis=-1, keepdims=True) + NORM_EPS)
+        n_all[span((core * 4 + shard) * 128 + j * 16, 16), :] = (hidden * inv * gain_two).astype(bf16)
+        return carry
+
+    lax.fori_loop(0, 8, norm_two, 0)
+    send_rows(1)
+    send_weight(4)
+    send_weight(5)
+    take_rows(0)
+    for i in (2, 3):
+        for d in order:
+            take(i, d)
+    take_rows(1)
+    take_shared(2)
+    take_shared(3)
+    have_rows(0)
+    have_rows(1)
+
+    act, gate_delta, up_delta = v["act"], v["gd"], v["ud"]
+    gs, us, gr = v["gs"], v["us"], v["gr"]
+    pending = [(i, d) for i in (4, 5) for d in order]
+
+    def service():
+        if pending:
+            take(*pending.pop(0))
+
+    def products(offset, width, m):
+        at = pl.ds(m * 512, 512)
+        for n in range(0, width, 256):
+            size = min(256, width - n)
+            cols = pl.ds(offset + n, size)
+            gs[:, n : n + size] = jnp.dot(n_all[at, :], g_buf[:, cols], preferred_element_type=f32)
+            us[:, n : n + size] = jnp.dot(n_all[at, :], u_buf[:, cols], preferred_element_type=f32)
+            gr[:, n : n + size] = dot_nt(cot_all[at, :], d_buf[cols, :])
+        column = first_unit + offset + lax.broadcasted_iota(jnp.int32, (1, width), 1)
+        owned = (column >= shard * 2240) & (column < (shard + 1) * 2240)
+
+        def body(j, carry):
+            part = pl.ds(pl.multiple_of(j * 16, 16), 16)
+            to = pl.ds(pl.multiple_of(m * 512 + j * 16, 16), 16)
+            cols = pl.ds(offset, width)
+            gate, up, grad = gs[part, 0:width], us[part, 0:width], gr[part, 0:width]
+            sig = jax.nn.sigmoid(gate)
+            silu = gate * sig
+            act[to, cols] = jnp.where(owned, silu * up, 0.0).astype(bf16)
+            gate_delta[to, cols] = jnp.where(owned, grad * up * sig * (1.0 + gate * (1.0 - sig)), 0.0).astype(bf16)
+            up_delta[to, cols] = jnp.where(owned, grad * silu, 0.0).astype(bf16)
+            return carry
+
+        lax.fori_loop(0, 32, body, 0)
+
+    def transpose(src, cols, dst):
+        def body(j, carry):
+            at = pl.ds(pl.multiple_of(j * 128, 128), 128)
+            dst[:, at] = src[at, cols].T
+            return carry
+
+        lax.fori_loop(0, 8, body, 0)
+
+    outs = {}
+
+    def write(name, buf, at, cols=None):
+        n = 9 + len(outs)
+        src = buf.at[at] if cols is None else buf.at[at, cols]
+        dst = v[name].at[at] if cols is None else v[name].at[at, cols]
+        copy = pltpu.make_async_copy(src, dst, v["local"].at[n])
+        copy.start()
+        outs[n] = copy
+
+    for tile, (offset, width, _) in enumerate(TILES):
+        cols = pl.ds(offset, width)
+        for m in range(2):
+            products(offset, width, m)
+            service()
+        transpose(act, cols, v["act_t"].at[pl.ds(0, width)])
+        if tile == 0:
+            transpose(n_all, pl.ds(0, 1536), v["n_t"])
+        service()
+        for n in range(3):
+            out = pl.ds(n * 512, 512)
+            v["d_grad"][cols, out] = (
+                jnp.dot(v["act_t"][0:width, :], cot_all[:, out], preferred_element_type=f32) * grad_scale
+            ).astype(bf16)
+        write("pd", v["d_grad"], cols)
+        service()
+        for delta, buf, name in ((gate_delta, v["g_grad"], "pg"), (up_delta, v["u_grad"], "pu")):
+            for m in range(3):
+                at = pl.ds(m * 512, 512)
+                buf[at, cols] = (
+                    jnp.dot(v["n_t"][at, :], delta[:, cols], preferred_element_type=f32) * grad_scale
+                ).astype(bf16)
+            write(name, buf, pl.ds(0, 1536), cols)
+            service()
+        while pending:
+            service()
+        if tile == 0:
+            take_shared(4)
+            take_shared(5)
+    keep_q.wait()
+    keep_o.wait()
+    for i in (0, 1):
+        for d in order:
+            p = peer_of(shard, d)
             hop(i, d, p, shard).wait_send()
             across(i, d, p, odd).wait_send()
-            if weights[i][4]:
-                for part in (False, True):
-                    onward(i, d, p, core, part).wait_send()
-                    onward(i, d, p, other, part).wait_recv()
-    cot_onward(0, shard, core).wait_send()
-    cot_onward(0, shard, other).wait_recv()
-    for n, (src, buf, dst) in enumerate(loads):
-        pltpu.make_async_copy(buf, dst, local.at[n]).wait()
-
-
-def any_spec():
-    return pl.BlockSpec(memory_space=pl.ANY)
-
-
-def vmem_spec():
-    return pl.BlockSpec(memory_space=pltpu.VMEM)
-
-
-def params(**more):
-    return pltpu.CompilerParams(has_side_effects=True, vmem_limit_bytes=VMEM_BYTES, **more)
-
-
-def front(wq, wo, wg, wu, cot, small):
+            for part in (False, True):
+                onward(i, d, p, core, part).wait_send()
+    for m in range(2):
+        at = pl.ds(m * 512, 512)
+        for n in range(3):
+            cols = pl.ds(n * 512, 512)
+            q_buf[at, cols] = (dot_nt(gate_delta[at, :], g_buf[cols, :]) + dot_nt(up_delta[at, :], u_buf[cols, :])).astype(bf16)
+        write("p_back", q_buf, at, pl.ds(0, 1536))
+    for m in range(2):
+        at = pl.ds(m * 512, 512)
+        for n in range(3):
+            cols = pl.ds(n * 512, 512)
+            o_buf[at, cols] = jnp.dot(act[at, :], d_buf[:, cols], preferred_element_type=f32).astype(bf16)
+        write("p_out", o_buf, at)
+    for copy in outs.values():
+        copy.wait()
+    for d in order:
+        p = peer_of(shard, d)
+        small_hop(d, p, shard).wait_send()
+        for i in (2, 3, 4, 5):
+            hop(i, d, p, shard).wait_send()
+            across(i, d, p, odd).wait_send()
+        for a in range(2):
+            row_hop(a, d, p, shard).wait_send()
+    for a in range(2):
+        for d in (0,) + order:
+            row_onward(a, d, peer_of(shard, d), core).wait_send()
+
+
+def forward(grad_scale, **given):
     bf16 = jnp.bfloat16
-    shapes = [(1536, 2048), (1536, 1536), (1536, WINDOW), (1536, WINDOW), (1024, 1536), (4, 16, 512)]
-    bounce = [wq.shape, wo.shape, (384, WINDOW), (384, WINDOW), cot.shape, small.shape]
-    return pl.pallas_call(
-        front_kernel,
-        out_shape=[jax.ShapeDtypeStruct(s, bf16) for s in shapes],
-        in_specs=[any_spec()] * 6,
-        out_specs=[any_spec()] * 6,
-        scratch_shapes=[pltpu.VMEM(s, bf16) for s in bounce]
-        + [
-            pltpu.SemaphoreType.DMA((18,)),
-            pltpu.SemaphoreType.DMA((18,)),
-            pltpu.SemaphoreType.DMA((16,)),
-            pltpu.SemaphoreType.DMA((16,)),
-            pltpu.SemaphoreType.DMA((12,)),
-            pltpu.SemaphoreType.DMA((12,)),
-            pltpu.SemaphoreType.DMA((6,)),
-        ],
-        compiler_params=params(),
-    )(wq, wo, wg, wu, cot, small)
-
-
-def gather_kernel(x, out, send, recv, fsend, frecv, local):
-    replica, shard, core = place()
-    mate = (replica + 1 - 2 * core, shard)
-
-    def block(owner, c):
-        return out.at[pl.ds(pl.multiple_of((c * 4 + owner) * 128, 128), 128)]
-
-    for d in (3, 1, 2):
-        remote(x, block(shard, core), send.at[d], recv.at[d], (replica, peer_of(shard, d))).start()
-    remote(x, block(shard, core), fsend.at[0], frecv.at[0], mate).start()
-    own = pltpu.make_async_copy(x, block(shard, core), local)
-    own.start()
-    for d in (1, 2, 3):
-        p = peer_of(shard, d)
-        remote(x, block(p, core), send.at[d], recv.at[d], (replica, p)).wait_recv()
-        remote(block(p, core), block(p, core), fsend.at[d], frecv.at[d], mate).start()
-    own.wait()
-    for d in (1, 2, 3):
-        p = peer_of(shard, d)
-        remote(x, block(shard, core), send.at[d], recv.at[d], (replica, p)).wait_send()
-        remote(block(p, core), block(p, core), fsend.at[d], frecv.at[d], mate).wait_send()
-        remote(x, block(p, 1 - core), fsend.at[d], frecv.at[d], mate).wait_recv()
-    remote(x, block(shard, core), fsend.at[0], frecv.at[0], mate).wait_send()
-    remote(x, block(shard, 1 - core), fsend.at[0], frecv.at[0], mate).wait_recv()
-
-
-def plane_gather(x):
-    return pl.pallas_call(
-        gather_kernel,
-        out_shape=jax.ShapeDtypeStruct((x.shape[0] * 8, x.shape[1]), x.dtype),
-        in_specs=[vmem_spec()],
-        out_specs=vmem_spec(),
-        scratch_shapes=[pltpu.SemaphoreType.DMA((4,))] * 4 + [pltpu.SemaphoreType.DMA],
-        compiler_params=params(),
-    )(x)
-
-
-CHUNK = 128
-DOWN_CHUNKS = (64, 64) + (128,) * 8
-ATTENTION_CHUNKS = (64, 64, 64, 64, 32, 32, 32, 32)
-CHUNKS = len(DOWN_CHUNKS) + 24 + len(ATTENTION_CHUNKS)
-SCORE_SCALE = 1.0 / math.sqrt(HD)
-
-
-def row_spans(sizes):
-    return [pl.ds(sum(sizes[:k]), size) for k, size in enumerate(sizes)]
-
-
-def dot_nt(a, b):
-    return lax.dot_general(a, b, (((1,), (1,)), ((), ())), preferred_element_type=jnp.float32)
-
-
-def dot_tn(a, b):
-    return lax.dot_general(a, b, (((0,), (0,)), ((), ())), preferred_element_type=jnp.float32)
-
-
-def row_loop(rows, step, body, init):
-    return lax.fori_loop(0, rows // step, lambda j, c: body(pl.ds(pl.multiple_of(j * step, step), step), c), init)
+    f32 = jnp.float32
+    dma = pltpu.SemaphoreType.DMA
+    in_vmem = ("x", "small", "cos", "sin")
+    outs = {
+        "q_full": ((1536, 2048), bf16, any_spec()),
+        "o_full": ((1536, 1536), bf16, any_spec()),
+        "pd": ((WINDOW, 1536), bf16, any_spec()),
+        "pg": ((1536, WINDOW), bf16, any_spec()),
+        "pu": ((1536, WINDOW), bf16, any_spec()),
+        "p_back": ((1024, 1536), bf16, any_spec()),
+        "p_out": ((1024, 1536), bf16, any_spec()),
+        "hidden": ((128, 1536), f32, vmem_spec()),
+        "nrm": ((128, 1536), bf16, vmem_spec()),
+        "ctx": ((128, 1536), bf16, vmem_spec()),
+        "qry": ((128, 1536), bf16, vmem_spec()),
+        "key": ((128, KV * HD), bf16, vmem_spec()),
+        "val": ((128, KV * HD), bf16, vmem_spec()),
+        "lse": ((128, HD), f32, vmem_spec()),
+        "gains": ((8, 1536), f32, vmem_spec()),
+    }
+    scratch = {
+        "q_buf": pltpu.VMEM((1536, 2048), bf16),
+        "o_buf": pltpu.VMEM((1536, 1536), bf16),
+        "g_buf": pltpu.VMEM((1536, WINDOW), bf16),
+        "u_buf": pltpu.VMEM((1536, WINDOW), bf16),
+        "d_buf": pltpu.VMEM((WINDOW, 1536), bf16),
+        "n_all": pltpu.VMEM((1024, 1536), bf16),
+        "n_t": pltpu.VMEM((1536, 1024), bf16),
+        "cot_all": pltpu.VMEM((1024, 1536), bf16),
+        "small_all": pltpu.VMEM((4, 16, 512), bf16),
+        "prj": pltpu.VMEM((128, 2048), f32),
+        "act": pltpu.VMEM((1024, WINDOW), bf16),
+        "gd": pltpu.VMEM((1024, WINDOW), bf16),
+        "ud": pltpu.VMEM((1024, WINDOW), bf16),
+        "act_t": pltpu.VMEM((640, 1024), bf16),
+        "gs": pltpu.VMEM((512, 640), f32),
+        "us": pltpu.VMEM((512, 640), f32),
+        "gr": pltpu.VMEM((512, 640), f32),
+        "d_grad": pltpu.VMEM((WINDOW, 1536), bf16),
+        "g_grad": pltpu.VMEM((1536, WINDOW), bf16),
+        "u_grad": pltpu.VMEM((1536, WINDOW), bf16),
+        "send": dma((27,)),
+        "recv": dma((27,)),
+        "zsend": dma((18,)),
+        "zrecv": dma((18,)),
+        "fsend": dma((20,)),
+        "frecv": dma((20,)),
+        "local": dma((20,)),
+    }
+    return dict(zip(outs, pl.pallas_call(
+        functools.partial(forward_kernel, grad_scale, (*given, *outs, *scratch)),
+        out_shape=[jax.ShapeDtypeStruct(s, dt) for s, dt, _ in outs.values()],
+        in_specs=[vmem_spec() if name in in_vmem else any_spec() for name in given],
+        out_specs=[spec for _, _, spec in outs.values()],
+        scratch_shapes=list(scratch.values()),
+        compiler_params=pltpu.CompilerParams(has_side_effects=True, vmem_limit_bytes=67043328),
+    )(*given.values())))
 
 
 def backward_kernel(levels, grad_scale, names, *refs):
@@ -1153,85 +1385,51 @@
     cotangent,
 ):
     f32 = jnp.float32
-    bf16 = jnp.bfloat16
     tok_count = block_input.shape[0]
     levels = lax.axis_size("replica") // 2
     grad_scale = 1.0 / math.sqrt(tok_count * lax.axis_size("replica") * lax.axis_size("shard"))
-    q_width = HEADS * HD
-    k_end = q_width + KV * HD
-    replica, shard, core = place()
+    shard = lax.axis_index("shard")
     cosine, sine_table = rope_tables(tok_count)
-    small = jnp.zeros((16, 512), bf16)
+    small = jnp.zeros((16, 512), jnp.bfloat16)
     small = small.at[0, :384].set(attn_gain).at[1, :].set(qkv_bias).at[2, :384].set(mlp_gain)
-    qkv_full, out_full, gate_own, up_own, cot_all, small_all = front(
-        qkv_weight, out_weight, gate_weight, up_weight, cotangent, small
-    )
-    gain_one = small_all[:, 0, :384].reshape(-1).astype(f32)
-    bias = small_all[:, 1, :].reshape(-1).astype(f32)
-    gain_two = small_all[:, 2, :384].reshape(-1).astype(f32)
-
-    xfloat = block_input.astype(f32)
-    inv_one = lax.rsqrt(jnp.mean(xfloat * xfloat, axis=-1, keepdims=True) + NORM_EPS)
-    normed_one = (xfloat * inv_one * gain_one).astype(bf16)
-    projected = jnp.dot(normed_one, qkv_full, preferred_element_type=f32) + bias
-    queries = rotate(projected[:, :q_width].reshape(tok_count, HEADS, HD), cosine, sine_table).astype(bf16)
-    queries = queries.reshape(tok_count, KV, HEADS // KV, HD)
-    key_rot = rotate(projected[:, q_width:k_end].reshape(tok_count, KV, HD), cosine, sine_table).astype(bf16)
-    values = projected[:, k_end:].reshape(tok_count, KV, HD).astype(bf16)
-    context, logsum = attend_forward(queries, key_rot, values)
-    hidden_res = xfloat + jnp.dot(context, out_full, preferred_element_type=f32)
-    inv_two = lax.rsqrt(jnp.mean(hidden_res * hidden_res, axis=-1, keepdims=True) + NORM_EPS)
-    normed_two = (hidden_res * inv_two * gain_two).astype(bf16)
-
-    normed_all = plane_gather(normed_two)
-    first = window_start(shard, core)
-    column = first + jnp.arange(WINDOW)
-    owned = (column >= shard * 2240) & (column < (shard + 1) * 2240)
-    padded = jnp.pad(down_weight, ((64, 64), (0, 0)))
-    down_own = lax.dynamic_slice_in_dim(padded, first - shard * 2240 + 64, WINDOW, 0)
-    gate_pre = jnp.dot(normed_all, gate_own, preferred_element_type=f32)
-    up_pre = jnp.dot(normed_all, up_own, preferred_element_type=f32)
-    sigmoid_gate = jax.nn.sigmoid(gate_pre)
-    silu_gate = gate_pre * sigmoid_gate
-    act_grad = jnp.einsum("td,fd->tf", cot_all, down_own, preferred_element_type=f32)
-    activation = jnp.where(owned, silu_gate * up_pre, 0.0).astype(bf16)
-    gate_delta = jnp.where(
-        owned, act_grad * up_pre * sigmoid_gate * (1.0 + gate_pre * (1.0 - sigmoid_gate)), 0.0
-    ).astype(bf16)
-    up_delta = jnp.where(owned, act_grad * silu_gate, 0.0).astype(bf16)
-    down_out = jnp.dot(activation, down_own, preferred_element_type=f32).astype(bf16)
-    back = (
-        jnp.einsum("tf,df->td", gate_delta, gate_own, preferred_element_type=f32)
-        + jnp.einsum("tf,df->td", up_delta, up_own, preferred_element_type=f32)
-    ).astype(bf16)
-    gate_part = (jnp.einsum("td,tf->df", normed_all, gate_delta, preferred_element_type=f32) * grad_scale).astype(bf16)
-    up_part = (jnp.einsum("td,tf->df", normed_all, up_delta, preferred_element_type=f32) * grad_scale).astype(bf16)
-    down_part = (jnp.einsum("tf,td->fd", activation, cot_all, preferred_element_type=f32) * grad_scale).astype(bf16)
-
-    sums = logsum.reshape(HEADS, tok_count).T
+    twice = jnp.concatenate([cosine[:, 0], cosine[:, 0]], axis=1)
+    turn = jnp.concatenate([-sine_table[:, 0], sine_table[:, 0]], axis=1)
+    got = forward(
+        grad_scale,
+        x=block_input,
+        small=small,
+        cos=twice,
+        sin=turn,
+        wq=qkv_weight,
+        wo=out_weight,
+        wg=gate_weight,
+        wu=up_weight,
+        wd=down_weight,
+        cot=cotangent,
+    )
     sum_attn, sum_down, sum_gate, sum_up, block_output, input_grad, vectors = backward(
         levels,
         grad_scale,
-        pd=down_part,
-        pg=gate_part,
-        pu=up_part,
-        p_back=back,
-        p_out=down_out,
-        wo=out_full,
-        wq=qkv_full,
-        hidden=hidden_res,
+        pd=got["pd"],
+        pg=got["pg"],
+        pu=got["pu"],
+        p_back=got["p_back"],
+        p_out=got["p_out"],
+        wo=got["o_full"],
+        wq=got["q_full"],
+        hidden=got["hidden"],
         x=block_input,
         cot=cotangent,
-        gain_one=gain_one[None, :],
-        gain_two=gain_two[None, :],
-        ctx=context,
-        nrm=normed_one,
-        qry=queries.reshape(tok_count, q_width),
-        key=key_rot.reshape(tok_count, KV * HD),
-        val=values.reshape(tok_count, KV * HD),
-        lse=jnp.pad(sums, ((0, 0), (0, HD - HEADS))),
-        cos=jnp.concatenate([cosine[:, 0], cosine[:, 0]], axis=1),
-        sin=jnp.concatenate([sine_table[:, 0], -sine_table[:, 0]], axis=1),
+        gain_one=got["gains"][0:1],
+        gain_two=got["gains"][1:2],
+        ctx=got["ctx"],
+        nrm=got["nrm"],
+        qry=got["qry"],
+        key=got["key"],
+        val=got["val"],
+        lse=got["lse"],
+        cos=twice,
+        sin=-turn,
     )
     gain_one_own, bias_own, gain_two_own = vectors[0, :384], vectors[0, 384:896], vectors[0, 896:]
     qkv_grad = jnp.concatenate([sum_attn[0, :, :1024], sum_attn[1, :, :1024]], axis=1).astype(f32)

time: 627 us -> 557 us (0.89)
  matrix products: 66.7 us -> 0 us
  other arithmetic: 22.2 us -> 15 us
    dot_general x13 -> x0, matrix products: 66.7 us -> none  [the longest x1 10.1 us: fast_device(): jnp.einsum('td,fd->tf', cot_all, down_own, preferred_element_type=f32)]
    pallas_call x2 -> x1, Pallas kernels: 158 us -> 162 us  [forward(): pl.pallas_call(functools.partial(forward_kernel, grad_scale, (*given, *ou...]
where the time goes in v5:
time: 557 us; the launch traced here: 549 us
  Pallas kernels  522 us (94%)
  other arithmetic  15 us (3%)
  local copies, waits for them, and re-layouts  11.3 us (2%)
    pallas_call x1, Pallas kernels, backward(): pl.pallas_call(functools.partial(backward_kernel, levels, grad_scale, (*g...  344 us
    pallas_call x1, Pallas kernels, forward(): pl.pallas_call(functools.partial(forward_kernel, grad_scale, (*given, *ou...  162 us
    pallas_call x1, Pallas kernels, widen(): pl.pallas_call(widen_kernel, grid=(384 // rows,), out_shape=[jax.ShapeDty...  15.7 us

profile of v5, /device:TPU:0, one launch (start us, length us, event | category | flops | bytes accessed | tf_op | source)
XLA Modules:
  0.0 549.0 jit_solution(887043174733977466)
XLA Ops:
  0.7 0.3 fusion.2
  0.9 0.8 fusion.3
  1.7 0.7 reshape.113
  2.4 0.6 scatter.10
  3.0 0.7 reshape.114
  3.7 1.3 scatter.11
  5.0 0.7 reshape.115
  5.7 1.3 scatter.14.refs_1_
  7.0 161.9 %shard_map.177 = (bf16[1536,2048]{1,0:T(8,128)(2,1)}, bf16[1536,1536]{1,0:T(8,128)(2,1)}, bf16[1152,1536]{1,0:T(8,128)(2,1)}, bf16[1536,1152]{1,0:T(8,128)(2,1)}...) custom-call(bf16[128,1536]{1,0:T(8,128)(2,1)} %refs_8_.3, ...), custom_call_target="tpu_custom_call" | custom-call | tf_op jit(solution)/shard_map/pallas_call | solution.py:783
  168.8 1.5 fusion.4
  170.3 344.3 %shard_map.178 = (bf16[2,384,1792]{2,1,0:T(8,128)(2,1)}, bf16[2,1152,1536]{2,1,0:T(8,128)(2,1)}, bf16[2,4,384,1152]{3,2,1,0:T(8,128)(2,1)}, bf16[2,4,384,1152]{3...) custom-call(bf16[1152,1536]{1,0:T(8,128)(2,1)} %get-tuple-element.70.refs_0_, ...), custom_call_target="tpu_custom_call" | custom-call | tf_op jit(solution)/shard_map/pallas_call | solution.py:1341
  514.6 15.7 %shard_map.179 = (f32[384,8960]{1,0:T(8,128)}, f32[384,8960]{1,0:T(8,128)}) custom-call(bf16[2,4,384,1152]{3,2,1,0:T(8,128)(2,1)} %get-tuple-element.89.x_gate, bf16[2,4,384,1152]{3,2,1,0:T(8,128)(2,1)} %get-tuple-element.90.x_up), custom_call_target="tpu_custom_call" | custom-call | tf_op jit(solution)/shard_map/pallas_call | solution.py:1366
  530.3 0.0 copy-start
  530.3 10.2 %dynamic-slice_convert_fusion = f32[2240,1536]{1,0:T(8,128)} fusion(bf16[2304,1536]{1,0:T(8,128)(2,1)} %bitcast.10, s32[]{:T(128)S(6)} %select_n.3), kind=kLoop, calls=%fused_computation | loop fusion | flops 3440640 | bytes 20643844 | tf_op jit(solution)/shard_map/convert_element_type | solution.py:1439
  540.5 0.0 copy-done
  540.5 0.1 slice_bitcast_fusion.3
  540.6 1.7 maximum_convert_fusion.1
  542.3 0.2 slice_bitcast_fusion.1
  542.5 0.0 copy-start.2
  542.5 0.0 copy-start.1
  542.5 2.0 maximum_convert_fusion
  544.5 1.3 slice_reduce_fusion
  545.9 1.3 slice.82
  547.2 0.0 copy-done.2
  547.2 0.7 copy.24
  547.9 0.0 copy-done.1
  547.9 0.9 copy.25
  (1 shorter events, 0.0 us)
Async XLA Ops:
  530.3 10.2 %copy-start = (bf16[2,384,1792]{2,1,0:T(8,128)(2,1)S(1)}, bf16[2,384,1792]{2,1,0:T(8,128)(2,1)}, u32[]{:S(2)}) copy-start(bf16[2,384,1792]{2,1,0:T(8,128)(2,1)} %get-tuple-element.88) | copy-start | bytes 8257540
  542.5 4.7 copy-start.2
  542.5 5.4 copy-start.1

commit v6 on v5

--- a/solution.py
+++ b/solution.py
@@ -341,7 +341,7 @@
 
 
 CHUNK = 128
-DOWN_CHUNKS = (64, 64) + (128,) * 8
+DOWN_CHUNKS = (64, 64) + (128,) * 7 + (64, 64)
 ATTENTION_CHUNKS = (64, 64, 64, 64, 32, 32, 32, 32)
 CHUNKS = len(DOWN_CHUNKS) + 24 + len(ATTENTION_CHUNKS)
 SCORE_SCALE = 1.0 / math.sqrt(HD)
@@ -1079,9 +1079,15 @@
         own_a[at, 0:1024] = (dot_tn(v["nrm_all"][:, at], v["prj_all"][...]) * grad_scale).astype(bf16)
         own_a[at, 1024:1792] = (dot_tn(v["ctx_all"][:, at], v["hid_all"][...]) * grad_scale).astype(bf16)
 
+    odd_chip = lax.rem(shard, 2)
+
+    def down_rows(c, at):
+        first = odd_chip * (1088 * c - 64 * (1 - c)) + (1 - odd_chip) * 1152 * c
+        return pl.ds(pl.multiple_of(first + at.start, 64), at.size)
+
     chunks = []
     for at in row_spans(DOWN_CHUNKS):
-        chunks.append((own_d, v["low_d"], v["high_d"], at, ("fill", 1), lambda c, at=at: v["fd"].at[c, at]))
+        chunks.append((own_d, v["low_d"], v["high_d"], at, ("none",), lambda c, at=at: v["fd"].at[down_rows(c, at)]))
     for d in range(4):
         for a in range(2):
             for k in range(3):
@@ -1117,7 +1123,7 @@
 
     def add(k, *refs):
         own, _, _, at, _, _ = chunks[k]
-        step = 32
+        step = 16
 
         def body(j, carry):
             rows = pl.ds(pl.multiple_of(at.start + j * step, step), step)
@@ -1133,6 +1139,22 @@
         _, _, _, at, _, dst = chunks[k]
         pltpu.make_async_copy(ref.at[at], dst(core), v["out_sem"].at[k]).start()
         remote(ref.at[at], dst(core), v["mate_send"].at[k], v["mate_recv"].at[k], mate).start()
+
+    def guarded(stage, k):
+        if k == 0:
+            pl.when(1 - odd_chip + core > 0)(lambda: stage(k))
+        elif k == len(DOWN_CHUNKS) - 1:
+            pl.when(odd_chip + 1 - core > 0)(lambda: stage(k))
+        else:
+            stage(k)
+
+    def guarded_mate(stage, k):
+        if k == 0:
+            pl.when(1 - odd_chip + other > 0)(lambda: stage(k))
+        elif k == len(DOWN_CHUNKS) - 1:
+            pl.when(odd_chip + 1 - other > 0)(lambda: stage(k))
+        else:
+            stage(k)
 
     def root_of(k):
         return levels // 2 - 1 + k % 2
@@ -1228,40 +1250,41 @@
     for copy in fills[1:]:
         copy.start()
     load_out.start()
+    fills[1].wait()
     for a in range(2):
         own_narrow(a).start()
         onward(a, 0, columns(narrow[a][0], shard, 384), shard, core).start()
     beside = {
-        0: [stage_sums],
-        11: [stage_hidden],
-        12: [stage_context],
-        13: [functools.partial(stage_heads, 0, 0)],
-        14: [functools.partial(stage_heads, 0, 1), stage_relay],
-        15: [functools.partial(stage_heads, 0, 2)],
-        16: [functools.partial(stage_heads, 1, 0)],
-        17: [functools.partial(stage_heads, 1, 1)],
-        18: [functools.partial(stage_heads, 1, 2), stage_send_projected],
-        19: [functools.partial(stage_normed, 0)],
-        20: [functools.partial(stage_normed, 1)],
-        21: [stage_input],
-        22: [stage_vec],
-        25: [stage_vec_out],
-        29: [stage_output],
-        30: [stage_gathered, functools.partial(stage_attention_parts, 0)],
-        31: [functools.partial(stage_attention_parts, 1)],
-        32: [functools.partial(stage_attention_parts, 2)],
+        2: [stage_sums],
+        12: [stage_hidden],
+        13: [stage_context],
+        14: [functools.partial(stage_heads, 0, 0)],
+        15: [functools.partial(stage_heads, 0, 1), stage_relay],
+        16: [functools.partial(stage_heads, 0, 2)],
+        17: [functools.partial(stage_heads, 1, 0)],
+        18: [functools.partial(stage_heads, 1, 1)],
+        19: [functools.partial(stage_heads, 1, 2), stage_send_projected],
+        20: [functools.partial(stage_normed, 0)],
+        21: [functools.partial(stage_normed, 1)],
+        22: [stage_input],
+        32: [stage_gathered, functools.partial(stage_attention_parts, 0)],
+        33: [functools.partial(stage_attention_parts, 1)],
+        34: [functools.partial(stage_attention_parts, 2)],
+        36: [stage_vec],
+        total + 8: [stage_vec_out],
+        total + 10: [stage_output],
     }
     stages = ((end_gather, 0), (gather_step, 6), (root_step, 10), (spread_step, 14), (end_spread, 20))
     for t in range(total + stages[-1][1]):
         for stage, lag in stages:
             if 0 <= t - lag < total:
-                stage(t - lag)
+                guarded(stage, t - lag)
         for stage in beside.get(t, ()):
             stage()
     for a in range(2):
         for d in (1, 2, 3):
             exchange(a, d, peer_of(shard, d)).wait_send()
-    for k in range(total):
+    def close(k):
         own, low, high, at, _, dst = chunks[k]
 
         @pl.when(level < levels - 1)
@@ -1274,7 +1297,14 @@
 
         pltpu.make_async_copy(own.at[at], dst(core), v["out_sem"].at[k]).wait()
         remote(own.at[at], dst(core), v["mate_send"].at[k], v["mate_recv"].at[k], mate).wait_send()
-        remote(own.at[at], dst(1 - core), v["mate_send"].at[k], v["mate_recv"].at[k], mate).wait_recv()
+
+    def close_mate(k):
+        own, low, high, at, _, dst = chunks[k]
+        remote(own.at[at], dst(other), v["mate_send"].at[k], v["mate_recv"].at[k], mate).wait_recv()
+
+    for k in range(total):
+        guarded(close, k)
+        guarded_mate(close_mate, k)
     for a in range(2):
         for d in (0, 1, 2, 3):
             p = peer_of(shard, d)
@@ -1298,7 +1328,7 @@
     in_hbm = ("pd", "pg", "pu", "p_back", "p_out", "wo", "wq")
     outs = {
         "fa": ((2, 384, 1792), bf16, any_spec()),
-        "fd": ((2, WINDOW, 1536), bf16, any_spec()),
+        "fd": ((2240, 1536), bf16, any_spec()),
         "fg": ((2, 4, 384, WINDOW), bf16, any_spec()),
         "fu": ((2, 4, 384, WINDOW), bf16, any_spec()),
         "block_out": ((128, 1536), bf16, vmem_spec()),
@@ -1348,9 +1378,9 @@
     )(*given.values())
 
 
-def widen_kernel(x_gate, x_up, out_gate, out_up):
+def widen_kernel(gate, up, down, attn, out_gate, out_up, out_down, out_qkv, out_out):
     f32 = jnp.float32
-    for x, out in ((x_gate, out_gate), (x_up, out_up)):
+    for x, out in ((gate, out_gate), (up, out_up)):
         for s in range(4):
             for c in range(2):
                 first = (s * 35) // 2 + c * 9
@@ -1359,16 +1389,33 @@
         for s in (1, 3):
             first = (s * 35) // 2
             out[:, first * 128 : (first + 1) * 128] = x[1, s - 1][:, 1024:].astype(f32) + x[0, s][:, :128].astype(f32)
+    out_down[...] = down[...].astype(f32)
+    for c in range(2):
+        out_qkv[:, c * 1024 : (c + 1) * 1024] = attn[c][:, :1024].astype(f32)
+        out_out[:, c * 768 : (c + 1) * 768] = attn[c][:, 1024:].astype(f32)
 
 
 def widen(*sums):
     rows = 32
+    f32 = jnp.float32
+    blocks = pl.BlockSpec((2, 4, rows, WINDOW), lambda i: (0, 0, i, 0))
+    down = pl.BlockSpec((224, 1536), lambda i: (jnp.minimum(i, 9), 0))
+
+    def whole(width):
+        return pl.BlockSpec((rows, width), lambda i: (i, 0))
+
     return pl.pallas_call(
         widen_kernel,
         grid=(384 // rows,),
-        out_shape=[jax.ShapeDtypeStruct((384, 8960), jnp.float32)] * 2,
-        in_specs=[pl.BlockSpec((2, 4, rows, WINDOW), lambda i: (0, 0, i, 0))] * 2,
-        out_specs=[pl.BlockSpec((rows, 8960), lambda i: (i, 0))] * 2,
+        out_shape=[
+            jax.ShapeDtypeStruct((384, 8960), f32),
+            jax.ShapeDtypeStruct((384, 8960), f32),
+            jax.ShapeDtypeStruct((2240, 1536), f32),
+            jax.ShapeDtypeStruct((384, 2048), f32),
+            jax.ShapeDtypeStruct((384, 1536), f32),
+        ],
+        in_specs=[blocks, blocks, down, pl.BlockSpec((2, rows, 1792), lambda i: (0, i, 0))],
+        out_specs=[whole(8960), whole(8960), down, whole(2048), whole(1536)],
     )(*sums)
 
 
@@ -1388,10 +1435,9 @@
     tok_count = block_input.shape[0]
     levels = lax.axis_size("replica") // 2
     grad_scale = 1.0 / math.sqrt(tok_count * lax.axis_size("replica") * lax.axis_size("shard"))
-    shard = lax.axis_index("shard")
     cosine, sine_table = rope_tables(tok_count)
-    small = jnp.zeros((16, 512), jnp.bfloat16)
-    small = small.at[0, :384].set(attn_gain).at[1, :].set(qkv_bias).at[2, :384].set(mlp_gain)
+    small = jnp.stack([jnp.pad(attn_gain, (0, 128)), qkv_bias, jnp.pad(mlp_gain, (0, 128))])
+    small = jnp.pad(small, ((0, 13), (0, 0)))
     twice = jnp.concatenate([cosine[:, 0], cosine[:, 0]], axis=1)
     turn = jnp.concatenate([-sine_table[:, 0], sine_table[:, 0]], axis=1)
     got = forward(
@@ -1432,12 +1478,7 @@
         sin=-turn,
     )
     gain_one_own, bias_own, gain_two_own = vectors[0, :384], vectors[0, 384:896], vectors[0, 896:]
-    qkv_grad = jnp.concatenate([sum_attn[0, :, :1024], sum_attn[1, :, :1024]], axis=1).astype(f32)
-    out_grad = jnp.concatenate([sum_attn[0, :, 1024:], sum_attn[1, :, 1024:]], axis=1).astype(f32)
-    down_grad = lax.dynamic_slice_in_dim(
-        sum_down.reshape(2 * WINDOW, 1536), lax.rem(shard, 2) * 64, 2240, 0
-    ).astype(f32)
-    gate_grad, up_grad = widen(sum_gate, sum_up)
+    gate_grad, up_grad, down_grad, qkv_grad, out_grad = widen(sum_gate, sum_up, sum_down, sum_attn)
     return (
         block_output,
         input_grad,

time: 557 us -> 538 us (0.966)
  other arithmetic: 15 us -> 1.65 us
    pallas_call x1, Pallas kernels: 344 us -> 330 us  [backward(): pl.pallas_call(functools.partial(backward_kernel, levels, grad_scale, (*g...]
    convert_element_type x3 -> x0, other arithmetic: 14 us -> none  [the longest x1 10.2 us: fast_device(): down_grad = lax.dynamic_slice_in_dim(sum_down.reshape(2 * WINDOW, 1536),...]
    pallas_call x1, Pallas kernels: 15.7 us -> 25.3 us  [widen(): pl.pallas_call(widen_kernel, grid=(384 // rows,), out_shape=[jax.ShapeDty...]
where the time goes in v6:
time: 538 us; the launch traced here: 527 us
  Pallas kernels  517 us (96%)
  local copies, waits for them, and re-layouts  7.8 us (1%)
    pallas_call x1, Pallas kernels, backward(): pl.pallas_call(functools.partial(backward_kernel, levels, grad_scale, (*g...  330 us
    pallas_call x1, Pallas kernels, forward(): pl.pallas_call(functools.partial(forward_kernel, grad_scale, (*given, *ou...  162 us
    pallas_call x1, Pallas kernels, widen(): pl.pallas_call(widen_kernel, grid=(384 // rows,), out_shape=[jax.ShapeDty...  25.3 us

profile of v6, /device:TPU:0, one launch (start us, length us, event | category | flops | bytes accessed | tf_op | source)
XLA Modules:
  0.0 527.2 jit_solution(2660097065546793246)
XLA Ops:
  0.7 0.7 pad.11
  1.4 0.7 pad.12
  2.0 0.7 stack.13
  2.7 0.6 fusion.7.refs_1_
  3.3 0.3 fusion.5
  3.6 0.8 fusion.8
  4.4 161.7 %shard_map.177 = (bf16[1536,2048]{1,0:T(8,128)(2,1)}, bf16[1536,1536]{1,0:T(8,128)(2,1)}, bf16[1152,1536]{1,0:T(8,128)(2,1)}, bf16[1536,1152]{1,0:T(8,128)(2,1)}...) custom-call(bf16[128,1536]{1,0:T(8,128)(2,1)} %refs_8_.3, ...), custom_call_target="tpu_custom_call" | custom-call | tf_op jit(solution)/shard_map/pallas_call | solution.py:783
  166.1 1.5 fusion.9
  167.6 329.7 %shard_map.178 = (bf16[2,384,1792]{2,1,0:T(8,128)(2,1)}, bf16[2240,1536]{1,0:T(8,128)(2,1)}, bf16[2,4,384,1152]{3,2,1,0:T(8,128)(2,1)}, bf16[2,4,384,1152]{3,2,1...) custom-call(bf16[1152,1536]{1,0:T(8,128)(2,1)} %get-tuple-element.37.refs_0_, ...), custom_call_target="tpu_custom_call" | custom-call | tf_op jit(solution)/shard_map/pallas_call | solution.py:1371
  497.3 1.3 slice.18
  498.6 1.3 slice_reduce_fusion
  499.9 0.0 copy-start.1
  499.9 0.0 copy-start
  499.9 25.3 %shard_map.179 = (f32[384,8960]{1,0:T(8,128)}, f32[384,8960]{1,0:T(8,128)}, f32[2240,1536]{1,0:T(8,128)}, f32[384,2048]{1,0:T(8,128)}, f32[384,1536]{1,0:T(8,128)}) custom-call(bf16[2,4,384,1152]{3,2,1,0:T(8,128)(2,1)} %get-tuple-element.55.gate, bf16[2,4,384,1152]{3,2,1,0:T(8,128)(2,1)} %get-tuple-element.56.up, bf16[2240,1536]{1,0:T(8,128)(2,1)} %get-tuple-element.57.down, ...), custom_call_target="tpu_custom_call" | custom-call | tf_op jit(solution)/shard_map/pallas_call | solution.py:1407
  525.2 0.0 copy-done.1
  525.2 0.7 copy.22
  525.9 0.0 copy-done
  525.9 0.9 copy.23
  (3 shorter events, 0.0 us)
Async XLA Ops:
  499.9 25.3 %copy-start.1 = (bf16[128,1536]{1,0:T(8,128)(2,1)S(1)}, bf16[128,1536]{1,0:T(8,128)(2,1)}, u32[]{:S(2)}) copy-start(bf16[128,1536]{1,0:T(8,128)(2,1)} %get-tuple-element.84) | copy-start | bytes 1179652
  499.9 26.0 %copy-start = (f32[128,1536]{1,0:T(8,128)S(1)}, f32[128,1536]{1,0:T(8,128)}, u32[]{:S(2)}) copy-start(f32[128,1536]{1,0:T(8,128)} %get-tuple-element.85) | copy-start | bytes 2359300

commit v7 on v6

--- a/solution.py
+++ b/solution.py
@@ -340,15 +340,9 @@
     return pltpu.CompilerParams(has_side_effects=True, vmem_limit_bytes=VMEM_BYTES, **more)
 
 
-CHUNK = 128
-DOWN_CHUNKS = (64, 64) + (128,) * 7 + (64, 64)
-ATTENTION_CHUNKS = (64, 64, 64, 64, 32, 32, 32, 32)
-CHUNKS = len(DOWN_CHUNKS) + 24 + len(ATTENTION_CHUNKS)
+DOWN_STEPS, GATE_STEPS, ATTENTION_STEPS = 18, 48, 12
+CHUNKS = DOWN_STEPS + GATE_STEPS + ATTENTION_STEPS
 SCORE_SCALE = 1.0 / math.sqrt(HD)
-
-
-def row_spans(sizes):
-    return [pl.ds(sum(sizes[:k]), size) for k, size in enumerate(sizes)]
 
 
 def dot_nt(a, b):
@@ -613,7 +607,7 @@
     have_rows(0)
     have_rows(1)
 
-    act, gate_delta, up_delta = v["act"], v["gd"], v["ud"]
+    act, gate_delta, up_delta = v["act_buf"], v["gd_buf"], v["ud_buf"]
     gs, us, gr = v["gs"], v["us"], v["gr"]
     pending = [(i, d) for i in (4, 5) for d in order]
 
@@ -671,7 +665,7 @@
             service()
         transpose(act, cols, v["act_t"].at[pl.ds(0, width)])
         if tile == 0:
-            transpose(n_all, pl.ds(0, 1536), v["n_t"])
+            transpose(n_all, pl.ds(0, 1536), v["n_t_buf"])
         service()
         for n in range(3):
             out = pl.ds(n * 512, 512)
@@ -680,19 +674,17 @@
             ).astype(bf16)
         write("pd", v["d_grad"], cols)
         service()
-        for delta, buf, name in ((gate_delta, v["g_grad"], "pg"), (up_delta, v["u_grad"], "pu")):
-            for m in range(3):
-                at = pl.ds(m * 512, 512)
-                buf[at, cols] = (
-                    jnp.dot(v["n_t"][at, :], delta[:, cols], preferred_element_type=f32) * grad_scale
-                ).astype(bf16)
-            write(name, buf, pl.ds(0, 1536), cols)
-            service()
+        for name, buf in (("act", act), ("gd", gate_delta), ("ud", up_delta)):
+            write(name, buf, pl.ds(0, 1024), cols)
         while pending:
             service()
         if tile == 0:
+            write("n_t", v["n_t_buf"], pl.ds(0, 1536))
             take_shared(4)
             take_shared(5)
+            write("w_g", g_buf, pl.ds(0, 1536))
+            write("w_u", u_buf, pl.ds(0, 1536))
+            write("w_d", d_buf, pl.ds(0, WINDOW))
     keep_q.wait()
     keep_o.wait()
     for i in (0, 1):
@@ -702,18 +694,6 @@
             across(i, d, p, odd).wait_send()
             for part in (False, True):
                 onward(i, d, p, core, part).wait_send()
-    for m in range(2):
-        at = pl.ds(m * 512, 512)
-        for n in range(3):
-            cols = pl.ds(n * 512, 512)
-            q_buf[at, cols] = (dot_nt(gate_delta[at, :], g_buf[cols, :]) + dot_nt(up_delta[at, :], u_buf[cols, :])).astype(bf16)
-        write("p_back", q_buf, at, pl.ds(0, 1536))
-    for m in range(2):
-        at = pl.ds(m * 512, 512)
-        for n in range(3):
-            cols = pl.ds(n * 512, 512)
-            o_buf[at, cols] = jnp.dot(act[at, :], d_buf[:, cols], preferred_element_type=f32).astype(bf16)
-        write("p_out", o_buf, at)
     for copy in outs.values():
         copy.wait()
     for d in order:
@@ -738,10 +718,13 @@
         "q_full": ((1536, 2048), bf16, any_spec()),
         "o_full": ((1536, 1536), bf16, any_spec()),
         "pd": ((WINDOW, 1536), bf16, any_spec()),
-        "pg": ((1536, WINDOW), bf16, any_spec()),
-        "pu": ((1536, WINDOW), bf16, any_spec()),
-        "p_back": ((1024, 1536), bf16, any_spec()),
-        "p_out": ((1024, 1536), bf16, any_spec()),
+        "act": ((1024, WINDOW), bf16, any_spec()),
+        "gd": ((1024, WINDOW), bf16, any_spec()),
+        "ud": ((1024, WINDOW), bf16, any_spec()),
+        "n_t": ((1536, 1024), bf16, any_spec()),
+        "w_g": ((1536, WINDOW), bf16, any_spec()),
+        "w_u": ((1536, WINDOW), bf16, any_spec()),
+        "w_d": ((WINDOW, 1536), bf16, any_spec()),
         "hidden": ((128, 1536), f32, vmem_spec()),
         "nrm": ((128, 1536), bf16, vmem_spec()),
         "ctx": ((128, 1536), bf16, vmem_spec()),
@@ -758,27 +741,25 @@
         "u_buf": pltpu.VMEM((1536, WINDOW), bf16),
         "d_buf": pltpu.VMEM((WINDOW, 1536), bf16),
         "n_all": pltpu.VMEM((1024, 1536), bf16),
-        "n_t": pltpu.VMEM((1536, 1024), bf16),
         "cot_all": pltpu.VMEM((1024, 1536), bf16),
         "small_all": pltpu.VMEM((4, 16, 512), bf16),
         "prj": pltpu.VMEM((128, 2048), f32),
-        "act": pltpu.VMEM((1024, WINDOW), bf16),
-        "gd": pltpu.VMEM((1024, WINDOW), bf16),
-        "ud": pltpu.VMEM((1024, WINDOW), bf16),
+        "act_buf": pltpu.VMEM((1024, WINDOW), bf16),
+        "gd_buf": pltpu.VMEM((1024, WINDOW), bf16),
+        "ud_buf": pltpu.VMEM((1024, WINDOW), bf16),
+        "n_t_buf": pltpu.VMEM((1536, 1024), bf16),
         "act_t": pltpu.VMEM((640, 1024), bf16),
         "gs": pltpu.VMEM((512, 640), f32),
         "us": pltpu.VMEM((512, 640), f32),
         "gr": pltpu.VMEM((512, 640), f32),
         "d_grad": pltpu.VMEM((WINDOW, 1536), bf16),
-        "g_grad": pltpu.VMEM((1536, WINDOW), bf16),
-        "u_grad": pltpu.VMEM((1536, WINDOW), bf16),
         "send": dma((27,)),
         "recv": dma((27,)),
         "zsend": dma((18,)),
         "zrecv": dma((18,)),
         "fsend": dma((20,)),
         "frecv": dma((20,)),
-        "local": dma((20,)),
+        "local": dma((24,)),
     }
     return dict(zip(outs, pl.pallas_call(
         functools.partial(forward_kernel, grad_scale, (*given, *outs, *scratch)),
@@ -801,52 +782,107 @@
     bf16 = jnp.bfloat16
     order = (3, 1, 2)
     own_a, own_d, own_g = v["own_a"], v["own_d"], v["own_g"]
-    sources = (v["pg"], v["pu"])
+    mat, act, wbuf, back, out = v["mat"], v["act_buf"], v["wbuf"], v["back"], v["out"]
+    odd_chip = lax.rem(shard, 2)
 
     def tokens(owner, c):
         return pl.ds(pl.multiple_of((c * 4 + owner) * 128, 128), 128)
 
-    def exchange(a, d, p):
-        rows = pl.ds(pl.multiple_of(p * 384, 384), 384)
+    def chip_at(d):
+        across = lax.rem(lax.rem(shard, 2) + lax.rem(d, 2), 2)
+        return lax.rem(shard // 2 + d // 2, 2) * 2 + across
+
+    def exchange(block, chip):
+        return remote(
+            v["blocks"].at[block - 2], own_g.at[pl.ds(pl.multiple_of(block * 384, 384), 384)],
+            v["xsend"].at[block], v["xrecv"].at[block], (replica, chip),
+        )
+
+    load_down = pltpu.make_async_copy(v["pd"], own_d, v["in_sem"].at[0])
+    load_normed = pltpu.make_async_copy(v["n_t"], wbuf.at[:, pl.ds(0, 1024)], v["in_sem"].at[1])
+    load_gate = pltpu.make_async_copy(v["w_g"], wbuf.at[:, pl.ds(WINDOW, WINDOW)], v["in_sem"].at[2])
+    load_up = pltpu.make_async_copy(v["w_u"], wbuf.at[:, pl.ds(0, WINDOW)], v["in_sem"].at[3])
+    load_wd = pltpu.make_async_copy(v["w_d"], wbuf.at[pl.ds(0, WINDOW), pl.ds(0, 1536)], v["in_sem"].at[4])
+    load_deltas = [
+        pltpu.make_async_copy(v["gd"], mat.at[0], v["in_sem"].at[5]),
+        pltpu.make_async_copy(v["ud"], mat.at[1], v["in_sem"].at[6]),
+    ]
+    load_act = pltpu.make_async_copy(v["act"], act, v["in_sem"].at[7])
+
+    def staged(block):
+        slot = lax.rem(block, 2)
+        return pltpu.make_async_copy(
+            back.at[pl.ds(pl.multiple_of(slot * 384, 384), 384), pl.ds(0, WINDOW)], v["blocks"].at[block - 2],
+            v["stage_sem"].at[slot],
+        )
+
+    def stage_gradient(block):
+        d, a = block // 2, lax.rem(block, 2)
+        rows = pl.ds(pl.multiple_of(chip_at(d) * 384, 384), 384)
+
+        @pl.when(block >= 4)
+        def _():
+            staged(block - 2).wait()
+
+        for n in range(3):
+            cols = pl.ds(n * 384, 384)
+            part = (
+                jnp.dot(wbuf[rows, 0:1024], mat[a, :, cols], preferred_element_type=f32) * grad_scale
+            ).astype(bf16)
+
+            @pl.when(d == 0)
+            def _():
+                own_g[pl.ds(pl.multiple_of(a * 384, 384), 384), cols] = part
+
+            @pl.when(d > 0)
+            def _():
+                back[pl.ds(pl.multiple_of(a * 384, 384), 384), cols] = part
+
+        @pl.when(block >= 2)
+        def _():
+            staged(block).start()
+
+    def start_back():
+        load_up.start()
+        staged(6).wait()
+        staged(7).wait()
+        load_gate.wait()
+        load_up.wait()
+
+    def piece(i):
+        return pl.ds(pl.multiple_of((i // 3) * 256, 256), 256), pl.ds(pl.multiple_of(lax.rem(i, 3) * 512, 512), 512)
+
+    def stage_back(i):
+        at, cols = piece(i)
+        back[at, cols] = (
+            dot_nt(mat[0, at, :], wbuf[cols, WINDOW : 2 * WINDOW]) + dot_nt(mat[1, at, :], wbuf[cols, 0:WINDOW])
+        ).astype(bf16)
+
+    def stage_out(i):
+        at, cols = piece(i)
+        out[at, cols] = jnp.dot(act[at, :], wbuf[0:WINDOW, cols], preferred_element_type=f32).astype(bf16)
+
+    partial = (back, out)
+    held, parts = v["held"], v["parts"]
+
+    def kept(a, d):
+        return partial[a].at[tokens(peer_of(shard, d), core)]
+
+    def to_mate(a, d):
         n = a * 4 + d
-        return remote(
-            sources[a].at[rows], own_g.at[pl.ds(a * 1536 + d * 384, 384)],
-            v["xsend"].at[n], v["xrecv"].at[n], (replica, p),
-        )
-
-    fills = [
-        None,
-        pltpu.make_async_copy(v["pd"], own_d, v["in_sem"].at[1]),
-    ]
-    for a in range(2):
-        rows = pl.ds(pl.multiple_of(shard * 384, 384), 384)
-        fills.append(
-            pltpu.make_async_copy(sources[a].at[rows], own_g.at[pl.ds(a * 1536, 384)], v["in_sem"].at[2 + a])
-        )
-
-    partial = (v["p_back"], v["p_out"])
-    held, kept, parts = v["held"], v["kept"], v["parts"]
-
-    def to_mate(a, d):
-        t = peer_of(shard, d)
-        n = a * 4 + d
-        return remote(partial[a].at[tokens(t, other)], held.at[a, d],
-                      v["csend"].at[n], v["crecv"].at[n], mate)
-
-    def keep(a, d):
-        return pltpu.make_async_copy(partial[a].at[tokens(peer_of(shard, d), core)], kept.at[a, d], v["keep_sem"].at[a * 4 + d])
+        return remote(partial[a].at[tokens(peer_of(shard, d), other)], held.at[a, d], v["csend"].at[n], v["crecv"].at[n], mate)
 
     def to_owner(a, d):
         n = a * 3 + d - 1
-        return remote(kept.at[a, d], parts.at[a, d - 1], v["psend"].at[n], v["precv"].at[n], (replica, peer_of(shard, d)))
+        return remote(kept(a, d), parts.at[a, d - 1], v["psend"].at[n], v["precv"].at[n], (replica, peer_of(shard, d)))
 
     def pair_sums(a):
         for d in order:
             to_mate(a, d).wait_recv()
-            keep(a, d).wait()
+            mine = kept(a, d)
 
             def body(rows, carry):
-                kept[a, d, rows, :] = (kept[a, d, rows, :].astype(f32) + held[a, d, rows, :].astype(f32)).astype(bf16)
+                mine[rows, :] = (mine[rows, :].astype(f32) + held[a, d, rows, :].astype(f32)).astype(bf16)
                 return carry
 
             row_loop(128, 32, body, 0)
@@ -854,17 +890,16 @@
 
     def collect(a):
         to_mate(a, 0).wait_recv()
-        keep(a, 0).wait()
         for d in order:
             to_owner(a, d).wait_recv()
 
     def full_sum(a, rows):
-        total = kept[a, 0, rows, :].astype(f32) + held[a, 0, rows, :].astype(f32)
+        total = kept(a, 0)[rows, :].astype(f32) + held[a, 0, rows, :].astype(f32)
         for d in (1, 2, 3):
             total = total + parts[a, d - 1, rows, :].astype(f32)
         return total
 
-    wide = ((v["hid"], v["hid_all"], 768), (v["prj"], v["prj_all"], 1024))
+    wide = ((v["hid"], mat.at[0, :, pl.ds(0, 768)], 768), (v["prj"], mat.at[1, :, pl.ds(0, 1024)], 1024))
     narrow = ((v["ctx"], v["ctx_all"], 384), (v["nrm"], v["nrm_all"], 384))
 
     def block(out, owner, c):
@@ -900,18 +935,20 @@
         ref, out, width = wide[a]
         return pltpu.make_async_copy(columns(ref, core, width), block(out, shard, core), v["local"].at[2 + a])
 
-    wbuf = v["wbuf"]
     load_out = pltpu.make_async_copy(v["wo"], wbuf.at[:, pl.ds(0, 1536)], v["local"].at[4])
-    load_qkv = pltpu.make_async_copy(v["wq"], wbuf, v["local"].at[5])
+    load_qkv = pltpu.make_async_copy(v["wq"], wbuf.at[:, pl.ds(0, 2048)], v["local"].at[5])
 
     def stage_sums():
         pair_sums(0)
         for d in order:
             for a in range(2):
                 narrow_copy(a, d, shard, peer_of(shard, d)).start()
-        for d in (1, 2, 3):
+        send_blocks((1, 2))
+
+    def send_blocks(offsets):
+        for d in offsets:
             for a in range(2):
-                exchange(a, d, peer_of(shard, d)).start()
+                exchange(d * 2 + a, peer_of(shard, d)).start()
 
     def stage_hidden():
         collect(0)
@@ -936,12 +973,14 @@
             wide_copy(0, d, False, core, shard, peer_of(shard, d)).start()
         own_wide(0).start()
 
-    def stage_context():
-        load_out.wait()
-        for e in range(4):
+    def stage_context(part):
+        if part == 0:
+            load_out.wait()
+        for e in (2 * part, 2 * part + 1):
             cols = pl.ds(e * 384, 384)
             v["cgrad"][:, cols] = dot_nt(v["hid"][...], wbuf[cols, 0:1536]).astype(bf16)
-        load_qkv.start()
+        if part == 1:
+            load_qkv.start()
 
     def unrotated(x):
         return x * v["cos"][...] + pltpu.roll(x, HD // 2, 1) * v["sin"][...]
@@ -987,7 +1026,7 @@
             load_qkv.wait()
         for e in (2 * part, 2 * part + 1):
             cols = pl.ds(e * 384, 384)
-            v["ngrad"][:, cols] = dot_nt(v["prj"][...], wbuf[cols, :])
+            v["input_grad"][:, cols] = dot_nt(v["prj"][...], wbuf[cols, 0:2048])
 
     vec, vin, vall = v["vec"], v["vin"], v["vall"]
     replicas = 2 * levels
@@ -1006,7 +1045,7 @@
         def body(rows, totals):
             total, bias = totals
             x = v["x"][rows, :].astype(f32)
-            grad = v["ngrad"][rows, :]
+            grad = v["input_grad"][rows, :]
             inv = lax.rsqrt(jnp.mean(x * x, axis=-1, keepdims=True) + NORM_EPS)
             scaled = gain * grad
             v["input_grad"][rows, :] = v["hgrad"][rows, :] + inv * (
@@ -1036,7 +1075,6 @@
         v["vsum"][...] = total
         for j in range(1, replicas):
             vec_spread(j, replica).start()
-        pair_sums(1)
 
     def stage_vec_out():
         vall[replica] = v["vsum"][...]
@@ -1076,235 +1114,274 @@
 
     def stage_attention_parts(j):
         at = pl.ds(j * 128, 128)
-        own_a[at, 0:1024] = (dot_tn(v["nrm_all"][:, at], v["prj_all"][...]) * grad_scale).astype(bf16)
-        own_a[at, 1024:1792] = (dot_tn(v["ctx_all"][:, at], v["hid_all"][...]) * grad_scale).astype(bf16)
-
-    odd_chip = lax.rem(shard, 2)
-
-    def down_rows(c, at):
+        own_a[at, 0:1024] = (dot_tn(v["nrm_all"][:, at], mat[1, :, 0:1024]) * grad_scale).astype(bf16)
+        own_a[at, 1024:1792] = (dot_tn(v["ctx_all"][:, at], mat[0, :, 0:768]) * grad_scale).astype(bf16)
+
+    def down_at(c, j):
         first = odd_chip * (1088 * c - 64 * (1 - c)) + (1 - odd_chip) * 1152 * c
-        return pl.ds(pl.multiple_of(first + at.start, 64), at.size)
-
-    chunks = []
-    for at in row_spans(DOWN_CHUNKS):
-        chunks.append((own_d, v["low_d"], v["high_d"], at, ("none",), lambda c, at=at: v["fd"].at[down_rows(c, at)]))
-    for d in range(4):
-        for a in range(2):
-            for k in range(3):
-                at = pl.ds(a * 1536 + d * 384 + k * CHUNK, CHUNK)
-                dst = (v["fg"], v["fu"])[a]
-                source = peer_of(shard, d)
-                chunks.append((
-                    own_g, v["low_g"], v["high_g"], at, ("fill", 2 + a) if d == 0 else ("x", a, d),
-                    lambda c, k=k, dst=dst, source=source: dst.at[c, source, pl.ds(k * CHUNK, CHUNK)],
-                ))
-    for at in row_spans(ATTENTION_CHUNKS):
-        chunks.append((own_a, v["low_a"], v["high_a"], at, ("none",), lambda c, at=at: v["fa"].at[c, at]))
-    total = len(chunks)
-    awaited = (set(), set())
+        return v["fd"].at[pl.ds(pl.multiple_of(first + j * 64, 64), 64)]
+
+    def gate_at(c, j):
+        group = j // 6
+        rows = pl.ds(pl.multiple_of(lax.rem(j, 6) * 64, 64), 64)
+        return v["fg"].at[lax.rem(group, 2), c, chip_at(group // 2), rows]
+
+    def attention_at(c, j):
+        return v["fa"].at[c, pl.ds(pl.multiple_of(j * 32, 32), 32)]
+
+    segments = (
+        (own_d, v["near_d"], v["far_d"], 64, 0, DOWN_STEPS, down_at),
+        (own_g, v["near_g"], v["far_g"], 64, DOWN_STEPS, DOWN_STEPS + GATE_STEPS, gate_at),
+        (own_a, v["near_a"], v["far_a"], 32, DOWN_STEPS + GATE_STEPS, CHUNKS, attention_at),
+    )
     end = (level == 0) | (level == levels - 1)
-
-    def arrive(what, seen):
-        if what in seen or what[0] == "none":
-            return
-        seen.add(what)
-        if what[0] == "fill":
-            fills[what[1]].wait()
-        else:
-            exchange(what[1], what[2], peer_of(shard, what[2])).wait_recv()
-
-    def up(k, ref):
-        own, low, high, at, _, _ = chunks[k]
-        return remote(ref.at[at], low.at[at], v["up_sem"].at[k], v["low_sem"].at[k], above)
-
-    def down(k, ref):
-        own, low, high, at, _, _ = chunks[k]
-        return remote(ref.at[at], high.at[at], v["down_sem"].at[k], v["high_sem"].at[k], below)
-
-    def add(k, *refs):
-        own, _, _, at, _, _ = chunks[k]
-        step = 16
-
-        def body(j, carry):
-            rows = pl.ds(pl.multiple_of(at.start + j * step, step), step)
-            value = own[rows, :].astype(f32)
-            for ref in refs:
-                value = value + ref[rows, :].astype(f32)
+    middle = levels // 2
+
+    def on(k, stage, c=None):
+        c = core if c is None else c
+        for n, segment in enumerate(segments):
+            j = k - segment[4]
+            inside = (k >= segment[4]) & (k < segment[5])
+            if n == 0:
+                inside &= (j > 0) | (1 - odd_chip + c > 0)
+                inside &= (j < DOWN_STEPS - 1) | (odd_chip + 1 - c > 0)
+            pl.when(inside)(functools.partial(stage, n, segment, j, k))
+
+    def rows_of(segment, j):
+        size = segment[3]
+        return pl.ds(pl.multiple_of(j * size, size), size)
+
+    def message(segment, j, k, upward, near):
+        own, near_ref, far_ref = segment[:3]
+        target = near_ref.at[rows_of(segment, j)] if near else far_ref.at[rows_of(segment, j // 2)]
+        sem = v["near_sem"] if near else v["far_sem"]
+        return remote(own.at[rows_of(segment, j)], target, v["part_sem"].at[k], sem.at[k], above if upward else below)
+
+    def result(segment, j, k, upward, from_own):
+        place_ = segment[6](core, j)
+        src = segment[0].at[rows_of(segment, j)] if from_own else place_
+        sem = v["up_sem"] if upward else v["down_sem"]
+        return remote(src, place_, sem.at[k], v["done_sem"].at[k], above if upward else below)
+
+    def keep_result(segment, j, k):
+        return pltpu.make_async_copy(segment[0].at[rows_of(segment, j)], segment[6](core, j), v["out_sem"].at[k])
+
+    def to_other_core(segment, j, k, from_own, c):
+        place_ = segment[6](c, j)
+        src = segment[0].at[rows_of(segment, j)] if from_own else place_
+        return remote(src, place_, v["mate_send"].at[k], v["mate_recv"].at[k], mate)
+
+    def add(segment, j, with_far):
+        own, near_ref, far_ref, size = segment[:4]
+
+        def body(i, carry):
+            rows = pl.ds(pl.multiple_of(j * size + i * 16, 16), 16)
+            value = own[rows, :].astype(f32) + near_ref[rows, :].astype(f32)
+            if with_far:
+                value = value + far_ref[pl.ds(pl.multiple_of((j // 2) * size + i * 16, 16), 16), :].astype(f32)
             own[rows, :] = value.astype(own.dtype)
             return carry
 
-        lax.fori_loop(0, at.size // step, body, 0)
-
-    def finish(k, ref):
-        _, _, _, at, _, dst = chunks[k]
-        pltpu.make_async_copy(ref.at[at], dst(core), v["out_sem"].at[k]).start()
-        remote(ref.at[at], dst(core), v["mate_send"].at[k], v["mate_recv"].at[k], mate).start()
-
-    def guarded(stage, k):
-        if k == 0:
-            pl.when(1 - odd_chip + core > 0)(lambda: stage(k))
-        elif k == len(DOWN_CHUNKS) - 1:
-            pl.when(odd_chip + 1 - core > 0)(lambda: stage(k))
-        else:
-            stage(k)
-
-    def guarded_mate(stage, k):
-        if k == 0:
-            pl.when(1 - odd_chip + other > 0)(lambda: stage(k))
-        elif k == len(DOWN_CHUNKS) - 1:
-            pl.when(odd_chip + 1 - other > 0)(lambda: stage(k))
-        else:
-            stage(k)
+        lax.fori_loop(0, size // 16, body, 0)
+
+    def arrived(n, j):
+        if n != 1:
+            return
+        group = j // 6
+
+        @pl.when((lax.rem(j, 6) == 0) & (group >= 2))
+        def _():
+            exchange(group, shard).wait_recv()
 
     def root_of(k):
-        return levels // 2 - 1 + k % 2
-
-    def end_gather(k):
-        own = chunks[k][0]
-
+        return middle - 1 + lax.rem(k, 2)
+
+    def end_gather(n, segment, j, k):
         @pl.when(end)
         def _():
-            arrive(chunks[k][4], awaited[0])
+            arrived(n, j)
 
         @pl.when(level == 0)
         def _():
-            up(k, own).start()
+            message(segment, j, k, True, True).start()
 
         @pl.when(level == levels - 1)
         def _():
-            down(k, own).start()
-
-    def gather_step(k):
-        own, low, high, at, what, _ = chunks[k]
-        root = root_of(k)
-
+            message(segment, j, k, False, True).start()
+
+    def gather_step(n, segment, j, k):
         @pl.when(~end)
         def _():
-            arrive(what, awaited[1])
-
-        if root > 1:
-
-            @pl.when((level > 0) & (level < root))
+            arrived(n, j)
+
+            @pl.when(level != root_of(k))
             def _():
-                up(k, own).wait_recv()
-                add(k, low)
-                up(k, own).start()
-
-        if root < levels - 2:
-
-            @pl.when((level < levels - 1) & (level > root))
+                message(segment, j, k, True, True).wait_recv()
+                add(segment, j, False)
+
+        for upward in (True, False):
+            towards = (level > 0) & (level < root_of(k)) if upward else (level < levels - 1) & (level > root_of(k))
+            crosses = level == (middle - 1 if upward else middle)
+
+            @pl.when(towards & crosses)
             def _():
-                down(k, own).wait_recv()
-                add(k, high)
-                down(k, own).start()
-
-    def root_step(k):
-        own, low, high, at, _, _ = chunks[k]
-
+                message(segment, j, k, upward, False).start()
+
+            if levels > 4:
+
+                @pl.when(towards & ~crosses)
+                def _():
+                    message(segment, j, k, upward, True).start()
+
+    def root_step(n, segment, j, k):
         @pl.when(level == root_of(k))
         def _():
-            up(k, own).wait_recv()
-            down(k, own).wait_recv()
-            add(k, low, high)
-            up(k, own).start()
-            down(k, own).start()
-            finish(k, own)
-
-    def spread_step(k):
-        own, low, high, at, _, _ = chunks[k]
+            message(segment, j, k, True, True).wait_recv()
+            message(segment, j, k, True, False).wait_recv()
+            add(segment, j, True)
+            result(segment, j, k, True, True).start()
+            result(segment, j, k, False, True).start()
+            keep_result(segment, j, k).start()
+            to_other_core(segment, j, k, True, core).start()
+
+    def spread_step(n, segment, j, k):
+        @pl.when(~end & (level != root_of(k)))
+        def _():
+            result(segment, j, k, True, False).wait_recv()
+
+            @pl.when(level < root_of(k))
+            def _():
+                result(segment, j, k, False, False).start()
+
+            @pl.when(level > root_of(k))
+            def _():
+                result(segment, j, k, True, False).start()
+
+            to_other_core(segment, j, k, False, core).start()
+
+    def end_spread(n, segment, j, k):
+        @pl.when(end)
+        def _():
+            result(segment, j, k, True, False).wait_recv()
+            to_other_core(segment, j, k, False, core).start()
+
+    def close(n, segment, j, k):
         root = root_of(k)
 
-        if root > 1:
-
-            @pl.when((level > 0) & (level < root))
-            def _():
-                down(k, own).wait_recv()
-                down(k, high).start()
-                finish(k, high)
-
-        if root < levels - 2:
-
-            @pl.when((level < levels - 1) & (level > root))
-            def _():
-                up(k, own).wait_recv()
-                up(k, low).start()
-                finish(k, low)
-
-    def end_spread(k):
-        own, low, high, at, _, _ = chunks[k]
-
-        @pl.when(level == 0)
+        @pl.when(level == root)
         def _():
-            down(k, own).wait_recv()
-            finish(k, high)
-
-        @pl.when(level == levels - 1)
+            result(segment, j, k, True, True).wait_send()
+            result(segment, j, k, False, True).wait_send()
+            keep_result(segment, j, k).wait()
+
+        @pl.when(level != root)
         def _():
-            up(k, own).wait_recv()
-            finish(k, low)
-
-    for a in range(2):
+            message(segment, j, k, True, True).wait_send()
+
+        @pl.when(~end & (level < root))
+        def _():
+            result(segment, j, k, False, False).wait_send()
+
+        @pl.when(~end & (level > root))
+        def _():
+            result(segment, j, k, True, False).wait_send()
+
+        to_other_core(segment, j, k, True, core).wait_send()
+
+    def close_mate(n, segment, j, k):
+        to_other_core(segment, j, k, True, other).wait_recv()
+
+    def start_mate(a):
         for d in order + (0,):
             to_mate(a, d).start()
-            keep(a, d).start()
-    for copy in fills[1:]:
+
+    load_down.start()
+    load_normed.start()
+    for copy in load_deltas:
         copy.start()
-    load_out.start()
-    fills[1].wait()
+    load_gate.start()
+    load_act.start()
     for a in range(2):
         own_narrow(a).start()
         onward(a, 0, columns(narrow[a][0], shard, 384), shard, core).start()
-    beside = {
-        2: [stage_sums],
-        12: [stage_hidden],
-        13: [stage_context],
-        14: [functools.partial(stage_heads, 0, 0)],
-        15: [functools.partial(stage_heads, 0, 1), stage_relay],
-        16: [functools.partial(stage_heads, 0, 2)],
-        17: [functools.partial(stage_heads, 1, 0)],
-        18: [functools.partial(stage_heads, 1, 1)],
-        19: [functools.partial(stage_heads, 1, 2), stage_send_projected],
-        20: [functools.partial(stage_normed, 0)],
-        21: [functools.partial(stage_normed, 1)],
-        22: [stage_input],
-        32: [stage_gathered, functools.partial(stage_attention_parts, 0)],
-        33: [functools.partial(stage_attention_parts, 1)],
-        34: [functools.partial(stage_attention_parts, 2)],
-        36: [stage_vec],
-        total + 8: [stage_vec_out],
-        total + 10: [stage_output],
-    }
-    stages = ((end_gather, 0), (gather_step, 6), (root_step, 10), (spread_step, 14), (end_spread, 20))
-    for t in range(total + stages[-1][1]):
-        for stage, lag in stages:
-            if 0 <= t - lag < total:
-                guarded(stage, t - lag)
-        for stage in beside.get(t, ()):
-            stage()
-    for a in range(2):
-        for d in (1, 2, 3):
-            exchange(a, d, peer_of(shard, d)).wait_send()
-    def close(k):
-        own, low, high, at, _, dst = chunks[k]
-
-        @pl.when(level < levels - 1)
-        def _():
-            up(k, own).wait_send()
-
-        @pl.when(level > 0)
-        def _():
-            down(k, own).wait_send()
-
-        pltpu.make_async_copy(own.at[at], dst(core), v["out_sem"].at[k]).wait()
-        remote(own.at[at], dst(core), v["mate_send"].at[k], v["mate_recv"].at[k], mate).wait_send()
-
-    def close_mate(k):
-        own, low, high, at, _, dst = chunks[k]
-        remote(own.at[at], dst(other), v["mate_send"].at[k], v["mate_recv"].at[k], mate).wait_recv()
-
-    for k in range(total):
-        guarded(close, k)
-        guarded_mate(close_mate, k)
+    load_down.wait()
+    lags = ((end_gather, 0), (gather_step, 8), (root_step, 14), (spread_step, 20), (end_spread, 28))
+    steps = CHUNKS + lags[-1][1]
+
+    def begin_products():
+        load_normed.wait()
+        for copy in load_deltas:
+            copy.wait()
+
+    def begin_out():
+        start_mate(0)
+        load_wd.start()
+        load_act.wait()
+
+    def end_out():
+        start_mate(1)
+        load_out.start()
+
+    def stage_projected():
+        stage_send_projected()
+        send_blocks((3,))
+
+    beside = [
+        (0, 1, begin_products),
+        (0, 8, stage_gradient),
+        (8, 1, start_back),
+        (8, 6, lambda i: (stage_back(2 * i), stage_back(2 * i + 1))),
+        (14, 1, begin_out),
+        (16, 1, stage_sums),
+        (17, 1, load_wd.wait),
+        (17, 4, lambda i: (stage_out(3 * i), stage_out(3 * i + 1), stage_out(3 * i + 2))),
+        (21, 1, end_out),
+        (22, 1, stage_hidden),
+        (24, 1, functools.partial(stage_context, 0)),
+        (25, 1, functools.partial(stage_context, 1)),
+    ]
+    for n in range(6):
+        beside.append((26 + n, 1, functools.partial(stage_heads, n // 3, n % 3)))
+    beside += [
+        (31, 1, stage_projected),
+        (32, 1, functools.partial(stage_normed, 0)),
+        (34, 1, functools.partial(stage_normed, 1)),
+        (36, 1, stage_input),
+        (38, 1, stage_relay),
+        (56, 1, stage_gathered),
+        (56, 1, functools.partial(stage_attention_parts, 0)),
+        (58, 1, functools.partial(stage_attention_parts, 1)),
+        (60, 1, functools.partial(stage_attention_parts, 2)),
+        (62, 1, functools.partial(pair_sums, 1)),
+        (64, 1, stage_vec),
+        (steps - 4, 1, stage_vec_out),
+        (steps - 2, 1, stage_output),
+    ]
+
+    def step(t, carry):
+        for stage, lag in lags:
+            on(t - lag, stage)
+        for first, count, stage in beside:
+            if count == 1:
+                pl.when(t == first)(stage)
+            else:
+                @pl.when((t >= first) & (t < first + count))
+                def _():
+                    stage(t - first)
+
+        return carry
+
+    lax.fori_loop(0, steps, step, 0)
+
+    def finish_step(k, carry):
+        on(k, close)
+        on(k, close_mate, other)
+        return carry
+
+    lax.fori_loop(0, CHUNKS, finish_step, 0)
+    for d in (1, 2, 3):
+        for a in range(2):
+            exchange(d * 2 + a, peer_of(shard, d)).wait_send()
     for a in range(2):
         for d in (0, 1, 2, 3):
             p = peer_of(shard, d)
@@ -1325,35 +1402,39 @@
     bf16 = jnp.bfloat16
     f32 = jnp.float32
     dma = pltpu.SemaphoreType.DMA
-    in_hbm = ("pd", "pg", "pu", "p_back", "p_out", "wo", "wq")
+    in_hbm = ("pd", "act", "gd", "ud", "n_t", "w_g", "w_u", "w_d", "wo", "wq")
     outs = {
         "fa": ((2, 384, 1792), bf16, any_spec()),
         "fd": ((2240, 1536), bf16, any_spec()),
-        "fg": ((2, 4, 384, WINDOW), bf16, any_spec()),
-        "fu": ((2, 4, 384, WINDOW), bf16, any_spec()),
+        "fg": ((2, 2, 4, 384, WINDOW), bf16, any_spec()),
+        "blocks": ((6, 384, WINDOW), bf16, any_spec()),
         "block_out": ((128, 1536), bf16, vmem_spec()),
         "input_grad": ((128, 1536), f32, vmem_spec()),
         "vec_out": ((8, 1280), f32, vmem_spec()),
     }
-    scratch = {}
-    for where in ("own", "low", "high"):
-        scratch[where + "_a"] = pltpu.VMEM((384, 1792), bf16)
-        scratch[where + "_d"] = pltpu.VMEM((WINDOW, 1536), bf16)
-        scratch[where + "_g"] = pltpu.VMEM((3072, WINDOW), bf16)
-    scratch |= {
+    scratch = {
+        "own_a": pltpu.VMEM((384, 1792), bf16),
+        "own_d": pltpu.VMEM((WINDOW, 1536), bf16),
+        "own_g": pltpu.VMEM((3072, WINDOW), bf16),
+        "near_a": pltpu.VMEM((384, 1792), bf16),
+        "near_d": pltpu.VMEM((WINDOW, 1536), bf16),
+        "near_g": pltpu.VMEM((3072, WINDOW), bf16),
+        "far_a": pltpu.VMEM((192, 1792), bf16),
+        "far_d": pltpu.VMEM((WINDOW // 2, 1536), bf16),
+        "far_g": pltpu.VMEM((1536, WINDOW), bf16),
+        "mat": pltpu.VMEM((2, 1024, WINDOW), bf16),
+        "act_buf": pltpu.VMEM((1024, WINDOW), bf16),
+        "wbuf": pltpu.VMEM((1536, 2 * WINDOW), bf16),
+        "back": pltpu.VMEM((1024, 1536), bf16),
+        "out": pltpu.VMEM((1024, 1536), bf16),
         "held": pltpu.VMEM((2, 4, 128, 1536), bf16),
-        "kept": pltpu.VMEM((2, 4, 128, 1536), bf16),
         "parts": pltpu.VMEM((2, 3, 128, 1536), bf16),
-        "wbuf": pltpu.VMEM((1536, 2048), bf16),
         "hgrad": pltpu.VMEM((128, 1536), f32),
-        "ngrad": pltpu.VMEM((128, 1536), f32),
         "hid": pltpu.VMEM((128, 1536), bf16),
         "cgrad": pltpu.VMEM((128, 1536), bf16),
         "prj": pltpu.VMEM((128, 2048), bf16),
         "ctx_all": pltpu.VMEM((1024, 384), bf16),
         "nrm_all": pltpu.VMEM((1024, 384), bf16),
-        "hid_all": pltpu.VMEM((1024, 768), bf16),
-        "prj_all": pltpu.VMEM((1024, 1024), bf16),
         "row_two": pltpu.VMEM((1, 1536), f32),
         "kv_sum": pltpu.VMEM((2, 128, HD), f32),
         "vec": pltpu.VMEM((4, 8, 1280), f32),
@@ -1362,10 +1443,12 @@
         "vall": pltpu.VMEM((2 * levels, 8, 1280), f32),
     }
     counts = {
-        "xsend": 8, "xrecv": 8, "csend": 8, "crecv": 8, "keep_sem": 8, "psend": 6, "precv": 6, "gsend": 24, "grecv": 24,
-        "fsend": 8, "frecv": 8, "local": 6, "in_sem": 4, "vsend": 2 + 2 * levels, "vrecv": 2 + 2 * levels,
+        "xsend": 8, "xrecv": 8, "stage_sem": 2, "csend": 8, "crecv": 8, "psend": 6, "precv": 6, "gsend": 24, "grecv": 24,
+        "fsend": 8, "frecv": 8, "local": 6, "in_sem": 8, "vsend": 2 + 2 * levels, "vrecv": 2 + 2 * levels,
     }
-    for name in ("up_sem", "down_sem", "low_sem", "high_sem", "mate_send", "mate_recv", "out_sem"):
+    for name in (
+        "part_sem", "near_sem", "far_sem", "up_sem", "down_sem", "done_sem", "mate_send", "mate_recv", "out_sem"
+    ):
         counts[name] = CHUNKS
     scratch |= {name: dma((n,)) for name, n in counts.items()}
     return pl.pallas_call(
@@ -1398,7 +1481,9 @@
 def widen(*sums):
     rows = 32
     f32 = jnp.float32
-    blocks = pl.BlockSpec((2, 4, rows, WINDOW), lambda i: (0, 0, i, 0))
+    def blocks(a):
+        return pl.BlockSpec((None, 2, 4, rows, WINDOW), lambda i: (a, 0, 0, i, 0))
+
     down = pl.BlockSpec((224, 1536), lambda i: (jnp.minimum(i, 9), 0))
 
     def whole(width):
@@ -1414,7 +1499,7 @@
             jax.ShapeDtypeStruct((384, 2048), f32),
             jax.ShapeDtypeStruct((384, 1536), f32),
         ],
-        in_specs=[blocks, blocks, down, pl.BlockSpec((2, rows, 1792), lambda i: (0, i, 0))],
+        in_specs=[blocks(0), blocks(1), down, pl.BlockSpec((2, rows, 1792), lambda i: (0, i, 0))],
         out_specs=[whole(8960), whole(8960), down, whole(2048), whole(1536)],
     )(*sums)
 
@@ -1453,14 +1538,17 @@
         wd=down_weight,
         cot=cotangent,
     )
-    sum_attn, sum_down, sum_gate, sum_up, block_output, input_grad, vectors = backward(
+    sum_attn, sum_down, sum_gate, _, block_output, input_grad, vectors = backward(
         levels,
         grad_scale,
         pd=got["pd"],
-        pg=got["pg"],
-        pu=got["pu"],
-        p_back=got["p_back"],
-        p_out=got["p_out"],
+        act=got["act"],
+        gd=got["gd"],
+        ud=got["ud"],
+        n_t=got["n_t"],
+        w_g=got["w_g"],
+        w_u=got["w_u"],
+        w_d=got["w_d"],
         wo=got["o_full"],
         wq=got["q_full"],
         hidden=got["hidden"],
@@ -1478,7 +1566,7 @@
         sin=-turn,
     )
     gain_one_own, bias_own, gain_two_own = vectors[0, :384], vectors[0, 384:896], vectors[0, 896:]
-    gate_grad, up_grad, down_grad, qkv_grad, out_grad = widen(sum_gate, sum_up, sum_down, sum_attn)
+    gate_grad, up_grad, down_grad, qkv_grad, out_grad = widen(sum_gate, sum_gate, sum_down, sum_attn)
     return (
         block_output,
         input_grad,

time: 538 us -> 512 us (0.952); the launches traced: 527 us -> 510 us
  Pallas kernels: 517 us -> 500 us
    pallas_call x1, Pallas kernels: 162 us -> 147 us  [forward(): pl.pallas_call(functools.partial(forward_kernel, grad_scale, (*given, *ou...]
where the time goes in v7:
time: 512 us; the launch traced here: 510 us
  Pallas kernels  500 us (98%)
  local copies, waits for them, and re-layouts  7.8 us (2%)
    pallas_call x1, Pallas kernels, backward(): pl.pallas_call(functools.partial(backward_kernel, levels, grad_scale, (*g...  327 us
    pallas_call x1, Pallas kernels, forward(): pl.pallas_call(functools.partial(forward_kernel, grad_scale, (*given, *ou...  147 us
    pallas_call x1, Pallas kernels, widen(): pl.pallas_call(widen_kernel, grid=(384 // rows,), out_shape=[jax.ShapeDty...  25.3 us

profile of v7, /device:TPU:0, one launch (start us, length us, event | category | flops | bytes accessed | tf_op | source)
XLA Modules:
  0.0 509.6 jit_solution(14983587685860570262)
XLA Ops:
  0.7 0.7 pad.11
  1.4 0.7 pad.12
  2.0 0.7 stack.13
  2.7 0.6 fusion.7.refs_1_
  3.3 0.3 fusion.5
  3.6 0.8 fusion.8
  4.4 146.8 %shard_map.177 = (bf16[1536,2048]{1,0:T(8,128)(2,1)}, bf16[1536,1536]{1,0:T(8,128)(2,1)}, bf16[1152,1536]{1,0:T(8,128)(2,1)}, bf16[1024,1152]{1,0:T(8,128)(2,1)}...) custom-call(bf16[128,1536]{1,0:T(8,128)(2,1)} %refs_11_.1, ...), custom_call_target="tpu_custom_call" | custom-call | tf_op jit(solution)/shard_map/pallas_call | solution.py:764
  151.2 1.5 fusion.9
  152.7 327.4 %shard_map.178 = (bf16[2,384,1792]{2,1,0:T(8,128)(2,1)}, bf16[2240,1536]{1,0:T(8,128)(2,1)}, bf16[2,2,4,384,1152]{4,3,2,1,0:T(8,128)(2,1)}, bf16[6,384,1152]{2,1...) custom-call(bf16[1152,1536]{1,0:T(8,128)(2,1)} %get-tuple-element.39.refs_0_, ...), custom_call_target="tpu_custom_call" | custom-call | tf_op jit(solution)/shard_map/pallas_call | solution.py:1454
  480.1 1.3 slice.18
  481.4 1.3 slice_reduce_fusion
  482.7 0.0 copy-start.1
  482.7 0.0 copy-start
  482.7 25.3 %shard_map.179 = (f32[384,8960]{1,0:T(8,128)}, f32[384,8960]{1,0:T(8,128)}, f32[2240,1536]{1,0:T(8,128)}, f32[384,2048]{1,0:T(8,128)}, f32[384,1536]{1,0:T(8,128)}) custom-call(bf16[2,2,4,384,1152]{4,3,2,1,0:T(8,128)(2,1)} %get-tuple-element.60.gate.up, bf16[2,2,4,384,1152]{4,3,2,1,0:T(8,128)(2,1)} %get-tuple-element.60.gate.up, ...), custom_call_target="tpu_custom_call" | custom-call | tf_op jit(solution)/shard_map/pallas_call | solution.py:1492
  508.0 0.0 copy-done.1
  508.0 0.7 copy.22
  508.8 0.0 copy-done
  508.8 0.9 copy.23
  (3 shorter events, 0.0 us)
Async XLA Ops:
  482.7 25.3 %copy-start.1 = (bf16[128,1536]{1,0:T(8,128)(2,1)S(1)}, bf16[128,1536]{1,0:T(8,128)(2,1)}, u32[]{:S(2)}) copy-start(bf16[128,1536]{1,0:T(8,128)(2,1)} %get-tuple-element.88) | copy-start | bytes 1179652
  482.7 26.0 %copy-start = (f32[128,1536]{1,0:T(8,128)S(1)}, f32[128,1536]{1,0:T(8,128)}, u32[]{:S(2)}) copy-start(f32[128,1536]{1,0:T(8,128)} %get-tuple-element.89) | copy-start | bytes 2359300

commit v8 on v7

--- a/solution.py
+++ b/solution.py
@@ -357,7 +357,7 @@
     return lax.fori_loop(0, rows // step, lambda j, c: body(pl.ds(pl.multiple_of(j * step, step), step), c), init)
 
 
-TILES = ((0, 640, 192), (640, 512, 160))
+TILES = ((0, 640, 160), (640, 512, 160))
 
 
 def forward_kernel(grad_scale, names, *refs):
@@ -406,6 +406,13 @@
             v["send"].at[n], v["recv"].at[n], (replica, t),
         )
 
+    def relay(i, way, t, o):
+        _, out, size, shared, _ = weights[i]
+        first = o * 384 + base(i, core) + odd * shared
+        ref = out.at[span(first, 64)] if way == 1 else out.at[span(first + 64, size - shared - 64)]
+        n = i * 2 + way - 1
+        return remote(ref, ref, v["rsend"].at[n], v["rrecv"].at[n], (replica, t))
+
     def across(i, d, o, whose):
         _, out, size, shared, _ = weights[i]
         ref = out.at[span(o * 384 + base(i, core) + whose * (size - shared), shared)]
@@ -426,6 +433,11 @@
         return remote(row_sets[a].at[tokens(shard, core)], row_sets[a].at[tokens(o, core)], v["send"].at[n], v["recv"].at[n],
                       (replica, t))
 
+    def row_relay(a, way, t, o):
+        ref = row_sets[a].at[span((core * 4 + o) * 128 + 64 * (way - 1), 64)]
+        n = 4 + a * 2 + way - 1
+        return remote(ref, ref, v["rsend"].at[n], v["rrecv"].at[n], (replica, t))
+
     def row_onward(a, d, o, c):
         n = 12 + a * 4 + d
         ref = row_sets[a].at[tokens(o, c)]
@@ -436,29 +448,43 @@
         return remote(v["small"], small_all.at[o], v["send"].at[n], v["recv"].at[n], (replica, t))
 
     def send_rows(a):
-        for d in order:
+        for d in (1, 2):
             row_hop(a, d, peer_of(shard, d), shard).start()
         row_onward(a, 0, shard, core).start()
 
     def take_rows(a):
-        for d in order:
+        for d in (1, 2):
             p = peer_of(shard, d)
             row_hop(a, d, p, p).wait_recv()
+            row_relay(a, d, peer_of(shard, 3 - d), p).start()
             row_onward(a, d, p, core).start()
+
+    def take_far_rows(a):
+        p = peer_of(shard, 3)
+        for way in (1, 2):
+            row_relay(a, way, p, p).wait_recv()
+        row_onward(a, 3, p, core).start()
 
     def have_rows(a):
         for d in (0,) + order:
             row_onward(a, d, peer_of(shard, d), other).wait_recv()
 
     def send_weight(i):
-        for d in order:
+        for d in (1, 2) if weights[i][4] else order:
             hop(i, d, peer_of(shard, d), shard).start()
 
     def take(i, d):
         p = peer_of(shard, d)
-        hop(i, d, p, p).wait_recv()
+        relayed = weights[i][4]
+        if relayed and d == 3:
+            for way in (1, 2):
+                relay(i, way, p, p).wait_recv()
+        else:
+            hop(i, d, p, p).wait_recv()
+            if relayed:
+                relay(i, d, peer_of(shard, 3 - d), p).start()
         across(i, d, p, odd).start()
-        if weights[i][4]:
+        if relayed:
             onward(i, d, p, core, False).start()
 
     def take_shared(i):
@@ -506,11 +532,6 @@
     def _():
         d_buf[span(1088 - 1088 * odd_chip, 64), :] = jnp.zeros((64, 1536), bf16)
 
-    loads[0].wait()
-    send_rows(0)
-    send_weight(2)
-    send_weight(3)
-
     small_all[shard] = v["small"][...]
     for d in order:
         p = peer_of(shard, d)
@@ -528,7 +549,7 @@
         return carry
 
     row_loop(128, 16, norm_body, 0)
-    for copy in loads[1:]:
+    for copy in loads:
         copy.wait()
 
     @pl.when(inside)
@@ -536,8 +557,13 @@
         rest.wait()
 
     for i in (0, 1):
-        for d in order:
+        for d in (1, 2):
             take(i, d)
+    send_rows(0)
+    send_weight(2)
+    send_weight(3)
+    take(0, 3)
+    take(1, 3)
     take_shared(0)
     have_other_half(0)
     keep_q = pltpu.make_async_copy(q_buf, v["q_full"], v["local"].at[7])
@@ -595,13 +621,15 @@
 
     lax.fori_loop(0, 8, norm_two, 0)
     send_rows(1)
-    send_weight(4)
-    send_weight(5)
     take_rows(0)
     for i in (2, 3):
         for d in order:
             take(i, d)
     take_rows(1)
+    send_weight(4)
+    send_weight(5)
+    take_far_rows(0)
+    take_far_rows(1)
     take_shared(2)
     take_shared(3)
     have_rows(0)
@@ -690,7 +718,9 @@
     for i in (0, 1):
         for d in order:
             p = peer_of(shard, d)
-            hop(i, d, p, shard).wait_send()
+            if d < 3:
+                hop(i, d, p, shard).wait_send()
+                relay(i, d, peer_of(shard, 3 - d), p).wait_send()
             across(i, d, p, odd).wait_send()
             for part in (False, True):
                 onward(i, d, p, core, part).wait_send()
@@ -703,7 +733,9 @@
             hop(i, d, p, shard).wait_send()
             across(i, d, p, odd).wait_send()
         for a in range(2):
-            row_hop(a, d, p, shard).wait_send()
+            if d < 3:
+                row_hop(a, d, p, shard).wait_send()
+                row_relay(a, d, peer_of(shard, 3 - d), p).wait_send()
     for a in range(2):
         for d in (0,) + order:
             row_onward(a, d, peer_of(shard, d), core).wait_send()
@@ -755,6 +787,8 @@
         "d_grad": pltpu.VMEM((WINDOW, 1536), bf16),
         "send": dma((27,)),
         "recv": dma((27,)),
+        "rsend": dma((8,)),
+        "rrecv": dma((8,)),
         "zsend": dma((18,)),
         "zrecv": dma((18,)),
         "fsend": dma((20,)),
@@ -952,7 +986,7 @@
 
     def stage_hidden():
         collect(0)
-        gain = v["gain_two"][...]
+        gain = v["gains"][1:2, :]
 
         def body(rows, total):
             grad = full_sum(0, rows)
@@ -983,7 +1017,7 @@
             load_qkv.start()
 
     def unrotated(x):
-        return x * v["cos"][...] + pltpu.roll(x, HD // 2, 1) * v["sin"][...]
+        return x * v["cos"][...] - pltpu.roll(x, HD // 2, 1) * v["sin"][...]
 
     def stage_heads(g, part):
         keys = v["key"][:, g * HD : (g + 1) * HD]
@@ -1040,7 +1074,7 @@
         return remote(v["vsum"], vall.at[slot], v["vsend"].at[2 + j], v["vrecv"].at[2 + j], (target, shard))
 
     def stage_input():
-        gain = v["gain_one"][...]
+        gain = v["gains"][0:1, :]
 
         def body(rows, totals):
             total, bias = totals
@@ -1327,27 +1361,27 @@
         send_blocks((3,))
 
     beside = [
-        (0, 1, begin_products),
-        (0, 8, stage_gradient),
-        (8, 1, start_back),
-        (8, 6, lambda i: (stage_back(2 * i), stage_back(2 * i + 1))),
-        (14, 1, begin_out),
-        (16, 1, stage_sums),
-        (17, 1, load_wd.wait),
-        (17, 4, lambda i: (stage_out(3 * i), stage_out(3 * i + 1), stage_out(3 * i + 2))),
-        (21, 1, end_out),
-        (22, 1, stage_hidden),
-        (24, 1, functools.partial(stage_context, 0)),
-        (25, 1, functools.partial(stage_context, 1)),
+        (9, 1, begin_products),
+        (9, 4, lambda i: (stage_gradient(2 * i), stage_gradient(2 * i + 1))),
+        (13, 1, start_back),
+        (13, 4, lambda i: (stage_back(3 * i), stage_back(3 * i + 1), stage_back(3 * i + 2))),
+        (17, 1, begin_out),
+        (19, 1, stage_sums),
+        (20, 1, load_wd.wait),
+        (20, 4, lambda i: (stage_out(3 * i), stage_out(3 * i + 1), stage_out(3 * i + 2))),
+        (24, 1, end_out),
+        (25, 1, stage_hidden),
+        (26, 1, functools.partial(stage_context, 0)),
+        (27, 1, functools.partial(stage_context, 1)),
     ]
     for n in range(6):
-        beside.append((26 + n, 1, functools.partial(stage_heads, n // 3, n % 3)))
+        beside.append((28 + n, 1, functools.partial(stage_heads, n // 3, n % 3)))
     beside += [
-        (31, 1, stage_projected),
-        (32, 1, functools.partial(stage_normed, 0)),
-        (34, 1, functools.partial(stage_normed, 1)),
-        (36, 1, stage_input),
-        (38, 1, stage_relay),
+        (33, 1, stage_projected),
+        (34, 1, functools.partial(stage_normed, 0)),
+        (36, 1, functools.partial(stage_normed, 1)),
+        (38, 1, stage_input),
+        (40, 1, stage_relay),
         (56, 1, stage_gathered),
         (56, 1, functools.partial(stage_attention_parts, 0)),
         (58, 1, functools.partial(stage_attention_parts, 1)),
@@ -1461,8 +1495,10 @@
     )(*given.values())
 
 
-def widen_kernel(gate, up, down, attn, out_gate, out_up, out_down, out_qkv, out_out):
+def widen_kernel(gate, up, down, attn, block, grad, out_gate, out_up, out_down, out_qkv, out_out, out_block, out_grad):
     f32 = jnp.float32
+    out_block[...] = block[...]
+    out_grad[...] = grad[...]
     for x, out in ((gate, out_gate), (up, out_up)):
         for s in range(4):
             for c in range(2):
@@ -1486,6 +1522,8 @@
 
     down = pl.BlockSpec((224, 1536), lambda i: (jnp.minimum(i, 9), 0))
 
+    own_rows = pl.BlockSpec((16, 1536), lambda i: (jnp.minimum(i, 7), 0))
+
     def whole(width):
         return pl.BlockSpec((rows, width), lambda i: (i, 0))
 
@@ -1498,9 +1536,11 @@
             jax.ShapeDtypeStruct((2240, 1536), f32),
             jax.ShapeDtypeStruct((384, 2048), f32),
             jax.ShapeDtypeStruct((384, 1536), f32),
+            jax.ShapeDtypeStruct((128, 1536), jnp.bfloat16),
+            jax.ShapeDtypeStruct((128, 1536), f32),
         ],
-        in_specs=[blocks(0), blocks(1), down, pl.BlockSpec((2, rows, 1792), lambda i: (0, i, 0))],
-        out_specs=[whole(8960), whole(8960), down, whole(2048), whole(1536)],
+        in_specs=[blocks(0), blocks(1), down, pl.BlockSpec((2, rows, 1792), lambda i: (0, i, 0)), own_rows, own_rows],
+        out_specs=[whole(8960), whole(8960), down, whole(2048), whole(1536), own_rows, own_rows],
     )(*sums)
 
 
@@ -1521,8 +1561,9 @@
     levels = lax.axis_size("replica") // 2
     grad_scale = 1.0 / math.sqrt(tok_count * lax.axis_size("replica") * lax.axis_size("shard"))
     cosine, sine_table = rope_tables(tok_count)
-    small = jnp.stack([jnp.pad(attn_gain, (0, 128)), qkv_bias, jnp.pad(mlp_gain, (0, 128))])
-    small = jnp.pad(small, ((0, 13), (0, 0)))
+    gap = jnp.zeros((128,), jnp.bfloat16)
+    rest = jnp.zeros((13 * 512,), jnp.bfloat16)
+    small = jnp.concatenate([attn_gain, gap, qkv_bias, mlp_gain, gap, rest]).reshape(16, 512)
     twice = jnp.concatenate([cosine[:, 0], cosine[:, 0]], axis=1)
     turn = jnp.concatenate([-sine_table[:, 0], sine_table[:, 0]], axis=1)
     got = forward(
@@ -1554,8 +1595,7 @@
         hidden=got["hidden"],
         x=block_input,
         cot=cotangent,
-        gain_one=got["gains"][0:1],
-        gain_two=got["gains"][1:2],
+        gains=got["gains"],
         ctx=got["ctx"],
         nrm=got["nrm"],
         qry=got["qry"],
@@ -1563,10 +1603,12 @@
         val=got["val"],
         lse=got["lse"],
         cos=twice,
-        sin=-turn,
+        sin=turn,
     )
     gain_one_own, bias_own, gain_two_own = vectors[0, :384], vectors[0, 384:896], vectors[0, 896:]
-    gate_grad, up_grad, down_grad, qkv_grad, out_grad = widen(sum_gate, sum_gate, sum_down, sum_attn)
+    gate_grad, up_grad, down_grad, qkv_grad, out_grad, block_output, input_grad = widen(
+        sum_gate, sum_gate, sum_down, sum_attn, block_output, input_grad
+    )
     return (
         block_output,
         input_grad,

time: 512 us -> 501 us (0.979)
  Pallas kernels: 500 us -> 492 us
    pallas_call x1, Pallas kernels: 147 us -> 139 us  [forward(): pl.pallas_call(functools.partial(forward_kernel, grad_scale, (*given, *ou...]
where the time goes in v8:
time: 501 us
  Pallas kernels  492 us (98%)
  local copies, waits for them, and re-layouts  6.59 us (1%)
    pallas_call x1, Pallas kernels, backward(): pl.pallas_call(functools.partial(backward_kernel, levels, grad_scale, (*g...  327 us
    pallas_call x1, Pallas kernels, forward(): pl.pallas_call(functools.partial(forward_kernel, grad_scale, (*given, *ou...  139 us
    pallas_call x1, Pallas kernels, widen(): pl.pallas_call(widen_kernel, grid=(384 // rows,), out_shape=[jax.ShapeDty...  25.9 us

profile of v8, /device:TPU:0, one launch (start us, length us, event | category | flops | bytes accessed | tf_op | source)
XLA Modules:
  0.0 500.9 jit_solution(7679891269609801090)
XLA Ops:
  0.7 0.9 dynamic-update-slice
  1.5 0.2 dynamic-update-slice.1
  1.8 0.9 dynamic-update-slice.2
  2.6 0.9 dynamic-update-slice.3
  3.5 0.2 dynamic-update-slice.4
  3.7 0.3 dynamic-update-slice.5
  4.0 0.6 reshape.29.refs_1_
  4.6 0.3 fusion.2
  4.9 0.8 pad_maximum_fusion
  5.7 139.1 %shard_map.177 = (bf16[1536,2048]{1,0:T(8,128)(2,1)}, bf16[1536,1536]{1,0:T(8,128)(2,1)}, bf16[1152,1536]{1,0:T(8,128)(2,1)}, bf16[1024,1152]{1,0:T(8,128)(2,1)}...) custom-call(bf16[128,1536]{1,0:T(8,128)(2,1)} %refs_11_.1, ...), custom_call_target="tpu_custom_call" | custom-call | tf_op jit(solution)/shard_map/pallas_call | solution.py:798
  144.8 327.4 %shard_map.178 = (bf16[2,384,1792]{2,1,0:T(8,128)(2,1)}, bf16[2240,1536]{1,0:T(8,128)(2,1)}, bf16[2,2,4,384,1152]{4,3,2,1,0:T(8,128)(2,1)}, bf16[6,384,1152]{2,1...) custom-call(bf16[1152,1536]{1,0:T(8,128)(2,1)} %get-tuple-element.41.refs_0_, ...), custom_call_target="tpu_custom_call" | custom-call | tf_op jit(solution)/shard_map/pallas_call | solution.py:1488
  472.2 1.3 slice.10
  473.5 1.3 slice_reduce_fusion
  474.8 25.9 %shard_map.179 = (f32[384,8960]{1,0:T(8,128)}, f32[384,8960]{1,0:T(8,128)}, f32[2240,1536]{1,0:T(8,128)}, f32[384,2048]{1,0:T(8,128)}, f32[384,1536]{1,0:T(8,128...) custom-call(bf16[2,2,4,384,1152]{4,3,2,1,0:T(8,128)(2,1)} %get-tuple-element.59.gate.up, ...), custom_call_target="tpu_custom_call" | custom-call | tf_op jit(solution)/shard_map/pallas_call | solution.py:1530
  (4 shorter events, 0.0 us)

commit v9 on v8

--- a/solution.py
+++ b/solution.py
@@ -357,7 +357,7 @@
     return lax.fori_loop(0, rows // step, lambda j, c: body(pl.ds(pl.multiple_of(j * step, step), step), c), init)
 
 
-TILES = ((0, 640, 160), (640, 512, 160))
+TILES = ((0, 640, 160), (640, 512, 96))
 
 
 def forward_kernel(grad_scale, names, *refs):
@@ -1339,7 +1339,7 @@
         own_narrow(a).start()
         onward(a, 0, columns(narrow[a][0], shard, 384), shard, core).start()
     load_down.wait()
-    lags = ((end_gather, 0), (gather_step, 8), (root_step, 14), (spread_step, 20), (end_spread, 28))
+    lags = ((end_gather, 0), (gather_step, 8), (root_step, 10), (spread_step, 12), (end_spread, 18))
     steps = CHUNKS + lags[-1][1]
 
     def begin_products():

time: 501 us -> 472 us (0.942)
  Pallas kernels: 492 us -> 463 us
    pallas_call x1, Pallas kernels: 327 us -> 304 us  [backward(): pl.pallas_call(functools.partial(backward_kernel, levels, grad_scale, (*g...]
    pallas_call x1, Pallas kernels: 139 us -> 134 us  [forward(): pl.pallas_call(functools.partial(forward_kernel, grad_scale, (*given, *ou...]
where the time goes in v9:
time: 472 us
  Pallas kernels  463 us (98%)
  local copies, waits for them, and re-layouts  6.59 us (1%)
    pallas_call x1, Pallas kernels, backward(): pl.pallas_call(functools.partial(backward_kernel, levels, grad_scale, (*g...  304 us
    pallas_call x1, Pallas kernels, forward(): pl.pallas_call(functools.partial(forward_kernel, grad_scale, (*given, *ou...  134 us
    pallas_call x1, Pallas kernels, widen(): pl.pallas_call(widen_kernel, grid=(384 // rows,), out_shape=[jax.ShapeDty...  25.9 us

profile of v9, /device:TPU:0, one launch (start us, length us, event | category | flops | bytes accessed | tf_op | source)
XLA Modules:
  0.0 471.8 jit_solution(12036158282315742864)
XLA Ops:
  0.7 0.9 dynamic-update-slice
  1.5 0.2 dynamic-update-slice.1
  1.8 0.9 dynamic-update-slice.2
  2.6 0.9 dynamic-update-slice.3
  3.5 0.2 dynamic-update-slice.4
  3.7 0.3 dynamic-update-slice.5
  4.0 0.6 reshape.29.refs_1_
  4.6 0.3 fusion.2
  4.9 0.8 pad_maximum_fusion
  5.7 133.9 %shard_map.177 = (bf16[1536,2048]{1,0:T(8,128)(2,1)}, bf16[1536,1536]{1,0:T(8,128)(2,1)}, bf16[1152,1536]{1,0:T(8,128)(2,1)}, bf16[1024,1152]{1,0:T(8,128)(2,1)}...) custom-call(bf16[128,1536]{1,0:T(8,128)(2,1)} %refs_11_.1, ...), custom_call_target="tpu_custom_call" | custom-call | tf_op jit(solution)/shard_map/pallas_call | solution.py:798
  139.6 303.5 %shard_map.178 = (bf16[2,384,1792]{2,1,0:T(8,128)(2,1)}, bf16[2240,1536]{1,0:T(8,128)(2,1)}, bf16[2,2,4,384,1152]{4,3,2,1,0:T(8,128)(2,1)}, bf16[6,384,1152]{2,1...) custom-call(bf16[1152,1536]{1,0:T(8,128)(2,1)} %get-tuple-element.41.refs_0_, ...), custom_call_target="tpu_custom_call" | custom-call | tf_op jit(solution)/shard_map/pallas_call | solution.py:1488
  443.1 1.3 slice.10
  444.4 1.3 slice_reduce_fusion
  445.8 25.9 %shard_map.179 = (f32[384,8960]{1,0:T(8,128)}, f32[384,8960]{1,0:T(8,128)}, f32[2240,1536]{1,0:T(8,128)}, f32[384,2048]{1,0:T(8,128)}, f32[384,1536]{1,0:T(8,128...) custom-call(bf16[2,2,4,384,1152]{4,3,2,1,0:T(8,128)(2,1)} %get-tuple-element.59.gate.up, ...), custom_call_target="tpu_custom_call" | custom-call | tf_op jit(solution)/shard_map/pallas_call | solution.py:1530
  (4 shorter events, 0.0 us)

commit v10 on v9

--- a/solution.py
+++ b/solution.py
@@ -514,10 +514,14 @@
         d_buf.at[span(odd_chip * (1 - core) * 64, 1088)], v["local"].at[5],
     ))
 
+    send_weight(0)
+    send_weight(1)
+    v["small"][...] = jnp.zeros((16, 512), bf16)
+    v["small"][0:1, 0:384] = v["gain_one"][...].reshape(1, 384)
+    v["small"][1:2, :] = v["bias"][...].reshape(1, 512)
+    v["small"][2:3, 0:384] = v["gain_two"][...].reshape(1, 384)
     for d in order:
         small_hop(d, peer_of(shard, d), shard).start()
-    send_weight(0)
-    send_weight(1)
     for copy in loads:
         copy.start()
     rest = pltpu.make_async_copy(
@@ -643,22 +647,29 @@
         if pending:
             take(*pending.pop(0))
 
-    def products(offset, width, m):
+    def product(out, offset, width, m, one):
         at = pl.ds(m * 512, 512)
         for n in range(0, width, 256):
             size = min(256, width - n)
-            cols = pl.ds(offset + n, size)
-            gs[:, n : n + size] = jnp.dot(n_all[at, :], g_buf[:, cols], preferred_element_type=f32)
-            us[:, n : n + size] = jnp.dot(n_all[at, :], u_buf[:, cols], preferred_element_type=f32)
-            gr[:, n : n + size] = dot_nt(cot_all[at, :], d_buf[cols, :])
+            out[at, n : n + size] = one(at, pl.ds(offset + n, size))
+
+    def gate_product(offset, width, m):
+        product(gs, offset, width, m, lambda at, cols: jnp.dot(n_all[at, :], g_buf[:, cols], preferred_element_type=f32))
+
+    def up_product(offset, width, m):
+        product(us, offset, width, m, lambda at, cols: jnp.dot(n_all[at, :], u_buf[:, cols], preferred_element_type=f32))
+
+    def grad_product(offset, width, m):
+        product(gr, offset, width, m, lambda at, cols: dot_nt(cot_all[at, :], d_buf[cols, :]))
+
+    def activate(offset, width, m):
         column = first_unit + offset + lax.broadcasted_iota(jnp.int32, (1, width), 1)
         owned = (column >= shard * 2240) & (column < (shard + 1) * 2240)
 
         def body(j, carry):
-            part = pl.ds(pl.multiple_of(j * 16, 16), 16)
             to = pl.ds(pl.multiple_of(m * 512 + j * 16, 16), 16)
             cols = pl.ds(offset, width)
-            gate, up, grad = gs[part, 0:width], us[part, 0:width], gr[part, 0:width]
+            gate, up, grad = gs[to, 0:width], us[to, 0:width], gr[to, 0:width]
             sig = jax.nn.sigmoid(gate)
             silu = gate * sig
             act[to, cols] = jnp.where(owned, silu * up, 0.0).astype(bf16)
@@ -686,33 +697,49 @@
         copy.start()
         outs[n] = copy
 
+    write("w_d", d_buf, pl.ds(0, WINDOW))
     for tile, (offset, width, _) in enumerate(TILES):
         cols = pl.ds(offset, width)
-        for m in range(2):
-            products(offset, width, m)
-            service()
+        if tile == 0:
+            for m in range(2):
+                gate_product(offset, width, m)
+                up_product(offset, width, m)
+                grad_product(offset, width, m)
+                activate(offset, width, m)
+                service()
+        else:
+            for m in range(2):
+                grad_product(offset, width, m)
+                if len(pending) > 2:
+                    service()
+            while len(pending) > 3:
+                service()
+            take_shared(4)
+            for m in range(2):
+                gate_product(offset, width, m)
+            while pending:
+                service()
+            take_shared(5)
+            for m in range(2):
+                up_product(offset, width, m)
+                activate(offset, width, m)
+        write("w_g", g_buf, pl.ds(0, 1536), cols)
+        write("w_u", u_buf, pl.ds(0, 1536), cols)
         transpose(act, cols, v["act_t"].at[pl.ds(0, width)])
         if tile == 0:
             transpose(n_all, pl.ds(0, 1536), v["n_t_buf"])
-        service()
+            write("n_t", v["n_t_buf"], pl.ds(0, 1536))
+            service()
+        for name, buf in (("act", act), ("gd", gate_delta), ("ud", up_delta)):
+            write(name, buf, pl.ds(0, 1024), cols)
         for n in range(3):
             out = pl.ds(n * 512, 512)
             v["d_grad"][cols, out] = (
                 jnp.dot(v["act_t"][0:width, :], cot_all[:, out], preferred_element_type=f32) * grad_scale
             ).astype(bf16)
         write("pd", v["d_grad"], cols)
-        service()
-        for name, buf in (("act", act), ("gd", gate_delta), ("ud", up_delta)):
-            write(name, buf, pl.ds(0, 1024), cols)
-        while pending:
+        if tile == 0:
             service()
-        if tile == 0:
-            write("n_t", v["n_t_buf"], pl.ds(0, 1536))
-            take_shared(4)
-            take_shared(5)
-            write("w_g", g_buf, pl.ds(0, 1536))
-            write("w_u", u_buf, pl.ds(0, 1536))
-            write("w_d", d_buf, pl.ds(0, WINDOW))
     keep_q.wait()
     keep_o.wait()
     for i in (0, 1):
@@ -745,7 +772,7 @@
     bf16 = jnp.bfloat16
     f32 = jnp.float32
     dma = pltpu.SemaphoreType.DMA
-    in_vmem = ("x", "small", "cos", "sin")
+    in_vmem = ("x", "gain_one", "bias", "gain_two", "cos", "sin")
     outs = {
         "q_full": ((1536, 2048), bf16, any_spec()),
         "o_full": ((1536, 1536), bf16, any_spec()),
@@ -774,6 +801,7 @@
         "d_buf": pltpu.VMEM((WINDOW, 1536), bf16),
         "n_all": pltpu.VMEM((1024, 1536), bf16),
         "cot_all": pltpu.VMEM((1024, 1536), bf16),
+        "small": pltpu.VMEM((16, 512), bf16),
         "small_all": pltpu.VMEM((4, 16, 512), bf16),
         "prj": pltpu.VMEM((128, 2048), f32),
         "act_buf": pltpu.VMEM((1024, WINDOW), bf16),
@@ -781,9 +809,9 @@
         "ud_buf": pltpu.VMEM((1024, WINDOW), bf16),
         "n_t_buf": pltpu.VMEM((1536, 1024), bf16),
         "act_t": pltpu.VMEM((640, 1024), bf16),
-        "gs": pltpu.VMEM((512, 640), f32),
-        "us": pltpu.VMEM((512, 640), f32),
-        "gr": pltpu.VMEM((512, 640), f32),
+        "gs": pltpu.VMEM((1024, 640), f32),
+        "us": pltpu.VMEM((1024, 640), f32),
+        "gr": pltpu.VMEM((1024, 640), f32),
         "d_grad": pltpu.VMEM((WINDOW, 1536), bf16),
         "send": dma((27,)),
         "recv": dma((27,)),
@@ -1495,8 +1523,13 @@
     )(*given.values())
 
 
-def widen_kernel(gate, up, down, attn, block, grad, out_gate, out_up, out_down, out_qkv, out_out, out_block, out_grad):
+def widen_kernel(
+    gate, up, down, attn, block, grad, vec, out_gate, out_up, out_down, out_qkv, out_out, out_block, out_grad, gain_one, bias, gain_two
+):
     f32 = jnp.float32
+    gain_one[...] = vec[0, 0:384]
+    bias[...] = vec[0, 384:896]
+    gain_two[...] = vec[0, 896:1280]
     out_block[...] = block[...]
     out_grad[...] = grad[...]
     for x, out in ((gate, out_gate), (up, out_up)):
@@ -1515,14 +1548,17 @@
 
 
 def widen(*sums):
-    rows = 32
+    rows = 96
     f32 = jnp.float32
     def blocks(a):
         return pl.BlockSpec((None, 2, 4, rows, WINDOW), lambda i: (a, 0, 0, i, 0))
 
-    down = pl.BlockSpec((224, 1536), lambda i: (jnp.minimum(i, 9), 0))
-
-    own_rows = pl.BlockSpec((16, 1536), lambda i: (jnp.minimum(i, 7), 0))
+    down = pl.BlockSpec((560, 1536), lambda i: (i, 0))
+
+    own_rows = pl.BlockSpec((32, 1536), lambda i: (i, 0))
+
+    def line(width):
+        return pl.BlockSpec((width,), lambda i: (0,))
 
     def whole(width):
         return pl.BlockSpec((rows, width), lambda i: (i, 0))
@@ -1538,9 +1574,13 @@
             jax.ShapeDtypeStruct((384, 1536), f32),
             jax.ShapeDtypeStruct((128, 1536), jnp.bfloat16),
             jax.ShapeDtypeStruct((128, 1536), f32),
+            jax.ShapeDtypeStruct((384,), f32),
+            jax.ShapeDtypeStruct((512,), f32),
+            jax.ShapeDtypeStruct((384,), f32),
         ],
-        in_specs=[blocks(0), blocks(1), down, pl.BlockSpec((2, rows, 1792), lambda i: (0, i, 0)), own_rows, own_rows],
-        out_specs=[whole(8960), whole(8960), down, whole(2048), whole(1536), own_rows, own_rows],
+        in_specs=[blocks(0), blocks(1), down, pl.BlockSpec((2, rows, 1792), lambda i: (0, i, 0)), own_rows, own_rows,
+                  pl.BlockSpec((8, 1280), lambda i: (0, 0))],
+        out_specs=[whole(8960), whole(8960), down, whole(2048), whole(1536), own_rows, own_rows, line(384), line(512), line(384)],
     )(*sums)
 
 
@@ -1561,15 +1601,14 @@
     levels = lax.axis_size("replica") // 2
     grad_scale = 1.0 / math.sqrt(tok_count * lax.axis_size("replica") * lax.axis_size("shard"))
     cosine, sine_table = rope_tables(tok_count)
-    gap = jnp.zeros((128,), jnp.bfloat16)
-    rest = jnp.zeros((13 * 512,), jnp.bfloat16)
-    small = jnp.concatenate([attn_gain, gap, qkv_bias, mlp_gain, gap, rest]).reshape(16, 512)
     twice = jnp.concatenate([cosine[:, 0], cosine[:, 0]], axis=1)
     turn = jnp.concatenate([-sine_table[:, 0], sine_table[:, 0]], axis=1)
     got = forward(
         grad_scale,
         x=block_input,
-        small=small,
+        gain_one=attn_gain,
+        bias=qkv_bias,
+        gain_two=mlp_gain,
         cos=twice,
         sin=turn,
         wq=qkv_weight,
@@ -1605,9 +1644,8 @@
         cos=twice,
         sin=turn,
     )
-    gain_one_own, bias_own, gain_two_own = vectors[0, :384], vectors[0, 384:896], vectors[0, 896:]
-    gate_grad, up_grad, down_grad, qkv_grad, out_grad, block_output, input_grad = widen(
-        sum_gate, sum_gate, sum_down, sum_attn, block_output, input_grad
+    gate_grad, up_grad, down_grad, qkv_grad, out_grad, block_output, input_grad, gain_one_own, bias_own, gain_two_own = widen(
+        sum_gate, sum_gate, sum_down, sum_attn, block_output, input_grad, vectors
     )
     return (
         block_output,

time: 472 us -> 465 us (0.985)
  local copies, waits for them, and re-layouts: 6.59 us -> 0 us
where the time goes in v10:
time: 465 us
  Pallas kernels  463 us (100%)
    pallas_call x1, Pallas kernels, backward(): pl.pallas_call(functools.partial(backward_kernel, levels, grad_scale, (*g...  303 us
    pallas_call x1, Pallas kernels, forward(): pl.pallas_call(functools.partial(forward_kernel, grad_scale, (*given, *ou...  137 us
    pallas_call x1, Pallas kernels, widen(): pl.pallas_call(widen_kernel, grid=(384 // rows,), out_shape=[jax.ShapeDty...  22.7 us

profile of v10, /device:TPU:0, one launch (start us, length us, event | category | flops | bytes accessed | tf_op | source)
XLA Modules:
  0.0 465.1 jit_solution(5385284861534447185)
XLA Ops:
  0.7 0.3 fusion.2
  0.9 0.8 pad_maximum_fusion
  1.7 137.2 %shard_map.177 = (bf16[1536,2048]{1,0:T(8,128)(2,1)}, bf16[1536,1536]{1,0:T(8,128)(2,1)}, bf16[1152,1536]{1,0:T(8,128)(2,1)}, bf16[1024,1152]{1,0:T(8,128)(2,1)}...) custom-call(bf16[128,1536]{1,0:T(8,128)(2,1)} %refs_11_.3, ...), custom_call_target="tpu_custom_call" | custom-call | tf_op jit(solution)/shard_map/pallas_call | solution.py:826
  138.9 303.3 %shard_map.178 = (bf16[2,384,1792]{2,1,0:T(8,128)(2,1)}, bf16[2240,1536]{1,0:T(8,128)(2,1)}, bf16[2,2,4,384,1152]{4,3,2,1,0:T(8,128)(2,1)}, bf16[6,384,1152]{2,1...) custom-call(bf16[1152,1536]{1,0:T(8,128)(2,1)} %get-tuple-element.44.refs_0_, ...), custom_call_target="tpu_custom_call" | custom-call | tf_op jit(solution)/shard_map/pallas_call | solution.py:1516
  442.3 22.7 %shard_map.179 = (f32[384,8960]{1,0:T(8,128)}, f32[384,8960]{1,0:T(8,128)}, f32[2240,1536]{1,0:T(8,128)}, f32[384,2048]{1,0:T(8,128)}, f32[384,1536]{1,0:T(8,128...) custom-call(bf16[2,2,4,384,1152]{4,3,2,1,0:T(8,128)(2,1)} %get-tuple-element.6, ...), custom_call_target="tpu_custom_call" | custom-call | tf_op jit(solution)/shard_map/pallas_call | solution.py:1566
  (1 shorter events, 0.0 us)

commit v11 on v10

--- a/solution.py
+++ b/solution.py
@@ -357,7 +357,7 @@
     return lax.fori_loop(0, rows // step, lambda j, c: body(pl.ds(pl.multiple_of(j * step, step), step), c), init)
 
 
-TILES = ((0, 640, 160), (640, 512, 96))
+TILES = ((0, 640, 192), (640, 512, 128))
 
 
 def forward_kernel(grad_scale, names, *refs):
@@ -384,8 +384,8 @@
         return pl.ds(pl.multiple_of((c * 4 + owner) * 128, 128), 128)
 
     weights = [
-        (lambda t: v["wq"], q_buf, 192, 80, True),
-        (lambda t: v["wo"], o_buf, 192, 80, True),
+        (lambda t: v["wq"], q_buf, 192, 48, True),
+        (lambda t: v["wo"], o_buf, 192, 48, True),
     ]
     for offset, width, shared in TILES:
         for name, buf in (("wg", g_buf), ("wu", u_buf)):
@@ -698,6 +698,7 @@
         outs[n] = copy
 
     write("w_d", d_buf, pl.ds(0, WINDOW))
+    write("cot_rows", cot_all, pl.ds(0, 1024))
     for tile, (offset, width, _) in enumerate(TILES):
         cols = pl.ds(offset, width)
         if tile == 0:
@@ -725,20 +726,19 @@
                 activate(offset, width, m)
         write("w_g", g_buf, pl.ds(0, 1536), cols)
         write("w_u", u_buf, pl.ds(0, 1536), cols)
-        transpose(act, cols, v["act_t"].at[pl.ds(0, width)])
+        for name, buf in (("act", act), ("gd", gate_delta), ("ud", up_delta)):
+            write(name, buf, pl.ds(0, 1024), cols)
         if tile == 0:
+            transpose(act, cols, v["act_t"])
             transpose(n_all, pl.ds(0, 1536), v["n_t_buf"])
             write("n_t", v["n_t_buf"], pl.ds(0, 1536))
             service()
-        for name, buf in (("act", act), ("gd", gate_delta), ("ud", up_delta)):
-            write(name, buf, pl.ds(0, 1024), cols)
-        for n in range(3):
-            out = pl.ds(n * 512, 512)
-            v["d_grad"][cols, out] = (
-                jnp.dot(v["act_t"][0:width, :], cot_all[:, out], preferred_element_type=f32) * grad_scale
-            ).astype(bf16)
-        write("pd", v["d_grad"], cols)
-        if tile == 0:
+            for n in range(3):
+                out = pl.ds(n * 512, 512)
+                v["d_grad"][:, out] = (
+                    jnp.dot(v["act_t"][...], cot_all[:, out], preferred_element_type=f32) * grad_scale
+                ).astype(bf16)
+            write("pd", v["d_grad"], cols)
             service()
     keep_q.wait()
     keep_o.wait()
@@ -776,7 +776,8 @@
     outs = {
         "q_full": ((1536, 2048), bf16, any_spec()),
         "o_full": ((1536, 1536), bf16, any_spec()),
-        "pd": ((WINDOW, 1536), bf16, any_spec()),
+        "pd": ((640, 1536), bf16, any_spec()),
+        "cot_rows": ((1024, 1536), bf16, any_spec()),
         "act": ((1024, WINDOW), bf16, any_spec()),
         "gd": ((1024, WINDOW), bf16, any_spec()),
         "ud": ((1024, WINDOW), bf16, any_spec()),
@@ -812,7 +813,7 @@
         "gs": pltpu.VMEM((1024, 640), f32),
         "us": pltpu.VMEM((1024, 640), f32),
         "gr": pltpu.VMEM((1024, 640), f32),
-        "d_grad": pltpu.VMEM((WINDOW, 1536), bf16),
+        "d_grad": pltpu.VMEM((640, 1536), bf16),
         "send": dma((27,)),
         "recv": dma((27,)),
         "rsend": dma((8,)),
@@ -860,7 +861,7 @@
             v["xsend"].at[block], v["xrecv"].at[block], (replica, chip),
         )
 
-    load_down = pltpu.make_async_copy(v["pd"], own_d, v["in_sem"].at[0])
+    load_down = pltpu.make_async_copy(v["pd"], own_d.at[pl.ds(0, 640)], v["in_sem"].at[0])
     load_normed = pltpu.make_async_copy(v["n_t"], wbuf.at[:, pl.ds(0, 1024)], v["in_sem"].at[1])
     load_gate = pltpu.make_async_copy(v["w_g"], wbuf.at[:, pl.ds(WINDOW, WINDOW)], v["in_sem"].at[2])
     load_up = pltpu.make_async_copy(v["w_u"], wbuf.at[:, pl.ds(0, WINDOW)], v["in_sem"].at[3])
@@ -870,6 +871,14 @@
         pltpu.make_async_copy(v["ud"], mat.at[1], v["in_sem"].at[6]),
     ]
     load_act = pltpu.make_async_copy(v["act"], act, v["in_sem"].at[7])
+    load_cot = pltpu.make_async_copy(v["cot_rows"], out, v["in_sem"].at[8])
+
+    def stage_down(n):
+        if n == 0:
+            load_act.wait()
+            load_cot.wait()
+        cols = pl.ds(n * 512, 512)
+        own_d[640:WINDOW, cols] = (dot_tn(act[:, 640:WINDOW], out[:, cols]) * grad_scale).astype(bf16)
 
     def staged(block):
         slot = lax.rem(block, 2)
@@ -1358,11 +1367,12 @@
             to_mate(a, d).start()
 
     load_down.start()
+    load_act.start()
+    load_cot.start()
     load_normed.start()
     for copy in load_deltas:
         copy.start()
     load_gate.start()
-    load_act.start()
     for a in range(2):
         own_narrow(a).start()
         onward(a, 0, columns(narrow[a][0], shard, 384), shard, core).start()
@@ -1378,7 +1388,6 @@
     def begin_out():
         start_mate(0)
         load_wd.start()
-        load_act.wait()
 
     def end_out():
         start_mate(1)
@@ -1389,6 +1398,9 @@
         send_blocks((3,))
 
     beside = [
+        (2, 1, functools.partial(stage_down, 0)),
+        (4, 1, functools.partial(stage_down, 1)),
+        (6, 1, functools.partial(stage_down, 2)),
         (9, 1, begin_products),
         (9, 4, lambda i: (stage_gradient(2 * i), stage_gradient(2 * i + 1))),
         (13, 1, start_back),
@@ -1464,7 +1476,7 @@
     bf16 = jnp.bfloat16
     f32 = jnp.float32
     dma = pltpu.SemaphoreType.DMA
-    in_hbm = ("pd", "act", "gd", "ud", "n_t", "w_g", "w_u", "w_d", "wo", "wq")
+    in_hbm = ("pd", "cot_rows", "act", "gd", "ud", "n_t", "w_g", "w_u", "w_d", "wo", "wq")
     outs = {
         "fa": ((2, 384, 1792), bf16, any_spec()),
         "fd": ((2240, 1536), bf16, any_spec()),
@@ -1506,7 +1518,7 @@
     }
     counts = {
         "xsend": 8, "xrecv": 8, "stage_sem": 2, "csend": 8, "crecv": 8, "psend": 6, "precv": 6, "gsend": 24, "grecv": 24,
-        "fsend": 8, "frecv": 8, "local": 6, "in_sem": 8, "vsend": 2 + 2 * levels, "vrecv": 2 + 2 * levels,
+        "fsend": 8, "frecv": 8, "local": 6, "in_sem": 9, "vsend": 2 + 2 * levels, "vrecv": 2 + 2 * levels,
     }
     for name in (
         "part_sem", "near_sem", "far_sem", "up_sem", "down_sem", "done_sem", "mate_send", "mate_recv", "out_sem"
@@ -1622,6 +1634,7 @@
         levels,
         grad_scale,
         pd=got["pd"],
+        cot_rows=got["cot_rows"],
         act=got["act"],
         gd=got["gd"],
         ud=got["ud"],

time: 465 us -> 463 us (level)
  no operation moved by 1% of the time
where the time goes in v11:
time: 463 us
  Pallas kernels  461 us (100%)
    pallas_call x1, Pallas kernels, backward(): pl.pallas_call(functools.partial(backward_kernel, levels, grad_scale, (*g...  304 us
    pallas_call x1, Pallas kernels, forward(): pl.pallas_call(functools.partial(forward_kernel, grad_scale, (*given, *ou...  135 us
    pallas_call x1, Pallas kernels, widen(): pl.pallas_call(widen_kernel, grid=(384 // rows,), out_shape=[jax.ShapeDty...  22.7 us

profile of v11, /device:TPU:0, one launch (start us, length us, event | category | flops | bytes accessed | tf_op | source)
XLA Modules:
  0.0 463.3 jit_solution(1696256098496918330)
XLA Ops:
  0.7 0.3 fusion.2
  0.9 0.8 pad_maximum_fusion
  1.7 135.1 %shard_map.177 = (bf16[1536,2048]{1,0:T(8,128)(2,1)}, bf16[1536,1536]{1,0:T(8,128)(2,1)}, bf16[640,1536]{1,0:T(8,128)(2,1)}, bf16[1024,1536]{1,0:T(8,128)(2,1)},...) custom-call(bf16[128,1536]{1,0:T(8,128)(2,1)} %refs_12_.1, ...), custom_call_target="tpu_custom_call" | custom-call | tf_op jit(solution)/shard_map/pallas_call | solution.py:827
  136.8 303.6 %shard_map.178 = (bf16[2,384,1792]{2,1,0:T(8,128)(2,1)}, bf16[2240,1536]{1,0:T(8,128)(2,1)}, bf16[2,2,4,384,1152]{4,3,2,1,0:T(8,128)(2,1)}, bf16[6,384,1152]{2,1...) custom-call(bf16[640,1536]{1,0:T(8,128)(2,1)} %get-tuple-element.45.refs_0_, ...), custom_call_target="tpu_custom_call" | custom-call | tf_op jit(solution)/shard_map/pallas_call | solution.py:1528
  440.4 22.7 %shard_map.179 = (f32[384,8960]{1,0:T(8,128)}, f32[384,8960]{1,0:T(8,128)}, f32[2240,1536]{1,0:T(8,128)}, f32[384,2048]{1,0:T(8,128)}, f32[384,1536]{1,0:T(8,128...) custom-call(bf16[2,2,4,384,1152]{4,3,2,1,0:T(8,128)(2,1)} %get-tuple-element.6, ...), custom_call_target="tpu_custom_call" | custom-call | tf_op jit(solution)/shard_map/pallas_call | solution.py:1578
  (1 shorter events, 0.0 us)
